TPU v7x, 32 devices: a whole 2x2x4 slice. The times are simulated.
32 devices in a mesh: dp: 8 (over z, x), head: 4 (over y, core).
Axes of the slice: x: 2, y: 2, z: 4, core: 2. Of those that a mesh axis runs over, the one named last changes fastest.
Arguments:
- inputs: bfloat16 [8192, 2048], P('dp'), may hold values from -6 to 6
- lengths: int32 [8], P('dp'), may hold values from 256 to 1024, as said below
- gain_attn: bfloat16 [2048], P('dp'), may hold values from 0.5 to 1.5
- w_query: bfloat16 [2048, 2048], P('dp', 'head'), may hold values from -0.25 to 0.25
- w_key: bfloat16 [2048, 2048], P('dp', 'head'), may hold values from -0.25 to 0.25
- w_value: bfloat16 [2048, 2048], P('dp', 'head'), may hold values from -0.125 to 0.125
- w_slot: bfloat16 [2048, 256], P('dp', 'head'), may hold values from -0.125 to 0.125
- gate_bias: float32 [256], P('head'), may hold values from 0 to 8
- w_out: bfloat16 [2048, 2048], P('head', 'dp'), may hold values from -0.5 to 0.5
- gain_ffn: bfloat16 [2048], P('dp'), may hold values from 0.5 to 1.5
- w_gate: bfloat16 [2048, 5632], P('dp', 'head'), may hold values from -0.125 to 0.125
- w_up: bfloat16 [2048, 5632], P('dp', 'head'), may hold values from -0.125 to 0.125
- w_down: bfloat16 [5632, 2048], P('head', 'dp'), may hold values from -0.078125 to 0.078125
- cotangent: bfloat16 [8192, 2048], P('dp'), may hold values from -6 to 6
Outputs:
- output: bfloat16 [8192, 2048], P('dp')
- grad_inputs: float32 [8192, 2048], P('dp')
- grad_gain_attn: float32 [2048], P('dp')
- grad_w_query: float32 [2048, 2048], P('dp', 'head')
- grad_w_key: float32 [2048, 2048], P('dp', 'head')
- grad_w_value: float32 [2048, 2048], P('dp', 'head')
- grad_w_slot: float32 [2048, 256], P('dp', 'head')
- grad_gate_bias: float32 [256], P('head')
- grad_w_out: float32 [2048, 2048], P('head', 'dp')
- grad_gain_ffn: float32 [2048], P('dp')
- grad_w_gate: float32 [2048, 5632], P('dp', 'head')
- grad_w_up: float32 [2048, 5632], P('dp', 'head')
- grad_w_down: float32 [5632, 2048], P('head', 'dp')
Inputs may be any that keep to these rules, and one draw needn't show every extreme that they name: lengths[s] is the number of valid leading positions of sequence s; some sequence has all 1024 valid.
All inputs are finite; a program needn't handle non-finite values.
Results may differ from a plain program's by a relative error of at most 0.014.
Values may be sent and summed in bfloat16 or wider, within the bound.
A program may use at most 256 MiB of HBM per device.

v0:
```python
import jax
import jax.numpy as jnp
from jax import lax
from jax.experimental import pallas as pl
from jax.experimental.pallas import tpu as pltpu
from jax.sharding import PartitionSpec as P

BLOCK = 64
TILE = 128
DP, HEAD = "dp", "head"
epsilon = 1e-06
PAIR = 2


def split_low(values):
    high = values.astype(jnp.bfloat16)
    return high, (values - high.astype(jnp.float32)).astype(jnp.bfloat16)


def dot_nn(left, right):
    return lax.dot_general(left, right, (((1,), (0,)), ((), ())), preferred_element_type=jnp.float32)


def dot_nt(left, right):
    return lax.dot_general(left, right, (((1,), (1,)), ((), ())), preferred_element_type=jnp.float32)


def lane_place():
    lanes = lax.broadcasted_iota(jnp.int32, (BLOCK, TILE), 1)
    return lanes, jnp.bitwise_and(lanes, BLOCK - 1)


def prefix_sum(values, place):
    step = 1
    while step < BLOCK:
        values = values + jnp.where(place >= step, pltpu.roll(values, step, 1), 0.0)
        step *= 2
    return values


def suffix_sum(values, place):
    step = 1
    while step < BLOCK:
        values = values + jnp.where(place < BLOCK - step, pltpu.roll(values, TILE - step, 1), 0.0)
        step *= 2
    return values


def to_band(square):
    rows = lax.broadcasted_iota(jnp.int32, (TILE, TILE), 0)
    step = 1
    while step < TILE:
        square = jnp.where(jnp.bitwise_and(rows, step) != 0, pltpu.roll(square, TILE - step, 1), square)
        step *= 2
    return square.T


def from_band(band):
    return pltpu.roll(band.T, 0, 1, stride=1, stride_axis=0)


def lag_row(lag):
    return slice((TILE - lag) % TILE, (TILE - lag) % TILE + 1)


def fill_products(product_ref, slot, writes, inside):
    product_ref[slot, 0] = writes
    power, powers, reach = inside, [], 1
    while reach < BLOCK:
        powers.append(power)
        for lag in range(reach):
            product_ref[slot, reach + lag] = power * pltpu.roll(product_ref[slot, lag], reach, 1)
        power = power * pltpu.roll(power, reach, 1)
        reach *= 2
    return powers


def lag_total(product_ref, slot, band_ref, start):
    sums = [start, None, None, None]
    for lag in range(BLOCK):
        term = product_ref[slot, lag] * band_ref[slot, lag_row(lag), :]
        held = sums[lag % 4]
        sums[lag % 4] = term if held is None else held + term
    return (sums[0] + sums[1]) + (sums[2] + sums[3])


def lag_mix(product_ref, slot, band_ref, weights):
    for lag in range(BLOCK):
        band_ref[slot, lag_row(lag), :] = jnp.sum(weights * product_ref[slot, lag], axis=0, keepdims=True)


def lag_back(powers, term_of, low, count, stride=1):
    if count == 1:
        return term_of(low)
    half = count // 2
    left = lag_back(powers, term_of, low, half, stride)
    right = lag_back(powers, term_of, low + half, half, stride)
    return left + pltpu.roll(powers[half.bit_length() - 1] * right, TILE - half * stride, 1)


def gate_terms(logits, valid, place):
    log_sig = jnp.minimum(logits, 0.0) - jnp.log1p(jnp.exp(-jnp.abs(logits)))
    logdecay = valid * log_sig * 0.125
    decay = jnp.exp(logdecay)
    series = -logdecay * (1.0 + logdecay * (0.5 + logdecay * (1.0 / 6.0 + logdecay * (1.0 / 24.0))))
    writes = valid * jnp.where(logdecay > -0.03, series, 1.0 - decay)
    inside = jnp.where(place == 0, 0.0, decay)
    before = prefix_sum(logdecay, place)
    after = suffix_sum(logdecay, place) - logdecay
    return decay, writes, inside, before, after


def stacked(values, lanes):
    return jnp.concatenate(
        [jnp.where(lanes < BLOCK, values, 0.0), jnp.where(lanes < BLOCK, 0.0, values)], axis=0
    )


def own_block(square, lanes):
    return jnp.where(lanes < BLOCK, square[:BLOCK], square[BLOCK:])


def forward_kernel(
    length_ref, qkv_ref, logit_ref, bias_ref,
    mixed_ref, state_ref, prob_ref, score_ref, mix_ref,
    gate_ref, carry_ref, band_ref, mix_band_ref, product_ref,
):
    width = mixed_ref.shape[1]
    tiles = mixed_ref.shape[0] // TILE
    scale = width ** -0.5
    lanes, place = lane_place()
    bias = bias_ref[...]

    def valid_of(tile):
        return (lanes + tile * TILE < length_ref[0]).astype(jnp.float32)

    def rows_of(tile):
        return pl.ds(pl.multiple_of(tile * TILE, TILE), TILE)

    def gather_writes(tile, none):
        logits = logit_ref[tile] + bias
        _, writes, inside, before, after = gate_terms(logits, valid_of(tile), place)
        gate_ref[tile, 0] = writes
        gate_ref[tile, 1] = inside
        gate_ref[tile, 2] = jnp.exp(before)
        gate_ref[tile, 3] = jnp.exp(before + after)
        high, low = split_low(stacked(jnp.exp(after) * writes, lanes))
        rows = qkv_ref[rows_of(tile), width:]
        added = dot_nn(high, rows) + dot_nn(low, rows)
        state_ref[tile] = added
        return none

    lax.fori_loop(0, tiles, gather_writes, 0)

    carry_ref[...] = jnp.zeros_like(carry_ref)

    def run_states(tile, none):
        for part in range(2):
            span = pl.ds(part * BLOCK, BLOCK)
            fade = gate_ref[tile, 3, :, part * BLOCK : part * BLOCK + 1]
            carried = carry_ref[...]
            added = state_ref[tile, span, :]
            state_ref[tile, span, :] = carried
            carry_ref[...] = fade * carried + added
        return none

    lax.fori_loop(0, tiles, run_states, 0)

    band_ref[...] = jnp.zeros_like(band_ref)
    mix_band_ref[...] = jnp.zeros_like(mix_band_ref)

    def mix_pair(pair, none):
        both = [(slot, PAIR * pair + slot) for slot in range(PAIR)]
        queries, scores, probs = {}, {}, {}
        for slot, tile in both:
            fill_products(product_ref, slot, gate_ref[tile, 0], gate_ref[tile, 1])
        for slot, tile in both:
            queries[slot] = qkv_ref[rows_of(tile), :width]
            band_ref[slot] = to_band(dot_nt(queries[slot], qkv_ref[rows_of(tile), width : 2 * width]) * scale)
        for slot, tile in both:
            high, low = split_low(state_ref[tile, :, :width])
            carried = own_block(dot_nt(high, queries[slot]) + dot_nt(low, queries[slot]), lanes)
            scores[slot] = gate_ref[tile, 2] * carried * scale
        for slot, tile in both:
            scores[slot] = lag_total(product_ref, slot, band_ref, scores[slot])
        for slot, tile in both:
            top = jnp.max(scores[slot], axis=0, keepdims=True)
            raised = jnp.exp(scores[slot] - top)
            probs[slot] = raised / jnp.sum(raised, axis=0, keepdims=True)
            score_ref[tile] = scores[slot]
            prob_ref[tile] = probs[slot]
        for slot, tile in both:
            lag_mix(product_ref, slot, mix_band_ref, probs[slot])
        for slot, tile in both:
            mixing = from_band(mix_band_ref[slot]).astype(jnp.bfloat16)
            mix_ref[tile] = mixing
            reach = stacked(probs[slot] * gate_ref[tile, 2], lanes).T.astype(jnp.bfloat16)
            result = dot_nn(mixing, qkv_ref[rows_of(tile), 2 * width :]) + dot_nn(
                reach, state_ref[tile, :, width:].astype(jnp.bfloat16)
            )
            rows = lax.broadcasted_iota(jnp.int32, (TILE, 1), 0) + tile * TILE
            mixed_ref[rows_of(tile), :] = jnp.where(rows < length_ref[0], result, 0.0).astype(jnp.bfloat16)
        return none

    lax.fori_loop(0, tiles // PAIR, mix_pair, 0)


def backward_kernel(
    length_ref, qkv_ref, logit_ref, bias_ref, back_ref, state_ref, prob_ref, score_ref, mix_ref,
    d_qkv_ref, d_bias_ref,
    adjoint_ref, gain_ref, key_band_ref, value_band_ref, band_ref, carry_ref, end_ref, cross_ref, product_ref,
):
    width = back_ref.shape[1]
    tiles = back_ref.shape[0] // TILE
    scale = width ** -0.5
    lanes, place = lane_place()
    bias = bias_ref[...]

    def valid_of(tile):
        return (lanes + tile * TILE < length_ref[0]).astype(jnp.float32)

    def rows_of(tile):
        return pl.ds(pl.multiple_of(tile * TILE, TILE), TILE)

    def back_of(tile):
        rows = lax.broadcasted_iota(jnp.int32, (TILE, 1), 0) + tile * TILE
        return jnp.where(rows < length_ref[0], back_ref[rows_of(tile), :], jnp.zeros((), back_ref.dtype))

    band_ref[...] = jnp.zeros_like(band_ref)

    def slopes(pair, none):
        both = [(slot, PAIR * pair + slot) for slot in range(PAIR)]
        fades, powers, queries, keys, backs, gains, d_scores = {}, {}, {}, {}, {}, {}, {}
        for slot, tile in both:
            decay, writes, inside, before, after = gate_terms(logit_ref[tile] + bias, valid_of(tile), place)
            fades[slot] = jnp.exp(before)
            gain_ref[tile, 2] = decay
            gain_ref[tile, 3] = writes
            gain_ref[tile, 4] = jnp.exp(after)
            gain_ref[tile, 5] = jnp.exp(before + after)
            powers[slot] = fill_products(product_ref, slot, writes, inside)
        for slot, tile in both:
            queries[slot] = qkv_ref[rows_of(tile), :width]
            keys[slot] = qkv_ref[rows_of(tile), width : 2 * width]
            backs[slot] = back_of(tile)
            key_band_ref[slot] = to_band(dot_nt(queries[slot], keys[slot]) * scale)
            value_band_ref[slot] = to_band(dot_nt(backs[slot], qkv_ref[rows_of(tile), 2 * width :]))
        for slot, tile in both:
            high, low = split_low(state_ref[tile, :, width:])
            carried = own_block(dot_nt(high, backs[slot]) + dot_nt(low, backs[slot]), lanes)
            gains[slot] = fades[slot] * carried
        for slot, tile in both:
            gains[slot] = lag_total(product_ref, slot, value_band_ref, gains[slot])
        for slot, tile in both:
            probs = prob_ref[tile]
            d_scores[slot] = probs * (gains[slot] - jnp.sum(probs * gains[slot], axis=0, keepdims=True))
            gain_ref[tile, 1] = d_scores[slot] * score_ref[tile] + probs * gains[slot]
        for slot, tile in both:
            lag_mix(product_ref, slot, band_ref, d_scores[slot])
        for slot, tile in both:
            probs = prob_ref[tile]

            def term_of(lag, slot=slot, probs=probs):
                row = lag_row(lag)
                return d_scores[slot] * key_band_ref[slot, row, :] + probs * value_band_ref[slot, row, :]

            group = 8
            for low in range(0, BLOCK, group):
                product_ref[slot, low // group] = lag_back(powers[slot], term_of, low, group)
            gain_ref[tile, 0] = lag_back(
                powers[slot][group.bit_length() - 1 :], lambda index, slot=slot: product_ref[slot, index], 0, BLOCK // group, group
            )
        for slot, tile in both:
            mixing = (from_band(band_ref[slot]) * scale).astype(jnp.bfloat16)
            reach = stacked(d_scores[slot] * fades[slot] * scale, lanes)
            held = stacked(prob_ref[tile] * fades[slot], lanes).astype(jnp.bfloat16)
            d_qkv_ref[rows_of(tile), :width] = (
                dot_nn(mixing, keys[slot])
                + dot_nn(reach.T.astype(jnp.bfloat16), state_ref[tile, :, :width].astype(jnp.bfloat16))
            ).astype(jnp.bfloat16)
            adjoint_ref[tile, :, :width] = dot_nn(reach.astype(jnp.bfloat16), queries[slot])
            adjoint_ref[tile, :, width:] = dot_nn(held, backs[slot])
            d_qkv_ref[rows_of(tile), width : 2 * width] = dot_nn(mixing.T, queries[slot]).astype(jnp.bfloat16)
            d_qkv_ref[rows_of(tile), 2 * width : 3 * width] = dot_nn(mix_ref[tile].T, backs[slot]).astype(jnp.bfloat16)
        return none

    lax.fori_loop(0, tiles // PAIR, slopes, 0)

    carry_ref[...] = jnp.zeros_like(carry_ref)
    end_ref[...] = jnp.zeros_like(end_ref)

    def run_adjoints(count, none):
        tile = tiles - 1 - count
        for part in (1, 0):
            span = pl.ds(part * BLOCK, BLOCK)
            fade = gain_ref[tile, 5, :, part * BLOCK : part * BLOCK + 1]
            carried = carry_ref[...]
            added = adjoint_ref[tile, span, :]
            adjoint_ref[tile, span, :] = carried
            cross_ref[tile, span, :] = jnp.broadcast_to(
                jnp.sum(carried * end_ref[...], axis=1, keepdims=True), (BLOCK, TILE)
            )
            end_ref[...] = state_ref[tile, span, :]
            carry_ref[...] = fade * carried + added
        return none

    lax.fori_loop(0, tiles, run_adjoints, 0)

    d_bias_ref[...] = jnp.zeros_like(d_bias_ref)

    def finish(tile, none):
        key_rows = qkv_ref[rows_of(tile), width : 2 * width]
        value_rows = qkv_ref[rows_of(tile), 2 * width :]
        adjoint = adjoint_ref[tile]
        high, low = split_low(adjoint)
        rows = qkv_ref[rows_of(tile), width:]
        carried = own_block(dot_nt(high, rows) + dot_nt(low, rows), lanes)
        decay, writes, rest = gain_ref[tile, 2], gain_ref[tile, 3], gain_ref[tile, 4]
        d_writes = gain_ref[tile, 0] + rest * carried
        tail = stacked(rest * writes, lanes).T.astype(jnp.bfloat16)
        d_qkv_ref[rows_of(tile), width : 3 * width] = (
            d_qkv_ref[rows_of(tile), width : 3 * width].astype(jnp.float32) + dot_nn(tail, high)
        ).astype(jnp.bfloat16)
        cross = own_block(cross_ref[tile], lanes)
        d_decay = suffix_sum(gain_ref[tile, 1] - writes * d_writes, place) + cross - decay * d_writes
        logits = logit_ref[tile] + bias
        d_logit = valid_of(tile) * d_decay * jax.nn.sigmoid(-logits) * 0.125
        d_bias_ref[...] += jnp.broadcast_to(jnp.sum(d_logit, axis=1, keepdims=True), (BLOCK, TILE))
        d_qkv_ref[rows_of(tile), 3 * width :] = jnp.concatenate([d_logit, jnp.zeros_like(d_logit)], axis=0).T.astype(jnp.bfloat16)
        return none

    lax.fori_loop(0, tiles, finish, 0)


def mixer_forward(length, qkv, logits, bias):
    rows, width = qkv.shape[0], qkv.shape[1] // 3
    tiles = rows // TILE
    f32 = jnp.float32
    return pl.pallas_call(
        forward_kernel,
        out_shape=(
            jax.ShapeDtypeStruct((rows, width), jnp.bfloat16),
            jax.ShapeDtypeStruct((tiles, TILE, 2 * width), f32),
            jax.ShapeDtypeStruct((tiles, BLOCK, TILE), f32),
            jax.ShapeDtypeStruct((tiles, BLOCK, TILE), f32),
            jax.ShapeDtypeStruct((tiles, TILE, TILE), jnp.bfloat16),
        ),
        in_specs=[pl.BlockSpec(memory_space=pltpu.SMEM)] + [pl.BlockSpec(memory_space=pltpu.VMEM)] * 3,
        out_specs=[pl.BlockSpec(memory_space=pltpu.VMEM)] * 5,
        scratch_shapes=[
            pltpu.VMEM((tiles, 4, BLOCK, TILE), f32),
            pltpu.VMEM((BLOCK, 2 * width), f32),
            pltpu.VMEM((PAIR, TILE, TILE), f32),
            pltpu.VMEM((PAIR, TILE, TILE), f32),
            pltpu.VMEM((PAIR, BLOCK, BLOCK, TILE), f32),
        ],
        name="mixer_forward",
    )(length, qkv, logits, bias)


def mixer_backward(length, qkv, logits, bias, back, saved):
    rows, width = qkv.shape[0], qkv.shape[1] // 3
    tiles = rows // TILE
    f32 = jnp.float32
    return pl.pallas_call(
        backward_kernel,
        out_shape=(
            jax.ShapeDtypeStruct((rows, 3 * width + 2 * BLOCK), jnp.bfloat16),
            jax.ShapeDtypeStruct((BLOCK, TILE), f32),
        ),
        in_specs=[pl.BlockSpec(memory_space=pltpu.SMEM)] + [pl.BlockSpec(memory_space=pltpu.VMEM)] * 8,
        out_specs=[pl.BlockSpec(memory_space=pltpu.VMEM)] * 2,
        scratch_shapes=[
            pltpu.VMEM((tiles, TILE, 2 * width), f32),
            pltpu.VMEM((tiles, 6, BLOCK, TILE), f32),
            pltpu.VMEM((PAIR, TILE, TILE), f32),
            pltpu.VMEM((PAIR, TILE, TILE), f32),
            pltpu.VMEM((PAIR, TILE, TILE), f32),
            pltpu.VMEM((BLOCK, 2 * width), f32),
            pltpu.VMEM((BLOCK, 2 * width), f32),
            pltpu.VMEM((tiles, TILE, TILE), f32),
            pltpu.VMEM((PAIR, BLOCK, BLOCK, TILE), f32),
        ],
        name="mixer_backward",
    )(length, qkv, logits, bias, back, *saved)


def to_low(values):
    return values.astype(jnp.bfloat16)


def to_wide(values):
    return values.astype(jnp.float32)


def dot_tn(left, right):
    return lax.dot_general(left, right, (((0,), (0,)), ((), ())), preferred_element_type=jnp.float32)


def tie(values, *earlier):
    return lax.optimization_barrier((values,) + earlier)[0]


def ring_order(size):
    return list(range(0, size, 2)) + list(range(size - 1 - size % 2, 0, -2))


def hop_pairs(order, hop):
    size = len(order)
    return [(order[i], order[(i + hop) % size]) for i in range(size)]


def ring_gather(shard, order):
    size = len(order)
    up, down = hop_pairs(order, 1), hop_pairs(order, -1)
    pieces = [shard] + [None] * (size - 1)
    from_low, from_high = shard, shard
    for step in range(1, (size + 1) // 2):
        from_low = lax.ppermute(from_low, DP, up)
        from_high = lax.ppermute(from_high, DP, down)
        pieces[size - step], pieces[step] = from_low, from_high
    if size % 2 == 0:
        half = shard.shape[0] // 2
        first = lax.ppermute(from_low[:half], DP, up)
        second = lax.ppermute(from_high[half:], DP, down)
        pieces[size // 2] = (first, second)
    return pieces


def ring_scatter(piece_of, order):
    size = len(order)
    up, down = hop_pairs(order, 1), hop_pairs(order, -1)
    half_count = (size - 1) // 2
    up_sum, down_sum = None, None
    if size % 2 == 0:
        farthest = piece_of(size // 2)
        half = farthest.shape[0] // 2
        up_half = lax.ppermute(to_low(farthest[:half]), DP, up)
        down_half = lax.ppermute(to_low(farthest[half:]), DP, down)
        up_sum = jnp.concatenate([to_wide(up_half), jnp.zeros(up_half.shape, jnp.float32)], axis=0)
        down_sum = jnp.concatenate([jnp.zeros(down_half.shape, jnp.float32), to_wide(down_half)], axis=0)
    for step in range(half_count, 0, -1):
        up_piece, down_piece = to_wide(piece_of(step)), to_wide(piece_of(size - step))
        if up_sum is not None:
            up_piece, down_piece = up_piece + up_sum, down_piece + down_sum
        up_sum = to_wide(lax.ppermute(to_low(up_piece), DP, up))
        down_sum = to_wide(lax.ppermute(to_low(down_piece), DP, down))
    return piece_of(0), to_low(up_sum), to_low(down_sum)


def total_sum(values, axis):
    count = lax.axis_size(axis)
    step = 1
    while step < count:
        values = values + lax.ppermute(values, axis, [(i, i ^ step) for i in range(count)])
        step *= 2
    return values


def move_kernel(places_ref, source_ref, target_ref):
    target_ref[...] = source_ref[...]


def move_columns(matrix, places, inverse):
    size = places.shape[0]
    rows, columns = matrix.shape
    width = columns // size
    if width % 128:
        split = matrix.reshape(rows, size, width)
        if inverse:
            places = jnp.argsort(places)
        return jnp.take(split, places, axis=1).reshape(rows, columns)

    def plain(step, places_ref):
        return (0, step)

    def placed(step, places_ref):
        return (0, places_ref[step])

    return pl.pallas_call(
        move_kernel,
        out_shape=jax.ShapeDtypeStruct(matrix.shape, matrix.dtype),
        grid_spec=pltpu.PrefetchScalarGridSpec(
            num_scalar_prefetch=1,
            grid=(size,),
            in_specs=[pl.BlockSpec((rows, width), plain if inverse else placed)],
            out_specs=pl.BlockSpec((rows, width), placed if inverse else plain),
        ),
        cost_estimate=pl.CostEstimate(flops=0, bytes_accessed=2 * matrix.size * matrix.dtype.itemsize, transcendentals=0),
    )(places, matrix)


ROWS = 128
WIDE = 256
LIMIT = 62 * 1024 * 1024


def vmem_call(body, out_shape, operands, scratch=(), scalars=1, anywhere=0, flops=0, moved=0):
    spaces = (
        [pl.BlockSpec(memory_space=pltpu.SMEM)] * scalars
        + [pl.BlockSpec(memory_space=pltpu.VMEM)] * (len(operands) - scalars - anywhere)
        + [pl.BlockSpec(memory_space=pl.ANY)] * anywhere
    )
    return pl.pallas_call(
        body,
        out_shape=out_shape,
        in_specs=spaces,
        out_specs=[pl.BlockSpec(memory_space=pltpu.VMEM)] * len(out_shape),
        scratch_shapes=list(scratch),
        compiler_params=pltpu.CompilerParams(vmem_limit_bytes=LIMIT),
        cost_estimate=pl.CostEstimate(flops=flops, bytes_accessed=moved, transcendentals=0),
    )(*operands)


def load_blocks(sources, target_ref, sems, blocks, low=0):
    groups = []
    for block in blocks:
        copies = []
        for first, span in block:
            start = 0
            for source in sources:
                rows = source.shape[0]
                index = sum(map(len, groups)) + len(copies)
                copies.append(
                    pltpu.make_async_copy(
                        source.at[:, pl.ds(low + first, span)],
                        target_ref.at[pl.ds(start, rows), pl.ds(first, span)],
                        sems.at[index],
                    )
                )
                start += rows
        groups.append(copies)
    for copies in groups:
        for copy in copies:
            copy.start()
    return groups


def finish(copies):
    for copy in copies:
        copy.wait()


def flat_pieces(pieces):
    flat = []
    for piece in pieces:
        flat += list(piece) if isinstance(piece, tuple) else [piece]
    return flat


def give_halves(block_ref, parity, parts, columns, kept_refs, sent_refs):
    rows = block_ref.shape[0] // parts // 2
    for part in range(parts):
        kept_refs[part][:, columns] = block_ref[pl.ds((2 * part + parity) * rows, rows), :].astype(jnp.bfloat16)
        sent_refs[part][:, columns] = block_ref[pl.ds((2 * part + 1 - parity) * rows, rows), :].astype(jnp.bfloat16)


def project_call(left, pieces, parity, parts, low, keep):
    rows, depth = left.shape
    flat = flat_pieces(pieces)
    count = len(flat)
    total = sum(piece.shape[0] for piece in flat)

    def body(parity_ref, left_ref, *refs):
        sources, outs = refs[:count], refs[count:]
        block_ref, sems = outs[-2:]
        weight_ref = outs[-3]
        finish(load_blocks(sources, weight_ref, sems, [[(0, depth)]], low)[0])
        parity = parity_ref[0]

        def one(step, none):
            columns = pl.ds(pl.multiple_of(step * WIDE, WIDE), WIDE)
            block_ref[...] = dot_nt(left_ref[...], weight_ref[columns, :])
            give_halves(block_ref, parity, parts, columns, outs[:parts], outs[parts : 2 * parts])
            return none

        lax.fori_loop(0, total // WIDE, one, 0)

    half = jax.ShapeDtypeStruct((rows // parts // 2, total), jnp.bfloat16)
    weight = (total, depth)
    outs = vmem_call(
        body,
        [half] * (2 * parts) + ([jax.ShapeDtypeStruct(weight, jnp.bfloat16)] if keep else []),
        (parity, left, *flat),
        scratch=([] if keep else [pltpu.VMEM(weight, jnp.bfloat16)])
        + [
            pltpu.VMEM((rows, WIDE), jnp.float32),
            pltpu.SemaphoreType.DMA((count,)),
        ],
        anywhere=count, flops=2 * rows * depth * total, moved=2 * (rows * depth + depth * total + rows * total),
    )
    return outs[:parts], outs[parts : 2 * parts], outs[2 * parts :]


def query_call(rows_low, factor, pieces, slots, columns_all):
    rows, depth = rows_low.shape
    flat = flat_pieces(pieces)
    count = len(flat)
    wide = columns_all - 2 * slots
    blocks = [[(wide, 2 * slots)]] + [[(start, 2 * WIDE)] for start in range(0, wide, 2 * WIDE)]

    def body(rows_ref, factor_ref, *refs):
        sources = refs[:count]
        qkv_ref, logit_ref, normed_ref, gain_ref, weight_ref, sems = refs[count:]
        groups = load_blocks(sources, weight_ref, sems, blocks)
        finish(groups[0])
        gain_ref[...] = weight_ref[:, wide:].astype(jnp.float32).T[slots : slots + 8]

        def norm_rows(step, none):
            span = pl.ds(pl.multiple_of(step * TILE, TILE), TILE)
            values = rows_ref[span, :].astype(jnp.float32)
            normed_ref[span, :] = (values * factor_ref[span, :] * gain_ref[0:1, :]).astype(jnp.bfloat16)
            return none

        lax.fori_loop(0, rows // TILE, norm_rows, 0)
        logits = dot_nn(normed_ref[...], weight_ref[:, wide:])
        for tile in range(rows // TILE):
            logit_ref[tile] = logits[tile * TILE : (tile + 1) * TILE, :].T[:slots]
        for copies in groups[1:]:
            finish(copies)

        def one(step, none):
            columns = pl.ds(pl.multiple_of(step * WIDE, WIDE), WIDE)
            qkv_ref[:, columns] = dot_nn(normed_ref[...], weight_ref[:, columns]).astype(jnp.bfloat16)
            return none

        lax.fori_loop(0, wide // WIDE, one, 0)

    return vmem_call(
        body,
        [
            jax.ShapeDtypeStruct((rows, wide), jnp.bfloat16),
            jax.ShapeDtypeStruct((rows // TILE, slots, TILE), jnp.float32),
            jax.ShapeDtypeStruct((rows, depth), jnp.bfloat16),
            jax.ShapeDtypeStruct((8, depth), jnp.float32),
        ],
        (rows_low, factor, *flat),
        scratch=[pltpu.VMEM((depth, columns_all), jnp.bfloat16), pltpu.SemaphoreType.DMA((count * len(blocks),))],
        scalars=0, anywhere=count,
        flops=2 * rows * depth * columns_all, moved=2 * (rows + columns_all) * depth + 2 * rows * columns_all,
    )


def feed_call(normed, back, pieces, parity, earlier, parts):
    rows, depth = normed.shape
    flat = flat_pieces(pieces)
    count = len(flat)
    hidden = flat[0].shape[1] // 3
    given = 0 if earlier is None else 2
    blocks = [
        [(part * hidden, WIDE) for part in range(3)],
        [(part * hidden + WIDE, hidden - WIDE) for part in range(3)],
    ]

    def body(parity_ref, *refs):
        sources = refs[: count + 2 + given]
        outs = refs[count + 2 + given :]
        hidden_ref, pair_ref = outs[:2]
        total_refs = outs[2 : 4 if earlier is None else 4 + 2 * parts]
        outs = outs[2 + len(total_refs) :]
        weight_ref, normed_ref, back_ref, block_ref = outs[:4]
        sems = outs[-1]
        held = [
            pltpu.make_async_copy(sources[count], normed_ref, sems.at[6 * count]),
            pltpu.make_async_copy(sources[count + 1], back_ref, sems.at[6 * count + 1]),
        ]
        held[0].start()
        held[1].start()
        groups = load_blocks(sources[:count], weight_ref, sems, blocks)
        if given:
            sum_ref = outs[4]
            held += [
                pltpu.make_async_copy(sources[count + 2 + i], sum_ref.at[i], sems.at[6 * count + 2 + i]) for i in range(2)
            ]
            held[2].start()
            held[3].start()

        def act(start, span):
            def columns(base):
                return pl.ds(start + base, span)

            gate_act = dot_nn(normed_ref[...], weight_ref[:, columns(0)])
            up_act = dot_nn(normed_ref[...], weight_ref[:, columns(hidden)])
            d_hidden = dot_nn(back_ref[...], weight_ref[:, columns(2 * hidden)])
            sigma = 1.0 / (1.0 + jnp.exp(-gate_act))
            gated = gate_act * sigma
            hidden_ref[:, columns(0)] = (gated * up_act).astype(jnp.bfloat16)
            pair_ref[:, columns(hidden)] = (d_hidden * gated).astype(jnp.bfloat16)
            pair_ref[:, columns(0)] = (
                d_hidden * up_act * (sigma * (1.0 + gate_act * (1.0 - sigma)))
            ).astype(jnp.bfloat16)

        finish(held[:2])
        finish(groups[0])
        act(0, WIDE)
        for copies in groups[1:]:
            finish(copies)

        def act_wide(step, none):
            act(pl.multiple_of(step * WIDE, WIDE), WIDE)
            return none

        lax.fori_loop(1, hidden // WIDE, act_wide, 0)
        if hidden % WIDE:
            act(hidden // WIDE * WIDE, hidden % WIDE)
        finish(held[2:])
        parity = parity_ref[0]

        def one(step, none):
            columns = pl.ds(pl.multiple_of(step * WIDE, WIDE), WIDE)
            d_block = dot_nt(pair_ref[...], weight_ref[columns, : 2 * hidden])
            y_block = dot_nt(hidden_ref[...], weight_ref[columns, 2 * hidden :])
            if not given:
                total_refs[0][:, columns] = d_block.astype(jnp.bfloat16)
                total_refs[1][:, columns] = y_block.astype(jnp.bfloat16)
            else:
                block_ref[...] = d_block + sum_ref[0, :, columns].astype(jnp.float32)
                give_halves(block_ref, parity, parts, columns, total_refs[:parts], total_refs[parts : 2 * parts])
                block_ref[...] = y_block + sum_ref[1, :, columns].astype(jnp.float32)
                give_halves(block_ref, parity, 1, columns, total_refs[2 * parts :][:1], total_refs[2 * parts + 1 :])
            return none

        lax.fori_loop(0, depth // WIDE, one, 0)

    low = jnp.bfloat16
    outs = [jax.ShapeDtypeStruct((rows, hidden), low), jax.ShapeDtypeStruct((rows, 2 * hidden), low)]
    if earlier is None:
        outs += [jax.ShapeDtypeStruct((rows, depth), low)] * 2
    else:
        outs += [jax.ShapeDtypeStruct((rows // parts // 2, depth), low)] * (2 * parts)
        outs += [jax.ShapeDtypeStruct((rows // 2, depth), low)] * 2
    scratch = [
        pltpu.VMEM((depth, 3 * hidden), low),
        pltpu.VMEM((rows, depth), low),
        pltpu.VMEM((rows, depth), low),
        pltpu.VMEM((rows, WIDE), jnp.float32),
    ]
    if given:
        scratch.append(pltpu.VMEM((2, rows, depth), low))
    scratch.append(pltpu.SemaphoreType.DMA((6 * count + 2 + given,)))
    return vmem_call(
        body, outs, (parity, *flat, normed, back, *(earlier or ())),
        scratch=scratch, anywhere=count + 2 + given,
        flops=2 * rows * depth * hidden * 6, moved=2 * (3 * rows * depth + 3 * depth * hidden + 3 * rows * hidden),
    )


def sum_specs(parts, steps, rows, depth):
    share = steps // parts // 2

    def spec(index):
        return pl.BlockSpec((rows, depth), lambda step, scalars: (jnp.clip(step - index * share, 0, share - 1), 0))

    return [spec(index) for index in range(2 * parts)]


def place_row(parts, steps):
    share = steps // parts // 2

    def place(step, scalars):
        span = step // share
        part, other = span // 2, span % 2
        half = jnp.where(other == 0, scalars[0], 1 - scalars[0])
        return ((2 * part + half) * share + step % share, 0)

    return place


def pick_sum(step, share, refs):
    value = refs[0][...]
    for index, ref in enumerate(refs[1:]):
        value = jnp.where(step >= (index + 1) * share, ref[...], value)
    return value.astype(jnp.float32)


def row_call(body, scalars, parts, sums, whole, fixed, outs, narrow=()):
    rows, depth = whole[0].shape
    steps = rows // ROWS
    place = place_row(parts, steps)
    block = pl.BlockSpec((ROWS, depth), place)
    ones = [pl.BlockSpec(array.shape, lambda step, scalars: (0, 0)) for array in fixed]
    moved = sum(a.size * a.dtype.itemsize for a in list(sums) + list(whole))
    moved += sum(rows * depth * jnp.dtype(kind).itemsize for kind in outs)
    return pl.pallas_call(
        body,
        out_shape=[jax.ShapeDtypeStruct((rows, depth), kind) for kind in outs]
        + [jax.ShapeDtypeStruct((rows, count), jnp.bfloat16) for count in narrow],
        grid_spec=pltpu.PrefetchScalarGridSpec(
            num_scalar_prefetch=1,
            grid=(steps,),
            in_specs=sum_specs(parts, steps, ROWS, depth) + [block] * len(whole) + ones,
            out_specs=[block] * len(outs) + [pl.BlockSpec((ROWS, count), place) for count in narrow],
        ),
        compiler_params=pltpu.CompilerParams(vmem_limit_bytes=LIMIT),
        cost_estimate=pl.CostEstimate(flops=10 * rows * depth, bytes_accessed=moved, transcendentals=0),
    )(scalars, *sums, *whole, *fixed)


def norm_factor(values):
    return lax.rsqrt(jnp.mean(values * values, axis=-1, keepdims=True) + epsilon)


def norm_call(scalars, sums, rows_in, gain):
    parts, steps = len(sums) // 2, rows_in.shape[0] // ROWS

    def body(scalar_ref, *refs):
        sum_refs = refs[: 2 * parts]
        rows_ref, gain_ref, resid_ref, normed_ref = refs[2 * parts :]
        total = pick_sum(pl.program_id(0), steps // parts // 2, sum_refs)
        resid = rows_ref[...].astype(jnp.float32) + total
        resid_ref[...] = resid.astype(jnp.bfloat16)
        normed_ref[...] = (resid * norm_factor(resid) * gain_ref[...]).astype(jnp.bfloat16)

    return row_call(body, scalars, parts, sums, [rows_in], [gain], [jnp.bfloat16, jnp.bfloat16])


def norm_back(total, values, gain):
    factor = norm_factor(values)
    hat = values * factor
    scaled = gain * total
    return factor * (scaled - hat * jnp.mean(scaled * hat, axis=-1, keepdims=True))


def norm_back_call(scalars, sums, resid, back, gain, full_out):
    parts, steps = len(sums) // 2, resid.shape[0] // ROWS

    def body(scalar_ref, *refs):
        sum_refs = refs[: 2 * parts]
        resid_ref, back_ref, gain_ref, out_ref, d_attn_ref, d_mixed_ref = refs[2 * parts :]
        total = pick_sum(pl.program_id(0), steps // parts // 2, sum_refs)
        slope = norm_back(total, resid_ref[...].astype(jnp.float32), gain_ref[...])
        d_attn = (back_ref[...].astype(jnp.float32) + slope).astype(jnp.bfloat16)
        d_attn_ref[...] = d_attn
        d_mixed_ref[...] = dot_nn(d_attn, out_ref[...]).astype(jnp.bfloat16)

    return row_call(body, scalars, parts, sums, [resid, back], [gain, full_out], [jnp.bfloat16], [full_out.shape[1]])


def store_placed(target_ref, values, scalar_ref, size):
    share = values.shape[1] // size
    if share % 128:
        target_ref[...] = values
        return
    for index in range(size):
        columns = pl.ds(pl.multiple_of(scalar_ref[1 + index] * share, 128), share)
        target_ref[:, columns] = values[:, index * share : (index + 1) * share]


def replaced(matrix, places):
    size = places.shape[0]
    share = matrix.shape[1] // size
    if share % 128 == 0:
        return matrix
    return jnp.take(matrix.reshape(-1, size, share), jnp.argsort(places), axis=1).reshape(matrix.shape)


def last_call(scalars, sums, d_resid, rows_in, gain, size):
    parts, steps = len(sums) // 2, rows_in.shape[0] // ROWS

    def body(scalar_ref, *refs):
        sum_refs = refs[: 2 * parts]
        d_resid_ref, rows_ref, gain_ref, out_ref = refs[2 * parts :]
        total = pick_sum(pl.program_id(0), steps // parts // 2, sum_refs)
        slope = norm_back(total, rows_ref[...].astype(jnp.float32), gain_ref[...])
        store_placed(out_ref, d_resid_ref[...].astype(jnp.float32) + slope, scalar_ref, size)

    (out,) = row_call(body, scalars, parts, sums, [d_resid, rows_in], [gain], [jnp.float32])
    return replaced(out, scalars[1:])


def output_call(scalars, sums, resid, size):
    parts, steps = len(sums) // 2, resid.shape[0] // ROWS

    def body(scalar_ref, *refs):
        sum_refs = refs[: 2 * parts]
        resid_ref, out_ref = refs[2 * parts :]
        total = pick_sum(pl.program_id(0), steps // parts // 2, sum_refs)
        store_placed(out_ref, (resid_ref[...].astype(jnp.float32) + total).astype(jnp.bfloat16), scalar_ref, size)

    (out,) = row_call(body, scalars, parts, sums, [resid], [], [jnp.bfloat16])
    return replaced(out, scalars[1:])


def sum_refs_of(refs):
    total = refs[0][...].astype(jnp.float32)
    for ref in refs[1:]:
        total = total + ref[...].astype(jnp.float32)
    return total


def finish_feed(grads, w_gate, w_up, spans):
    share, count = w_gate.shape

    def body(*refs):
        grad_refs = refs[: len(grads)]
        gate_ref, up_ref, d_gate_ref, d_up_ref, d_down_ref, gain_ref = refs[len(grads) :]
        for index, (low, high) in enumerate(spans):
            span = high - low
            total = sum_refs_of(grad_refs[3 * index : 3 * index + 3])
            d_gate_ref[:, low:high] = total[:, :span]
            d_up_ref[:, low:high] = total[:, span : 2 * span]
            d_down_ref[low:high, :] = total[:, 2 * span :].T
        gain_ref[...] = jnp.sum(
            gate_ref[...].astype(jnp.float32) * d_gate_ref[...] + up_ref[...].astype(jnp.float32) * d_up_ref[...],
            axis=1, keepdims=True,
        )

    shapes = [(share, count), (share, count), (count, share), (share, 1)]
    return vmem_call(
        body, [jax.ShapeDtypeStruct(shape, jnp.float32) for shape in shapes],
        (*grads, w_gate, w_up), scalars=0, moved=share * count * 36,
    )


def finish_mix(grads, mix_shard, width, slots):
    share = mix_shard.shape[0]
    used, start = 3 * width + slots, 3 * width + 2 * BLOCK

    def body(*refs):
        grad_refs = refs[: len(grads)]
        shard_ref, query_ref, key_ref, value_ref, slot_ref, out_ref, gain_ref = refs[len(grads) :]
        total = sum_refs_of(grad_refs)
        for index, ref in enumerate((query_ref, key_ref, value_ref)):
            ref[...] = total[:, index * width : (index + 1) * width]
        slot_ref[...] = total[:, 3 * width : used]
        out_ref[...] = total[:, start:].T
        gain_ref[...] = jnp.sum(shard_ref[:, :used].astype(jnp.float32) * total[:, :used], axis=1, keepdims=True)

    shapes = [(share, width)] * 3 + [(share, slots), (width, share), (share, 1)]
    return vmem_call(
        body, [jax.ShapeDtypeStruct(shape, jnp.float32) for shape in shapes],
        (*grads, mix_shard), scalars=0, moved=share * start * 14,
    )


def exchange(kept, sent):
    heads = lax.axis_size(HEAD)
    near = [(i, i ^ 1) for i in range(heads)]
    far = [(i, i ^ 2) for i in range(heads)]
    sums = []
    for own, given in zip(kept, sent):
        own = to_low(to_wide(own) + to_wide(lax.ppermute(given, HEAD, near)))
        own = to_low(to_wide(own) + to_wide(lax.ppermute(own, HEAD, far)))
        sums += [own, lax.ppermute(own, HEAD, near)]
    return sums


def layer(
    inputs,
    lengths,
    gain_attn,
    w_query,
    w_key,
    w_value,
    w_slot,
    gate_bias,
    w_out,
    gain_ffn,
    w_gate,
    w_up,
    w_down,
    cotangent,
):
    size = lax.axis_size(DP)
    order = ring_order(size)
    spots = [order.index(i) for i in range(size)]
    spot = jnp.array(spots, jnp.int32)[lax.axis_index(DP)]
    places = jnp.array(order + order, jnp.int32)[spot + jnp.arange(size, dtype=jnp.int32)]
    parity = jnp.bitwise_and(lax.axis_index(HEAD), 1).astype(jnp.int32)[None]
    scalars = jnp.concatenate([parity, places])
    share = gain_attn.shape[0]
    width, slots = w_query.shape[1], w_slot.shape[1]
    hidden_count = w_gate.shape[1]
    cut = (hidden_count // WIDE + 1) // 2 * WIDE
    spans = [(0, cut), (cut, hidden_count)]

    spare = jnp.zeros((share, 2 * BLOCK - slots - 2), w_slot.dtype)
    mix_shard = jnp.concatenate(
        [w_query, w_key, w_value, w_slot, gain_attn[:, None], gain_ffn[:, None], spare, w_out.T], axis=1
    )
    mix_count = 3 * width + 2 * BLOCK
    mix_pieces = ring_gather(mix_shard, order)
    down_rows = w_down.T
    feed_pieces = []
    for low, high in spans:
        shard = jnp.concatenate([w_gate[:, low:high], w_up[:, low:high], down_rows[:, low:high]], axis=1)
        feed_pieces.append(ring_gather(tie(shard, *flat_pieces([mix_pieces[size // 2]])), order))

    rows_low = move_columns(inputs, places, False)
    factor = norm_factor(to_wide(rows_low))
    back_low = move_columns(cotangent, places, False)
    rows_low, factor, _ = lax.optimization_barrier((rows_low, factor, back_low))

    qkv, logits, normed, gains = query_call(rows_low, factor, mix_pieces, slots, mix_count)
    gain_one, gain_two = gains[0:1], gains[1:2]
    bias = gate_bias[:, None]
    mixed, *saved = mixer_forward(lengths, qkv, logits, bias)
    kept, sent, (full_out,) = project_call(mixed, mix_pieces, parity, 2, mix_count, True)
    sums = exchange(kept, sent)
    resid, normed_two = norm_call(scalars, sums, rows_low, gain_two)

    middle = size // 2

    def grads_of(pairs):
        span = slice(middle * share, (middle + 1) * share)
        far = to_low(jnp.concatenate([dot_tn(left[:, span], right) for left, right in pairs], axis=1))
        grads = [to_low(dot_tn(left, right)) for left, right in pairs]

        def piece_of(index):
            if index == middle:
                return far
            return jnp.concatenate([grad[index * share : (index + 1) * share] for grad in grads], axis=1)

        return piece_of

    partial, feed_grads = None, []
    for pieces in feed_pieces:
        hidden, pair, *partial = feed_call(normed_two, back_low, pieces, parity, partial, 2)
        piece_of = grads_of([(normed_two, pair), (back_low, hidden)])
        feed_grads += ring_scatter(piece_of, order)

    sums = exchange(partial[:2], partial[2:4])
    d_attn, d_mixed = norm_back_call(scalars, sums, resid, back_low, gain_two, full_out)
    d_all, d_bias = mixer_backward(lengths, qkv, logits, bias, d_mixed, saved)
    bias_sum = total_sum(d_bias[:, 0], DP)
    mix_grads = ring_scatter(grads_of([(normed, d_all), (d_attn, mixed)]), order)
    kept, sent, _ = project_call(d_all, mix_pieces, parity, 2, 0, False)
    sums = exchange(kept, sent)
    early = exchange([partial[4]], partial[5:])
    output = output_call(scalars, early, resid, size)
    *feed_out, gain_sum_two = finish_feed(feed_grads, w_gate, w_up, spans)
    sums[0] = tie(sums[0], output)
    grad_inputs = last_call(scalars, sums, d_attn, rows_low, gain_one, size)
    *mix_out, gain_sum_one = finish_mix(mix_grads, mix_shard, width, slots)
    gain_sums = total_sum(jnp.stack([gain_sum_one[:, 0], gain_sum_two[:, 0]]), HEAD)

    return (
        output,
        grad_inputs,
        gain_sums[0] / to_wide(gain_attn),
        *mix_out[:4],
        bias_sum,
        mix_out[4],
        gain_sums[1] / to_wide(gain_ffn),
        *feed_out,
    )


def solution(mesh):
    in_specs = (
        P(DP, None),
        P(DP),
        P(DP),
        P(DP, HEAD),
        P(DP, HEAD),
        P(DP, HEAD),
        P(DP, HEAD),
        P(HEAD),
        P(HEAD, DP),
        P(DP),
        P(DP, HEAD),
        P(DP, HEAD),
        P(HEAD, DP),
        P(DP, None),
    )
    out_specs = (
        P(DP, None),
        P(DP, None),
        P(DP),
        P(DP, HEAD),
        P(DP, HEAD),
        P(DP, HEAD),
        P(DP, HEAD),
        P(HEAD),
        P(HEAD, DP),
        P(DP),
        P(DP, HEAD),
        P(DP, HEAD),
        P(HEAD, DP),
    )
    return jax.shard_map(layer, mesh=mesh, in_specs=in_specs, out_specs=out_specs, check_vma=False)
```

profile of v0, /device:TPU:0, one launch (start us, length us, event | category | flops | bytes accessed | tf_op | source)
XLA Modules:
  0.0 823.9 jit_solution(614389421341761613)
XLA Ops:
  9.8 24.5 %collective-permute-done.4.refs_1_ = bf16[256,2176]{1,0:T(8,128)(2,1)S(1)} collective-permute-done((bf16[256,2176]{1,0:T(8,128)(2,1)S(1)}, bf16[256,2176]{1,0:T(8,128)(2,1)S(1)}, u32[]{:S(2)}, u32[]{:S(2)}) %collective-permute-start.4) | collective-permute-done | bytes 1114144 | tf_op jit(solution)/shard_map/ppermute | solution.py:420
  37.1 23.1 %collective-permute-done.5.refs_2_ = bf16[256,2176]{1,0:T(8,128)(2,1)} collective-permute-done((bf16[256,2176]{1,0:T(8,128)(2,1)S(1)}, bf16[256,2176]{1,0:T(8,128)(2,1)}, u32[]{:S(2)}, u32[]{:S(2)}) %collective-permute-start.5) | collective-permute-done | bytes 1114144 | tf_op jit(solution)/shard_map/ppermute | solution.py:420
  66.8 7.4 shard_map.256.refs_10_.refs_5_
  103.3 16.3 %shard_map.257 = (bf16[1024,1536]{1,0:T(8,128)(2,1)}, f32[8,64,128]{2,1,0:T(8,128)}, bf16[1024,2048]{1,0:T(8,128)(2,1)}, f32[8,2048]{1,0:T(8,128)}) custom-call(bf16[1024,2048]{1,0:T(8,128)(2,1)} %shard_map.255.rows_ref.refs_4_.refs_5_, f32[1024,1]{1,0:T(8,128)} %copy.46.factor_ref, bf16[256,2176]{1,0:T(8,128)(2,1)} %copy-done.2, ...), custom_call_target="tpu_custom_call" | custom-call | flops 6979321856 | bytes 14417920 | tf_op jit(solution)/shard_map/pallas_call | solution.py:504
  119.6 25.6 %mixer_forward.1 = (bf16[1024,512]{1,0:T(8,128)(2,1)}, f32[8,128,1024]{2,1,0:T(8,128)}, f32[8,64,128]{2,1,0:T(8,128)}, f32[8,64,128]{2,1,0:T(8,128)}, bf16[8,128,128]{2,1,0:T(8,128)(2,1)}) custom-call(s32[1]{0:T(128)S(6)} %copy.62.length_ref, bf16[1024,1536]{1,0:T(8,128)(2,1)} %get-tuple-element.67.qkv_ref, f32[8,64,128]{2,1,0:T(8,128)} %get-tuple-element.68.logit_ref, ...), custom_call_target="tpu_custom_call" | custom-call | tf_op jit(solution)/shard_map/mixer_forward/pallas_call | solution.py:339
  145.2 10.0 %shard_map.258 = (bf16[256,2048]{1,0:T(8,128)(2,1)}, bf16[256,2048]{1,0:T(8,128)(2,1)}, bf16[256,2048]{1,0:T(8,128)(2,1)}, bf16[256,2048]{1,0:T(8,128)(2,1)}, bf16[2048,512]{1,0:T(8,128)(2,1)}) custom-call(s32[1]{0:T(128)} %bitcast.parity_ref, bf16[1024,512]{1,0:T(8,128)(2,1)} %get-tuple-element.69.left_ref, bf16[256,2176]{1,0:T(8,128)(2,1)} %copy-done.2, ...), custom_call_target="tpu_custom_call" | custom-call | flops 2147483648 | bytes 7340032 | tf_op jit(solution)/shard_map/pallas_call | solution.py:504
  162.2 18.9 %collective-permute-done.11.refs_8_ = bf16[256,1920]{1,0:T(8,128)(2,1)S(1)} collective-permute-done((bf16[256,1920]{1,0:T(8,128)(2,1)S(1)}, bf16[256,1920]{1,0:T(8,128)(2,1)S(1)}, u32[]{:S(2)}, u32[]{:S(2)}) %collective-permute-start.11) | collective-permute-done | bytes 983072 | tf_op jit(solution)/shard_map/ppermute | solution.py:419
  184.5 21.8 %collective-permute-done.26.refs_7_ = bf16[256,2304]{1,0:T(8,128)(2,1)S(1)} collective-permute-done((bf16[256,2304]{1,0:T(8,128)(2,1)}, bf16[256,2304]{1,0:T(8,128)(2,1)S(1)}, u32[]{:S(2)}, u32[]{:S(2)}) %collective-permute-start.26) | collective-permute-done | bytes 1179680 | tf_op jit(solution)/shard_map/ppermute | solution.py:419
  207.3 20.1 %collective-permute-done.12.refs_7_ = bf16[256,1920]{1,0:T(8,128)(2,1)S(1)} collective-permute-done((bf16[256,1920]{1,0:T(8,128)(2,1)S(1)}, bf16[256,1920]{1,0:T(8,128)(2,1)S(1)}, u32[]{:S(2)}, u32[]{:S(2)}) %collective-permute-start.12) | collective-permute-done | bytes 983072 | tf_op jit(solution)/shard_map/ppermute | solution.py:419
  232.5 19.5 %collective-permute-done.9.refs_2_ = bf16[256,1920]{1,0:T(8,128)(2,1)S(1)} collective-permute-done((bf16[256,1920]{1,0:T(8,128)(2,1)S(1)}, bf16[256,1920]{1,0:T(8,128)(2,1)S(1)}, u32[]{:S(2)}, u32[]{:S(2)}) %collective-permute-start.9) | collective-permute-done | bytes 983072 | tf_op jit(solution)/shard_map/ppermute | solution.py:420
  254.3 23.0 %collective-permute-done.24.refs_3_ = bf16[256,2304]{1,0:T(8,128)(2,1)S(1)} collective-permute-done((bf16[256,2304]{1,0:T(8,128)(2,1)S(1)}, bf16[256,2304]{1,0:T(8,128)(2,1)S(1)}, u32[]{:S(2)}, u32[]{:S(2)}) %collective-permute-start.24) | collective-permute-done | bytes 1179680 | tf_op jit(solution)/shard_map/ppermute | solution.py:420
  283.2 15.2 %collective-permute-done.10.refs_3_ = bf16[256,1920]{1,0:T(8,128)(2,1)S(1)} collective-permute-done((bf16[256,1920]{1,0:T(8,128)(2,1)S(1)}, bf16[256,1920]{1,0:T(8,128)(2,1)S(1)}, u32[]{:S(2)}, u32[]{:S(2)}) %collective-permute-start.10) | collective-permute-done | bytes 983072 | tf_op jit(solution)/shard_map/ppermute | solution.py:420
  302.4 10.0 %shard_map.259 = (bf16[1024,2048]{1,0:T(8,128)(2,1)}, bf16[1024,2048]{1,0:T(8,128)(2,1)}) custom-call(s32[9]{0:T(128)} %pad_add_fusion.scalar_ref, bf16[256,2048]{1,0:T(8,128)(2,1)} %copy-done.4, bf16[256,2048]{1,0:T(8,128)(2,1)} %copy-done.29, bf16[256,2048]{1,0:T(8,128)(2,1)} %copy-done.5, bf16[256,2048]{1,0:T(8,128)(2,1)} %copy-done.30, ...), custom_call_target="tpu_custom_call" | custom-call | flops 20971520 | bytes 16777216 | tf_op jit(solution)/shard_map/pallas_call | solution.py:784
  312.4 30.1 %shard_map.260 = (bf16[1024,768]{1,0:T(8,128)(2,1)}, bf16[1024,1536]{1,0:T(8,128)(2,1)}, bf16[1024,2048]{1,0:T(8,128)(2,1)}, bf16[1024,2048]{1,0:T(8,128)(2,1)}) custom-call(s32[1]{0:T(128)} %bitcast.parity_ref, bf16[256,2304]{1,0:T(8,128)(2,1)} %pad_maximum_fusion.refs_0_, bf16[256,2304]{1,0:T(8,128)(2,1)} %collective-permute-done.22.refs_1_, ...), custom_call_target="tpu_custom_call" | custom-call | flops 19327352832 | bytes 26738688 | tf_op jit(solution)/shard_map/pallas_call | solution.py:504
  342.5 32.5 %shard_map.261 = (bf16[1024,640]{1,0:T(8,128)(2,1)}, bf16[1024,1280]{1,0:T(8,128)(2,1)}, bf16[256,2048]{1,0:T(8,128)(2,1)}, bf16[256,2048]{1,0:T(8,128)(2,1)}, b...) custom-call(s32[1]{0:T(128)} %bitcast.parity_ref, ...), custom_call_target="tpu_custom_call" | custom-call | flops 16106127360 | bytes 24379392 | tf_op jit(solution)/shard_map/pallas_call | solution.py:504
  395.5 7.8 convolution_convert_fusion.1
  431.0 17.0 %collective-permute-done.62 = bf16[256,1920]{1,0:T(8,128)(2,1)S(1)} collective-permute-done((bf16[256,1920]{1,0:T(8,128)(2,1)S(1)}, bf16[256,1920]{1,0:T(8,128)(2,1)S(1)}, u32[]{:S(2)}, u32[]{:S(2)}) %collective-permute-start.62) | collective-permute-done | bytes 983072 | tf_op jit(solution)/shard_map/ppermute | solution.py:446
  452.7 17.8 %collective-permute-done.54 = bf16[256,2304]{1,0:T(8,128)(2,1)S(1)} collective-permute-done((bf16[256,2304]{1,0:T(8,128)(2,1)S(1)}, bf16[256,2304]{1,0:T(8,128)(2,1)S(1)}, u32[]{:S(2)}, u32[]{:S(2)}) %collective-permute-start.54) | collective-permute-done | bytes 1179680 | tf_op jit(solution)/shard_map/ppermute | solution.py:446
  475.2 13.2 %collective-permute-done.37 = bf16[256,2048]{1,0:T(8,128)(2,1)S(1)} collective-permute-done((bf16[256,2048]{1,0:T(8,128)(2,1)S(1)}, bf16[256,2048]{1,0:T(8,128)(2,1)S(1)}, u32[]{:S(2)}, u32[]{:S(2)}) %collective-permute-start.37) | collective-permute-done | bytes 1048608 | tf_op jit(solution)/shard_map/ppermute | solution.py:943
  499.1 16.9 %collective-permute-done.55 = bf16[256,2304]{1,0:T(8,128)(2,1)S(1)} collective-permute-done((bf16[256,2304]{1,0:T(8,128)(2,1)S(1)}, bf16[256,2304]{1,0:T(8,128)(2,1)S(1)}, u32[]{:S(2)}, u32[]{:S(2)}) %collective-permute-start.55) | collective-permute-done | bytes 1179680 | tf_op jit(solution)/shard_map/ppermute | solution.py:446
  520.6 13.1 %shard_map.263 = (bf16[1024,2048]{1,0:T(8,128)(2,1)}, bf16[1024,512]{1,0:T(8,128)(2,1)}) custom-call(s32[9]{0:T(128)} %pad_add_fusion.scalar_ref, bf16[256,2048]{1,0:T(8,128)(2,1)} %copy-done.6, bf16[256,2048]{1,0:T(8,128)(2,1)} %copy-done.32, bf16[256,2048]{1,0:T(8,128)(2,1)} %copy-done.7, bf16[256,2048]{1,0:T(8,128)(2,1)} %copy-done.33, ...), custom_call_target="tpu_custom_call" | custom-call | flops 20971520 | bytes 16777216 | tf_op jit(solution)/shard_map/pallas_call | solution.py:784
  533.6 52.6 %mixer_backward.1 = (bf16[1024,1664]{1,0:T(8,128)(2,1)}, f32[64,128]{1,0:T(8,128)}) custom-call(s32[1]{0:T(128)S(6)} %copy.62.length_ref, bf16[1024,1536]{1,0:T(8,128)(2,1)} %get-tuple-element.67.qkv_ref, f32[8,64,128]{2,1,0:T(8,128)} %get-tuple-element.68.logit_ref, f32[64,1]{1,0:T(8,128)} %copy.47.bias_ref, bf16[1024,512]{1,0:T(8,128)(2,1)} %get-tuple-element.87.back_ref, ...), custom_call_target="tpu_custom_call" | custom-call | tf_op jit(solution)/shard_map/mixer_backward/pallas_call | solution.py:365
  589.7 10.2 %convolution_convert_fusion.2 = bf16[2048,1664]{1,0:T(8,128)(2,1)S(1)} fusion(bf16[1024,2048]{1,0:T(8,128)(2,1)} %get-tuple-element.99, bf16[1024,1664]{1,0:T(8,128)(2,1)S(1)} %copy-done.52), kind=kOutput, calls=%fused_computation.4 | convolution fusion | flops 6982729728 | bytes 14417920 | tf_op jit(solution)/shard_map/dot_general | solution.py:397
  607.7 16.9 %shard_map.264 = (bf16[256,2048]{1,0:T(8,128)(2,1)}, bf16[256,2048]{1,0:T(8,128)(2,1)}, bf16[256,2048]{1,0:T(8,128)(2,1)}, bf16[256,2048]{1,0:T(8,128)(2,1)}) custom-call(s32[1]{0:T(128)} %bitcast.parity_ref, bf16[1024,1664]{1,0:T(8,128)(2,1)} %get-tuple-element.92.left_ref, bf16[256,2176]{1,0:T(8,128)(2,1)} %copy-done.2, bf16[256,2176]{1,0:T(8,128)(2,1)} %copy-done.21, ...), custom_call_target="tpu_custom_call" | custom-call | flops 6979321856 | bytes 14417920 | tf_op jit(solution)/shard_map/pallas_call | solution.py:504
  631.9 12.9 %collective-permute-done.72 = f32[64]{0:T(128)S(1)} collective-permute-done((f32[64]{0:T(128)S(1)}, f32[64]{0:T(128)S(1)}, u32[]{:S(2)}, u32[]{:S(2)}) %collective-permute-start.72) | collective-permute-done | bytes 288 | tf_op jit(solution)/shard_map/ppermute | solution.py:455
  656.4 37.9 %collective-permute-done.50 = bf16[256,2176]{1,0:T(8,128)(2,1)S(1)} collective-permute-done((bf16[256,2176]{1,0:T(8,128)(2,1)S(1)}, bf16[256,2176]{1,0:T(8,128)(2,1)S(1)}, u32[]{:S(2)}, u32[]{:S(2)}) %collective-permute-start.50) | collective-permute-done | bytes 1114144 | tf_op jit(solution)/shard_map/ppermute | solution.py:447
  698.5 20.5 %collective-permute-done.40 = bf16[256,2048]{1,0:T(8,128)(2,1)S(1)} collective-permute-done((bf16[256,2048]{1,0:T(8,128)(2,1)S(1)}, bf16[256,2048]{1,0:T(8,128)(2,1)S(1)}, u32[]{:S(2)}, u32[]{:S(2)}) %collective-permute-start.40) | collective-permute-done | bytes 1048608 | tf_op jit(solution)/shard_map/ppermute | solution.py:943
  725.9 20.6 %collective-permute-done.47 = bf16[256,2176]{1,0:T(8,128)(2,1)S(1)} collective-permute-done((bf16[256,2176]{1,0:T(8,128)(2,1)S(1)}, bf16[256,2176]{1,0:T(8,128)(2,1)S(1)}, u32[]{:S(2)}, u32[]{:S(2)}) %collective-permute-start.47) | collective-permute-done | bytes 1114144 | tf_op jit(solution)/shard_map/ppermute | solution.py:446
  751.4 20.3 %collective-permute-done.56.refs_1_ = bf16[256,2304]{1,0:T(8,128)(2,1)S(1)} collective-permute-done((bf16[256,2304]{1,0:T(8,128)(2,1)S(1)}, bf16[256,2304]{1,0:T(8,128)(2,1)S(1)}, u32[]{:S(2)}, u32[]{:S(2)}) %collective-permute-start.56) | collective-permute-done | bytes 1179680 | tf_op jit(solution)/shard_map/ppermute | solution.py:446
  782.6 11.2 %collective-permute-done.48.refs_1_ = bf16[256,2176]{1,0:T(8,128)(2,1)} collective-permute-done((bf16[256,2176]{1,0:T(8,128)(2,1)}, bf16[256,2176]{1,0:T(8,128)(2,1)}, u32[]{:S(2)}, u32[]{:S(2)}) %collective-permute-start.48) | collective-permute-done | bytes 1114144 | tf_op jit(solution)/shard_map/ppermute | solution.py:446
  799.0 8.6 %shard_map.262 = bf16[1024,2048]{1,0:T(8,128)(2,1)} custom-call(s32[9]{0:T(128)} %pad_add_fusion.scalar_ref, bf16[512,2048]{1,0:T(8,128)(2,1)} %add_convert_fusion.refs_0_, bf16[512,2048]{1,0:T(8,128)(2,1)} %collective-permute-done.32.refs_1_, bf16[1024,2048]{1,0:T(8,128)(2,1)} %get-tuple-element.81.refs_2_.refs_4_), custom_call_target="tpu_custom_call" | custom-call | flops 20971520 | bytes 12582912 | tf_op jit(solution)/shard_map/pallas_call | solution.py:784
  809.3 12.8 %shard_map.265 = f32[1024,2048]{1,0:T(8,128)} custom-call(s32[9]{0:T(128)} %pad_add_fusion.scalar_ref, bf16[256,2048]{1,0:T(8,128)(2,1)} %copy-done.3, bf16[256,2048]{1,0:T(8,128)(2,1)} %collective-permute-done.41.refs_1_, bf16[256,2048]{1,0:T(8,128)(2,1)} %add_convert_fusion.14.refs_2_, bf16[256,2048]{1,0:T(8,128)(2,1)} %collective-permute-done.44.refs_3_, ...), custom_call_target="tpu_custom_call" | custom-call | flops 20971520 | bytes 20971520 | tf_op jit(solution)/shard_map/pallas_call | solution.py:784
  (368 shorter events, 212.7 us)
Async XLA Ops:
  101.3 58.5 %collective-permute-start.25 = (bf16[256,2304]{1,0:T(8,128)(2,1)}, bf16[256,2304]{1,0:T(8,128)(2,1)}, u32[]{:S(2)}, u32[]{:S(2)}) collective-permute-start(bf16[256,2304]{1,0:T(8,128)(2,1)} %pad_maximum_fusion.refs_0_), channel_id=1, source_target_pairs={{0,8},{8,16},{16,24},{24,28},{28,20},{20,12},{12,4},{4,0},{1,9},{9... | collective-permute-start | bytes 3538952 | tf_op jit(solution)/shard_map/ppermute | solution.py:419
  102.2 58.0 %collective-permute-start.22 = (bf16[256,2304]{1,0:T(8,128)(2,1)}, bf16[256,2304]{1,0:T(8,128)(2,1)}, u32[]{:S(2)}, u32[]{:S(2)}) collective-permute-start(bf16[256,2304]{1,0:T(8,128)(2,1)} %pad_maximum_fusion.refs_0_), channel_id=1, source_target_pairs={{0,4},{8,0},{16,8},{24,16},{28,24},{20,28},{12,20},{4,12},{1,5},{9... | collective-permute-start | bytes 3538952 | tf_op jit(solution)/shard_map/ppermute | solution.py:420
  159.7 46.6 %collective-permute-start.26 = (bf16[256,2304]{1,0:T(8,128)(2,1)}, bf16[256,2304]{1,0:T(8,128)(2,1)S(1)}, u32[]{:S(2)}, u32[]{:S(2)}) collective-permute-start(bf16[256,2304]{1,0:T(8,128)(2,1)} %collective-permute-done.25.refs_8_), channel_id=1, source_target_pairs={{0,8},{8,16},{16,24},{24,28},{28,20},{20,12},{12,4},{4,0},{1,9},{9... | collective-permute-start | bytes 3538952 | tf_op jit(solution)/shard_map/ppermute | solution.py:419
  160.2 69.2 %collective-permute-start.23 = (bf16[256,2304]{1,0:T(8,128)(2,1)}, bf16[256,2304]{1,0:T(8,128)(2,1)S(1)}, u32[]{:S(2)}, u32[]{:S(2)}) collective-permute-start(bf16[256,2304]{1,0:T(8,128)(2,1)} %collective-permute-done.22.refs_1_), channel_id=1, source_target_pairs={{0,4},{8,0},{16,8},{24,16},{28,24},{20,28},{12,20},{4,12},{1,5},{9... | collective-permute-start | bytes 3538952 | tf_op jit(solution)/shard_map/ppermute | solution.py:420
  181.1 47.9 %collective-permute-start.17 = (bf16[256,2048]{1,0:T(8,128)(2,1)S(1)}, bf16[256,2048]{1,0:T(8,128)(2,1)S(1)}, u32[]{:S(2)}, u32[]{:S(2)}) collective-permute-start(bf16[256,2048]{1,0:T(8,128)(2,1)S(1)} %add_convert_fusion.25), channel_id=1, source_target_pairs={{0,2},{1,3},{2,0},{3,1},{4,6},{5,7},{6,4},{7,5},{8,10},{9,11},{10,... | collective-permute-start | bytes 3145736 | tf_op jit(solution)/shard_map/ppermute | solution.py:943
  182.6 44.8 %collective-permute-start.12 = (bf16[256,1920]{1,0:T(8,128)(2,1)S(1)}, bf16[256,1920]{1,0:T(8,128)(2,1)S(1)}, u32[]{:S(2)}, u32[]{:S(2)}) collective-permute-start(bf16[256,1920]{1,0:T(8,128)(2,1)S(1)} %collective-permute-done.11.refs_8_), channel_id=1, source_target_pairs={{0,8},{8,16},{16,24},{24,28},{28,20},{20,12},{12,4},{4,0},{1,9},{9... | collective-permute-start | bytes 2949128 | tf_op jit(solution)/shard_map/ppermute | solution.py:419
  183.5 48.5 %collective-permute-start.20 = (bf16[256,2048]{1,0:T(8,128)(2,1)S(1)}, bf16[256,2048]{1,0:T(8,128)(2,1)S(1)}, u32[]{:S(2)}, u32[]{:S(2)}) collective-permute-start(bf16[256,2048]{1,0:T(8,128)(2,1)S(1)} %add_convert_fusion.23), channel_id=1, source_target_pairs={{0,2},{1,3},{2,0},{3,1},{4,6},{5,7},{6,4},{7,5},{8,10},{9,11},{10,... | collective-permute-start | bytes 3145736 | tf_op jit(solution)/shard_map/ppermute | solution.py:943
  206.3 46.3 %collective-permute-start.27 = (bf16[256,2304]{1,0:T(8,128)(2,1)S(1)}, bf16[256,2304]{1,0:T(8,128)(2,1)S(1)}, u32[]{:S(2)}, u32[]{:S(2)}) collective-permute-start(bf16[256,2304]{1,0:T(8,128)(2,1)S(1)} %collective-permute-done.26.refs_7_), channel_id=1, source_target_pairs={{0,8},{8,16},{16,24},{24,28},{28,20},{20,12},{12,4},{4,0},{1,9},{9... | collective-permute-start | bytes 3538952 | tf_op jit(solution)/shard_map/ppermute | solution.py:419
  229.0 50.2 %collective-permute-start.13 = (bf16[256,1920]{1,0:T(8,128)(2,1)S(1)}, bf16[256,1920]{1,0:T(8,128)(2,1)S(1)}, u32[]{:S(2)}, u32[]{:S(2)}) collective-permute-start(bf16[256,1920]{1,0:T(8,128)(2,1)S(1)} %collective-permute-done.12.refs_7_), channel_id=1, source_target_pairs={{0,8},{8,16},{16,24},{24,28},{28,20},{20,12},{12,4},{4,0},{1,9},{9... | collective-permute-start | bytes 2949128 | tf_op jit(solution)/shard_map/ppermute | solution.py:419
  229.4 47.9 %collective-permute-start.24 = (bf16[256,2304]{1,0:T(8,128)(2,1)S(1)}, bf16[256,2304]{1,0:T(8,128)(2,1)S(1)}, u32[]{:S(2)}, u32[]{:S(2)}) collective-permute-start(bf16[256,2304]{1,0:T(8,128)(2,1)S(1)} %collective-permute-done.23.refs_2_), channel_id=1, source_target_pairs={{0,4},{8,0},{16,8},{24,16},{28,24},{20,28},{12,20},{4,12},{1,5},{9... | collective-permute-start | bytes 3538952 | tf_op jit(solution)/shard_map/ppermute | solution.py:420
  232.0 68.1 %collective-permute-start.18 = (bf16[256,2048]{1,0:T(8,128)(2,1)S(1)}, bf16[256,2048]{1,0:T(8,128)(2,1)S(1)}, u32[]{:S(2)}, u32[]{:S(2)}) collective-permute-start(bf16[256,2048]{1,0:T(8,128)(2,1)S(1)} %add_convert_fusion.24.refs_0_), channel_id=1, source_target_pairs={{0,1},{1,0},{2,3},{3,2},{4,5},{5,4},{6,7},{7,6},{8,9},{9,8},{10,11... | collective-permute-start | bytes 3145736 | tf_op jit(solution)/shard_map/ppermute | solution.py:944
  252.0 49.3 %collective-permute-start.21 = (bf16[256,2048]{1,0:T(8,128)(2,1)S(1)}, bf16[256,2048]{1,0:T(8,128)(2,1)S(1)}, u32[]{:S(2)}, u32[]{:S(2)}) collective-permute-start(bf16[256,2048]{1,0:T(8,128)(2,1)S(1)} %add_convert_fusion.22.refs_2_), channel_id=1, source_target_pairs={{0,1},{1,0},{2,3},{3,2},{4,5},{5,4},{6,7},{7,6},{8,9},{9,8},{10,11... | collective-permute-start | bytes 3145736 | tf_op jit(solution)/shard_map/ppermute | solution.py:944
  252.7 45.7 %collective-permute-start.10 = (bf16[256,1920]{1,0:T(8,128)(2,1)S(1)}, bf16[256,1920]{1,0:T(8,128)(2,1)S(1)}, u32[]{:S(2)}, u32[]{:S(2)}) collective-permute-start(bf16[256,1920]{1,0:T(8,128)(2,1)S(1)} %collective-permute-done.9.refs_2_), channel_id=1, source_target_pairs={{0,4},{8,0},{16,8},{24,16},{28,24},{20,28},{12,20},{4,12},{1,5},{9... | collective-permute-start | bytes 2949128 | tf_op jit(solution)/shard_map/ppermute | solution.py:420
  298.4 44.1 %collective-permute-start.14 = (bf16[128,1920]{1,0:T(8,128)(2,1)}, bf16[128,1920]{1,0:T(8,128)(2,1)}, u32[]{:S(2)}, u32[]{:S(2)}) collective-permute-start(bf16[128,1920]{1,0:T(8,128)(2,1)} %slice.283), channel_id=1, source_target_pairs={{0,8},{8,16},{16,24},{24,28},{28,20},{20,12},{12,4},{4,0},{1,9},{9... | collective-permute-start | bytes 1474568 | tf_op jit(solution)/shard_map/ppermute | solution.py:424
  300.1 42.4 %collective-permute-start.15 = (bf16[128,1920]{1,0:T(8,128)(2,1)}, bf16[128,1920]{1,0:T(8,128)(2,1)}, u32[]{:S(2)}, u32[]{:S(2)}) collective-permute-start(bf16[128,1920]{1,0:T(8,128)(2,1)} %slice.284), channel_id=1, source_target_pairs={{0,4},{8,0},{16,8},{24,16},{28,24},{20,28},{12,20},{4,12},{1,5},{9... | collective-permute-start | bytes 1474568 | tf_op jit(solution)/shard_map/ppermute | solution.py:425
  417.0 73.4 %collective-permute-start.30 = (bf16[512,2048]{1,0:T(8,128)(2,1)S(1)}, bf16[512,2048]{1,0:T(8,128)(2,1)S(1)}, u32[]{:S(2)}, u32[]{:S(2)}) collective-permute-start(bf16[512,2048]{1,0:T(8,128)(2,1)S(1)} %copy-done.53), channel_id=1, source_target_pairs={{0,1},{1,0},{2,3},{3,2},{4,5},{5,4},{6,7},{7,6},{8,9},{9,8},{10,11... | collective-permute-start | bytes 6291464 | tf_op jit(solution)/shard_map/ppermute | solution.py:942
  428.1 42.5 %collective-permute-start.54 = (bf16[256,2304]{1,0:T(8,128)(2,1)S(1)}, bf16[256,2304]{1,0:T(8,128)(2,1)S(1)}, u32[]{:S(2)}, u32[]{:S(2)}) collective-permute-start(bf16[256,2304]{1,0:T(8,128)(2,1)S(1)} %add_convert_fusion.7), channel_id=1, source_target_pairs={{0,8},{8,16},{16,24},{24,28},{28,20},{20,12},{12,4},{4,0},{1,9},{9... | collective-permute-start | bytes 3538952 | tf_op jit(solution)/shard_map/ppermute | solution.py:446
  429.0 42.5 %collective-permute-start.58 = (bf16[256,2304]{1,0:T(8,128)(2,1)S(1)}, bf16[256,2304]{1,0:T(8,128)(2,1)S(1)}, u32[]{:S(2)}, u32[]{:S(2)}) collective-permute-start(bf16[256,2304]{1,0:T(8,128)(2,1)S(1)} %add_convert_fusion.4), channel_id=1, source_target_pairs={{0,4},{8,0},{16,8},{24,16},{28,24},{20,28},{12,20},{4,12},{1,5},{9... | collective-permute-start | bytes 3538952 | tf_op jit(solution)/shard_map/ppermute | solution.py:447
  474.0 42.0 %collective-permute-start.55 = (bf16[256,2304]{1,0:T(8,128)(2,1)S(1)}, bf16[256,2304]{1,0:T(8,128)(2,1)S(1)}, u32[]{:S(2)}, u32[]{:S(2)}) collective-permute-start(bf16[256,2304]{1,0:T(8,128)(2,1)S(1)} %add_convert_fusion.6), channel_id=1, source_target_pairs={{0,8},{8,16},{16,24},{24,28},{28,20},{20,12},{12,4},{4,0},{1,9},{9... | collective-permute-start | bytes 3538952 | tf_op jit(solution)/shard_map/ppermute | solution.py:446
  496.4 153.7 %collective-permute-start.31 = (bf16[512,2048]{1,0:T(8,128)(2,1)}, bf16[512,2048]{1,0:T(8,128)(2,1)}, u32[]{:S(2)}, u32[]{:S(2)}) collective-permute-start(bf16[512,2048]{1,0:T(8,128)(2,1)} %add_convert_fusion.1), channel_id=1, source_target_pairs={{0,2},{1,3},{2,0},{3,1},{4,6},{5,7},{6,4},{7,5},{8,10},{9,11},{10,... | collective-permute-start | bytes 6291464 | tf_op jit(solution)/shard_map/ppermute | solution.py:943
  606.3 38.5 %collective-permute-start.45 = (bf16[128,2176]{1,0:T(8,128)(2,1)}, bf16[128,2176]{1,0:T(8,128)(2,1)}, u32[]{:S(2)}, u32[]{:S(2)}) collective-permute-start(bf16[128,2176]{1,0:T(8,128)(2,1)} %get-tuple-element.186), channel_id=1, source_target_pairs={{0,8},{8,16},{16,24},{24,28},{28,20},{20,12},{12,4},{4,0},{1,9},{9... | collective-permute-start | bytes 1671176 | tf_op jit(solution)/shard_map/ppermute | solution.py:438
  644.8 80.0 %collective-permute-start.64 = (bf16[256,1920]{1,0:T(8,128)(2,1)S(1)}, bf16[256,1920]{1,0:T(8,128)(2,1)S(1)}, u32[]{:S(2)}, u32[]{:S(2)}) collective-permute-start(bf16[256,1920]{1,0:T(8,128)(2,1)S(1)} %copy-done.35), channel_id=1, source_target_pairs={{0,8},{8,16},{16,24},{24,28},{28,20},{20,12},{12,4},{4,0},{1,9},{9... | collective-permute-start | bytes 2949128 | tf_op jit(solution)/shard_map/ppermute | solution.py:446
  646.2 101.5 %collective-permute-start.68 = (bf16[256,1920]{1,0:T(8,128)(2,1)S(1)}, bf16[256,1920]{1,0:T(8,128)(2,1)S(1)}, u32[]{:S(2)}, u32[]{:S(2)}) collective-permute-start(bf16[256,1920]{1,0:T(8,128)(2,1)S(1)} %copy-done.34), channel_id=1, source_target_pairs={{0,4},{8,0},{16,8},{24,16},{28,24},{20,28},{12,20},{4,12},{1,5},{9... | collective-permute-start | bytes 2949128 | tf_op jit(solution)/shard_map/ppermute | solution.py:447
  648.5 75.3 %collective-permute-start.73 = (f32[64]{0:T(128)S(1)}, f32[64]{0:T(128)S(1)}, u32[]{:S(2)}, u32[]{:S(2)}) collective-permute-start(f32[64]{0:T(128)S(1)} %add.205), channel_id=1, source_target_pairs={{0,16},{4,20},{8,24},{12,28},{16,0},{20,4},{24,8},{28,12},{1,17},{... | collective-permute-start | bytes 776 | tf_op jit(solution)/shard_map/ppermute | solution.py:455
  649.4 44.9 %collective-permute-start.50 = (bf16[256,2176]{1,0:T(8,128)(2,1)S(1)}, bf16[256,2176]{1,0:T(8,128)(2,1)S(1)}, u32[]{:S(2)}, u32[]{:S(2)}) collective-permute-start(bf16[256,2176]{1,0:T(8,128)(2,1)S(1)} %add_convert_fusion.10), channel_id=1, source_target_pairs={{0,4},{8,0},{16,8},{24,16},{28,24},{20,28},{12,20},{4,12},{1,5},{9... | collective-permute-start | bytes 3342344 | tf_op jit(solution)/shard_map/ppermute | solution.py:447
  650.1 46.1 %collective-permute-start.46 = (bf16[256,2176]{1,0:T(8,128)(2,1)S(1)}, bf16[256,2176]{1,0:T(8,128)(2,1)S(1)}, u32[]{:S(2)}, u32[]{:S(2)}) collective-permute-start(bf16[256,2176]{1,0:T(8,128)(2,1)S(1)} %add_convert_fusion.13), channel_id=1, source_target_pairs={{0,8},{8,16},{16,24},{24,28},{28,20},{20,12},{12,4},{4,0},{1,9},{9... | collective-permute-start | bytes 3342344 | tf_op jit(solution)/shard_map/ppermute | solution.py:446
  723.8 48.0 %collective-permute-start.56 = (bf16[256,2304]{1,0:T(8,128)(2,1)S(1)}, bf16[256,2304]{1,0:T(8,128)(2,1)S(1)}, u32[]{:S(2)}, u32[]{:S(2)}) collective-permute-start(bf16[256,2304]{1,0:T(8,128)(2,1)S(1)} %copy-done.17), channel_id=1, source_target_pairs={{0,8},{8,16},{16,24},{24,28},{28,20},{20,12},{12,4},{4,0},{1,9},{9... | collective-permute-start | bytes 3538952 | tf_op jit(solution)/shard_map/ppermute | solution.py:446
  724.8 46.9 %collective-permute-start.60 = (bf16[256,2304]{1,0:T(8,128)(2,1)S(1)}, bf16[256,2304]{1,0:T(8,128)(2,1)S(1)}, u32[]{:S(2)}, u32[]{:S(2)}) collective-permute-start(bf16[256,2304]{1,0:T(8,128)(2,1)S(1)} %copy-done.18), channel_id=1, source_target_pairs={{0,4},{8,0},{16,8},{24,16},{28,24},{20,28},{12,20},{4,12},{1,5},{9... | collective-permute-start | bytes 3538952 | tf_op jit(solution)/shard_map/ppermute | solution.py:447
  746.4 52.6 %collective-permute-start.32 = (bf16[512,2048]{1,0:T(8,128)(2,1)}, bf16[512,2048]{1,0:T(8,128)(2,1)}, u32[]{:S(2)}, u32[]{:S(2)}) collective-permute-start(bf16[512,2048]{1,0:T(8,128)(2,1)} %add_convert_fusion.refs_0_), channel_id=1, source_target_pairs={{0,1},{1,0},{2,3},{3,2},{4,5},{5,4},{6,7},{7,6},{8,9},{9,8},{10,11... | collective-permute-start | bytes 6291464 | tf_op jit(solution)/shard_map/ppermute | solution.py:944
  749.8 44.0 %collective-permute-start.48 = (bf16[256,2176]{1,0:T(8,128)(2,1)}, bf16[256,2176]{1,0:T(8,128)(2,1)}, u32[]{:S(2)}, u32[]{:S(2)}) collective-permute-start(bf16[256,2176]{1,0:T(8,128)(2,1)} %add_convert_fusion.11), channel_id=1, source_target_pairs={{0,8},{8,16},{16,24},{24,28},{28,20},{20,12},{12,4},{4,0},{1,9},{9... | collective-permute-start | bytes 3342344 | tf_op jit(solution)/shard_map/ppermute | solution.py:446
  771.7 37.5 %collective-permute-start.41 = (bf16[256,2048]{1,0:T(8,128)(2,1)S(1)}, bf16[256,2048]{1,0:T(8,128)(2,1)}, u32[]{:S(2)}, u32[]{:S(2)}) collective-permute-start(bf16[256,2048]{1,0:T(8,128)(2,1)S(1)} %add_convert_fusion.16.refs_0_), channel_id=1, source_target_pairs={{0,1},{1,0},{2,3},{3,2},{4,5},{5,4},{6,7},{7,6},{8,9},{9,8},{10,11... | collective-permute-start | bytes 3145736 | tf_op jit(solution)/shard_map/ppermute | solution.py:944
  771.8 37.5 %collective-permute-start.44 = (bf16[256,2048]{1,0:T(8,128)(2,1)}, bf16[256,2048]{1,0:T(8,128)(2,1)}, u32[]{:S(2)}, u32[]{:S(2)}) collective-permute-start(bf16[256,2048]{1,0:T(8,128)(2,1)} %add_convert_fusion.14.refs_2_), channel_id=1, source_target_pairs={{0,1},{1,0},{2,3},{3,2},{4,5},{5,4},{6,7},{7,6},{8,9},{9,8},{10,11... | collective-permute-start | bytes 3145736 | tf_op jit(solution)/shard_map/ppermute | solution.py:944
  (113 other events, 2270.6 us)
where the time goes:
time: 834 us; the launch traced here: 824 us
  waiting for transfers between devices  386 us (46%)
  Pallas kernels  254 us (30%)
  starting transfers between devices  71.1 us (9%)
  matrix products  48.1 us (6%)
  other arithmetic  36.6 us (4%)
  local copies, waits for them, and re-layouts  25.7 us (3%)
    pallas_call x7, Pallas kernels, vmem_call(): pl.pallas_call(body, out_shape=out_shape, in_specs=spaces, out_specs=[pl....  116 us
    ppermute x9, waiting for transfers between devices, ring_scatter(): up_sum = to_wide(lax.ppermute(to_low(up_piece), DP, up))  106 us
    ppermute x9, waiting for transfers between devices, ring_gather(): from_high = lax.ppermute(from_high, DP, down)  106 us
    ppermute x9, waiting for transfers between devices, ring_gather(): from_low = lax.ppermute(from_low, DP, up)  61.5 us
    pallas_call x1, Pallas kernels, mixer_backward(): pl.pallas_call(backward_kernel, out_shape=(jax.ShapeDtypeStruct((rows, 3...  52.6 us
    dot_general x12, matrix products, dot_tn(): lax.dot_general(left, right, (((0,), (0,)), ((), ())), preferred_element_...  48.1 us
    pallas_call x4, Pallas kernels, row_call(): pl.pallas_call(body, out_shape=[jax.ShapeDtypeStruct((rows, depth), kind)...  44.5 us
    ppermute x9, waiting for transfers between devices, ring_scatter(): down_sum = to_wide(lax.ppermute(to_low(down_piece), DP, down))  40.6 us
  transfers between devices with their start and end apart: 74, of which 31 were waited for; matrix products, arithmetic and copies ran while one was open for 9% of the time, Pallas kernels for 27%

commit v1 on v0

--- a/solution.py
+++ b/solution.py
@@ -10,6 +10,7 @@
 DP, HEAD = "dp", "head"
 epsilon = 1e-06
 PAIR = 2
+LAGS = 16
 
 
 def split_low(values):
@@ -28,14 +29,6 @@
 def lane_place():
     lanes = lax.broadcasted_iota(jnp.int32, (BLOCK, TILE), 1)
     return lanes, jnp.bitwise_and(lanes, BLOCK - 1)
-
-
-def prefix_sum(values, place):
-    step = 1
-    while step < BLOCK:
-        values = values + jnp.where(place >= step, pltpu.roll(values, step, 1), 0.0)
-        step *= 2
-    return values
 
 
 def suffix_sum(values, place):
@@ -46,27 +39,46 @@
     return values
 
 
-def to_band(square):
-    rows = lax.broadcasted_iota(jnp.int32, (TILE, TILE), 0)
-    step = 1
-    while step < TILE:
-        square = jnp.where(jnp.bitwise_and(rows, step) != 0, pltpu.roll(square, TILE - step, 1), square)
-        step *= 2
-    return square.T
-
-
-def from_band(band):
-    return pltpu.roll(band.T, 0, 1, stride=1, stride_axis=0)
-
-
-def lag_row(lag):
-    return slice((TILE - lag) % TILE, (TILE - lag) % TILE + 1)
+def square_iotas():
+    return (
+        lax.broadcasted_iota(jnp.int32, (TILE, TILE), 0),
+        lax.broadcasted_iota(jnp.int32, (TILE, TILE), 1),
+    )
+
+
+def level_masks():
+    rows, columns = square_iotas()
+    masks = []
+    for half in (LAGS, 2 * LAGS):
+        same = jnp.bitwise_and(rows, -2 * half) == jnp.bitwise_and(columns, -2 * half)
+        apart = (jnp.bitwise_and(rows, half) == 0) & (jnp.bitwise_and(columns, half) != 0)
+        masks.append(same & apart)
+    return masks
+
+
+def level_parts(square, masks):
+    return jnp.concatenate([jnp.where(mask, square, 0.0) for mask in masks], axis=1)
+
+
+def take_band(square, band_ref, slot):
+    rows, columns = square_iotas()
+    apart = columns - rows
+    for lag in range(LAGS):
+        band_ref[slot, lag : lag + 1, :] = jnp.sum(jnp.where(apart == lag, square, 0.0), axis=0, keepdims=True)
+
+
+def put_band(square, band_ref, slot):
+    rows, columns = square_iotas()
+    apart = columns - rows
+    for lag in range(LAGS):
+        square = jnp.where(apart == lag, band_ref[slot, lag : lag + 1, :], square)
+    return square
 
 
 def fill_products(product_ref, slot, writes, inside):
     product_ref[slot, 0] = writes
     power, powers, reach = inside, [], 1
-    while reach < BLOCK:
+    while reach < LAGS:
         powers.append(power)
         for lag in range(reach):
             product_ref[slot, reach + lag] = power * pltpu.roll(product_ref[slot, lag], reach, 1)
@@ -76,26 +88,70 @@
 
 
 def lag_total(product_ref, slot, band_ref, start):
-    sums = [start, None, None, None]
-    for lag in range(BLOCK):
-        term = product_ref[slot, lag] * band_ref[slot, lag_row(lag), :]
-        held = sums[lag % 4]
-        sums[lag % 4] = term if held is None else held + term
-    return (sums[0] + sums[1]) + (sums[2] + sums[3])
+    sums = [start, None]
+    for lag in range(LAGS):
+        term = product_ref[slot, lag] * band_ref[slot, lag : lag + 1, :]
+        held = sums[lag % 2]
+        sums[lag % 2] = term if held is None else held + term
+    return sums[0] + sums[1]
 
 
 def lag_mix(product_ref, slot, band_ref, weights):
-    for lag in range(BLOCK):
-        band_ref[slot, lag_row(lag), :] = jnp.sum(weights * product_ref[slot, lag], axis=0, keepdims=True)
-
-
-def lag_back(powers, term_of, low, count, stride=1):
+    for lag in range(LAGS):
+        band_ref[slot, lag : lag + 1, :] = jnp.sum(weights * product_ref[slot, lag], axis=0, keepdims=True)
+
+
+def lag_back(powers, term_of, low, count):
     if count == 1:
         return term_of(low)
     half = count // 2
-    left = lag_back(powers, term_of, low, half, stride)
-    right = lag_back(powers, term_of, low + half, half, stride)
-    return left + pltpu.roll(powers[half.bit_length() - 1] * right, TILE - half * stride, 1)
+    left = lag_back(powers, term_of, low, half)
+    right = lag_back(powers, term_of, low + half, half)
+    return left + pltpu.roll(powers[half.bit_length() - 1] * right, TILE - half, 1)
+
+
+def two_rows(values):
+    high, low = split_low(values)
+    return jnp.concatenate([high, low], axis=0)
+
+
+def level_total(near, parts, faded):
+    high, low = split_low(parts)
+    lefts = jnp.concatenate([two_rows(left) for left in near], axis=0)
+    tall = dot_nn(lefts, high)
+    short = dot_nn(jnp.concatenate([split_low(left)[0] for left in near], axis=0), low)
+    total = 0.0
+    for index, right in enumerate(faded):
+        span = slice(index * TILE, (index + 1) * TILE)
+        rows = tall[2 * index * BLOCK : 2 * (index + 1) * BLOCK, span]
+        total = total + right * (rows[:BLOCK] + rows[BLOCK:] + short[index * BLOCK : (index + 1) * BLOCK, span])
+    return total
+
+
+def level_mix(square, near, faded, masks):
+    for left, right, mask in zip(near, faded, masks):
+        square = jnp.where(
+            mask,
+            lax.dot_general(
+                left.astype(jnp.bfloat16), right.astype(jnp.bfloat16), (((0,), (0,)), ((), ())),
+                preferred_element_type=jnp.float32,
+            ),
+            square,
+        )
+    return square
+
+
+def level_back(lefts, parts, rest):
+    rows = jnp.concatenate([two_rows(left) for left in lefts], axis=0)
+    high, low = split_low(jnp.concatenate(parts, axis=0))
+    tall = dot_nt(rows, high)
+    short = dot_nt(jnp.concatenate([split_low(left)[0] for left in lefts], axis=0), low)
+    total = 0.0
+    for index, factor in enumerate(rest):
+        span = slice(index * TILE, (index + 1) * TILE)
+        one = tall[2 * index * BLOCK : 2 * (index + 1) * BLOCK, span]
+        total = total + factor * (one[:BLOCK] + one[BLOCK:] + short[index * BLOCK : (index + 1) * BLOCK, span])
+    return total
 
 
 def gate_terms(logits, valid, place):
@@ -104,10 +160,22 @@
     decay = jnp.exp(logdecay)
     series = -logdecay * (1.0 + logdecay * (0.5 + logdecay * (1.0 / 6.0 + logdecay * (1.0 / 24.0))))
     writes = valid * jnp.where(logdecay > -0.03, series, 1.0 - decay)
-    inside = jnp.where(place == 0, 0.0, decay)
-    before = prefix_sum(logdecay, place)
-    after = suffix_sum(logdecay, place) - logdecay
-    return decay, writes, inside, before, after
+    low = jnp.bitwise_and(place, LAGS - 1)
+    inside = jnp.where(low == 0, 0.0, decay)
+    before, rest, step = logdecay, logdecay, 1
+    while step < LAGS:
+        before = before + jnp.where(low >= step, pltpu.roll(before, step, 1), 0.0)
+        rest = rest + jnp.where(low < LAGS - step, pltpu.roll(rest, TILE - step, 1), 0.0)
+        step *= 2
+    rest = rest - logdecay
+    scans = []
+    while step < BLOCK:
+        scans.append((jnp.exp(before), jnp.exp(rest)))
+        total, upper = before + rest, jnp.bitwise_and(place, step) != 0
+        before = before + jnp.where(upper, pltpu.roll(total, step, 1), 0.0)
+        rest = rest + jnp.where(upper, 0.0, pltpu.roll(total, TILE - step, 1))
+        step *= 2
+    return decay, writes, inside, before, rest, scans
 
 
 def stacked(values, lanes):
@@ -139,7 +207,10 @@
 
     def gather_writes(tile, none):
         logits = logit_ref[tile] + bias
-        _, writes, inside, before, after = gate_terms(logits, valid_of(tile), place)
+        _, writes, inside, before, after, scans = gate_terms(logits, valid_of(tile), place)
+        for index, (faded, rest) in enumerate(scans):
+            gate_ref[tile, 4 + 2 * index] = faded
+            gate_ref[tile, 5 + 2 * index] = rest * writes
         gate_ref[tile, 0] = writes
         gate_ref[tile, 1] = inside
         gate_ref[tile, 2] = jnp.exp(before)
@@ -166,21 +237,32 @@
 
     lax.fori_loop(0, tiles, run_states, 0)
 
-    band_ref[...] = jnp.zeros_like(band_ref)
-    mix_band_ref[...] = jnp.zeros_like(mix_band_ref)
+    masks = level_masks()
 
     def mix_pair(pair, none):
         both = [(slot, PAIR * pair + slot) for slot in range(PAIR)]
-        queries, scores, probs = {}, {}, {}
+        queries, scores, probs, squares = {}, {}, {}, {}
+
+        def faded_of(tile):
+            return [gate_ref[tile, 4], gate_ref[tile, 6]]
+
+        def near_of(tile):
+            return [gate_ref[tile, 5], gate_ref[tile, 7]]
+
+        for slot, tile in both:
+            queries[slot] = qkv_ref[rows_of(tile), :width]
+            squares[slot] = dot_nt(qkv_ref[rows_of(tile), width : 2 * width], queries[slot]) * scale
         for slot, tile in both:
             fill_products(product_ref, slot, gate_ref[tile, 0], gate_ref[tile, 1])
-        for slot, tile in both:
-            queries[slot] = qkv_ref[rows_of(tile), :width]
-            band_ref[slot] = to_band(dot_nt(queries[slot], qkv_ref[rows_of(tile), width : 2 * width]) * scale)
         for slot, tile in both:
             high, low = split_low(state_ref[tile, :, :width])
             carried = own_block(dot_nt(high, queries[slot]) + dot_nt(low, queries[slot]), lanes)
             scores[slot] = gate_ref[tile, 2] * carried * scale
+        for slot, tile in both:
+            take_band(squares[slot], band_ref, slot)
+            scores[slot] = scores[slot] + level_total(
+                near_of(tile), level_parts(squares[slot], masks), faded_of(tile)
+            )
         for slot, tile in both:
             scores[slot] = lag_total(product_ref, slot, band_ref, scores[slot])
         for slot, tile in both:
@@ -192,10 +274,12 @@
         for slot, tile in both:
             lag_mix(product_ref, slot, mix_band_ref, probs[slot])
         for slot, tile in both:
-            mixing = from_band(mix_band_ref[slot]).astype(jnp.bfloat16)
+            mixing = put_band(jnp.zeros((TILE, TILE), jnp.float32), mix_band_ref, slot)
+            mixing = level_mix(mixing, near_of(tile), [probs[slot] * one for one in faded_of(tile)], masks)
+            mixing = mixing.astype(jnp.bfloat16)
             mix_ref[tile] = mixing
             reach = stacked(probs[slot] * gate_ref[tile, 2], lanes).T.astype(jnp.bfloat16)
-            result = dot_nn(mixing, qkv_ref[rows_of(tile), 2 * width :]) + dot_nn(
+            result = dot_nn(mixing.T, qkv_ref[rows_of(tile), 2 * width :]) + dot_nn(
                 reach, state_ref[tile, :, width:].astype(jnp.bfloat16)
             )
             rows = lax.broadcasted_iota(jnp.int32, (TILE, 1), 0) + tile * TILE
@@ -226,13 +310,22 @@
         rows = lax.broadcasted_iota(jnp.int32, (TILE, 1), 0) + tile * TILE
         return jnp.where(rows < length_ref[0], back_ref[rows_of(tile), :], jnp.zeros((), back_ref.dtype))
 
-    band_ref[...] = jnp.zeros_like(band_ref)
+    masks = level_masks()
 
     def slopes(pair, none):
         both = [(slot, PAIR * pair + slot) for slot in range(PAIR)]
-        fades, powers, queries, keys, backs, gains, d_scores = {}, {}, {}, {}, {}, {}, {}
-        for slot, tile in both:
-            decay, writes, inside, before, after = gate_terms(logit_ref[tile] + bias, valid_of(tile), place)
+        fades, powers, queries, keys, backs, gains, d_scores, faded, rests, near = ({} for _ in range(10))
+        key_squares, value_squares = {}, {}
+        for slot, tile in both:
+            queries[slot] = qkv_ref[rows_of(tile), :width]
+            keys[slot] = qkv_ref[rows_of(tile), width : 2 * width]
+            backs[slot] = back_of(tile)
+            key_squares[slot] = dot_nt(keys[slot], queries[slot]) * scale
+            value_squares[slot] = dot_nt(qkv_ref[rows_of(tile), 2 * width :], backs[slot])
+        for slot, tile in both:
+            decay, writes, inside, before, after, scans = gate_terms(logit_ref[tile] + bias, valid_of(tile), place)
+            faded[slot], rests[slot] = [one for one, _ in scans], [one for _, one in scans]
+            near[slot] = [one * writes for one in rests[slot]]
             fades[slot] = jnp.exp(before)
             gain_ref[tile, 2] = decay
             gain_ref[tile, 3] = writes
@@ -240,16 +333,16 @@
             gain_ref[tile, 5] = jnp.exp(before + after)
             powers[slot] = fill_products(product_ref, slot, writes, inside)
         for slot, tile in both:
-            queries[slot] = qkv_ref[rows_of(tile), :width]
-            keys[slot] = qkv_ref[rows_of(tile), width : 2 * width]
-            backs[slot] = back_of(tile)
-            key_band_ref[slot] = to_band(dot_nt(queries[slot], keys[slot]) * scale)
-            value_band_ref[slot] = to_band(dot_nt(backs[slot], qkv_ref[rows_of(tile), 2 * width :]))
-        for slot, tile in both:
             high, low = split_low(state_ref[tile, :, width:])
             carried = own_block(dot_nt(high, backs[slot]) + dot_nt(low, backs[slot]), lanes)
             gains[slot] = fades[slot] * carried
         for slot, tile in both:
+            take_band(key_squares[slot], key_band_ref, slot)
+            take_band(value_squares[slot], value_band_ref, slot)
+            gains[slot] = gains[slot] + level_total(
+                near[slot], level_parts(value_squares[slot], masks), faded[slot]
+            )
+        for slot, tile in both:
             gains[slot] = lag_total(product_ref, slot, value_band_ref, gains[slot])
         for slot, tile in both:
             probs = prob_ref[tile]
@@ -261,27 +354,31 @@
             probs = prob_ref[tile]
 
             def term_of(lag, slot=slot, probs=probs):
-                row = lag_row(lag)
+                row = slice(lag, lag + 1)
                 return d_scores[slot] * key_band_ref[slot, row, :] + probs * value_band_ref[slot, row, :]
 
-            group = 8
-            for low in range(0, BLOCK, group):
-                product_ref[slot, low // group] = lag_back(powers[slot], term_of, low, group)
-            gain_ref[tile, 0] = lag_back(
-                powers[slot][group.bit_length() - 1 :], lambda index, slot=slot: product_ref[slot, index], 0, BLOCK // group, group
-            )
-        for slot, tile in both:
-            mixing = (from_band(band_ref[slot]) * scale).astype(jnp.bfloat16)
+            lefts = [jnp.concatenate([d_scores[slot] * one, probs * one], axis=1) for one in faded[slot]]
+            parts = [
+                jnp.concatenate(
+                    [jnp.where(mask, key_squares[slot], 0.0), jnp.where(mask, value_squares[slot], 0.0)], axis=1
+                )
+                for mask in masks
+            ]
+            gain_ref[tile, 0] = lag_back(powers[slot], term_of, 0, LAGS) + level_back(lefts, parts, rests[slot])
+        for slot, tile in both:
+            mixing = put_band(jnp.zeros((TILE, TILE), jnp.float32), band_ref, slot)
+            mixing = level_mix(mixing, near[slot], [d_scores[slot] * one for one in faded[slot]], masks)
+            mixing = (mixing * scale).astype(jnp.bfloat16)
             reach = stacked(d_scores[slot] * fades[slot] * scale, lanes)
             held = stacked(prob_ref[tile] * fades[slot], lanes).astype(jnp.bfloat16)
             d_qkv_ref[rows_of(tile), :width] = (
-                dot_nn(mixing, keys[slot])
+                dot_nn(mixing.T, keys[slot])
                 + dot_nn(reach.T.astype(jnp.bfloat16), state_ref[tile, :, :width].astype(jnp.bfloat16))
             ).astype(jnp.bfloat16)
             adjoint_ref[tile, :, :width] = dot_nn(reach.astype(jnp.bfloat16), queries[slot])
             adjoint_ref[tile, :, width:] = dot_nn(held, backs[slot])
-            d_qkv_ref[rows_of(tile), width : 2 * width] = dot_nn(mixing.T, queries[slot]).astype(jnp.bfloat16)
-            d_qkv_ref[rows_of(tile), 2 * width : 3 * width] = dot_nn(mix_ref[tile].T, backs[slot]).astype(jnp.bfloat16)
+            d_qkv_ref[rows_of(tile), width : 2 * width] = dot_nn(mixing, queries[slot]).astype(jnp.bfloat16)
+            d_qkv_ref[rows_of(tile), 2 * width : 3 * width] = dot_nn(mix_ref[tile], backs[slot]).astype(jnp.bfloat16)
         return none
 
     lax.fori_loop(0, tiles // PAIR, slopes, 0)
@@ -348,12 +445,13 @@
         in_specs=[pl.BlockSpec(memory_space=pltpu.SMEM)] + [pl.BlockSpec(memory_space=pltpu.VMEM)] * 3,
         out_specs=[pl.BlockSpec(memory_space=pltpu.VMEM)] * 5,
         scratch_shapes=[
-            pltpu.VMEM((tiles, 4, BLOCK, TILE), f32),
+            pltpu.VMEM((tiles, 8, BLOCK, TILE), f32),
             pltpu.VMEM((BLOCK, 2 * width), f32),
-            pltpu.VMEM((PAIR, TILE, TILE), f32),
-            pltpu.VMEM((PAIR, TILE, TILE), f32),
-            pltpu.VMEM((PAIR, BLOCK, BLOCK, TILE), f32),
+            pltpu.VMEM((PAIR, LAGS, TILE), f32),
+            pltpu.VMEM((PAIR, LAGS, TILE), f32),
+            pltpu.VMEM((PAIR, LAGS, BLOCK, TILE), f32),
         ],
+        compiler_params=pltpu.CompilerParams(vmem_limit_bytes=22 * MEBI),
         name="mixer_forward",
     )(length, qkv, logits, bias)
 
@@ -373,14 +471,15 @@
         scratch_shapes=[
             pltpu.VMEM((tiles, TILE, 2 * width), f32),
             pltpu.VMEM((tiles, 6, BLOCK, TILE), f32),
-            pltpu.VMEM((PAIR, TILE, TILE), f32),
-            pltpu.VMEM((PAIR, TILE, TILE), f32),
-            pltpu.VMEM((PAIR, TILE, TILE), f32),
+            pltpu.VMEM((PAIR, LAGS, TILE), f32),
+            pltpu.VMEM((PAIR, LAGS, TILE), f32),
+            pltpu.VMEM((PAIR, LAGS, TILE), f32),
             pltpu.VMEM((BLOCK, 2 * width), f32),
             pltpu.VMEM((BLOCK, 2 * width), f32),
             pltpu.VMEM((tiles, TILE, TILE), f32),
-            pltpu.VMEM((PAIR, BLOCK, BLOCK, TILE), f32),
+            pltpu.VMEM((PAIR, LAGS, BLOCK, TILE), f32),
         ],
+        compiler_params=pltpu.CompilerParams(vmem_limit_bytes=32 * MEBI),
         name="mixer_backward",
     )(length, qkv, logits, bias, back, *saved)
 
@@ -486,16 +585,17 @@
             in_specs=[pl.BlockSpec((rows, width), plain if inverse else placed)],
             out_specs=pl.BlockSpec((rows, width), placed if inverse else plain),
         ),
+        compiler_params=pltpu.CompilerParams(vmem_limit_bytes=8 * MEBI),
         cost_estimate=pl.CostEstimate(flops=0, bytes_accessed=2 * matrix.size * matrix.dtype.itemsize, transcendentals=0),
     )(places, matrix)
 
 
 ROWS = 128
 WIDE = 256
-LIMIT = 62 * 1024 * 1024
-
-
-def vmem_call(body, out_shape, operands, scratch=(), scalars=1, anywhere=0, flops=0, moved=0):
+MEBI = 1024 * 1024
+
+
+def vmem_call(body, out_shape, operands, limit, scratch=(), scalars=1, anywhere=0, flops=0, moved=0):
     spaces = (
         [pl.BlockSpec(memory_space=pltpu.SMEM)] * scalars
         + [pl.BlockSpec(memory_space=pltpu.VMEM)] * (len(operands) - scalars - anywhere)
@@ -507,7 +607,7 @@
         in_specs=spaces,
         out_specs=[pl.BlockSpec(memory_space=pltpu.VMEM)] * len(out_shape),
         scratch_shapes=list(scratch),
-        compiler_params=pltpu.CompilerParams(vmem_limit_bytes=LIMIT),
+        compiler_params=pltpu.CompilerParams(vmem_limit_bytes=limit * MEBI),
         cost_estimate=pl.CostEstimate(flops=flops, bytes_accessed=moved, transcendentals=0),
     )(*operands)
 
@@ -581,7 +681,7 @@
     outs = vmem_call(
         body,
         [half] * (2 * parts) + ([jax.ShapeDtypeStruct(weight, jnp.bfloat16)] if keep else []),
-        (parity, left, *flat),
+        (parity, left, *flat), 12 if keep else 22,
         scratch=([] if keep else [pltpu.VMEM(weight, jnp.bfloat16)])
         + [
             pltpu.VMEM((rows, WIDE), jnp.float32),
@@ -634,11 +734,25 @@
             jax.ShapeDtypeStruct((rows, depth), jnp.bfloat16),
             jax.ShapeDtypeStruct((8, depth), jnp.float32),
         ],
-        (rows_low, factor, *flat),
+        (rows_low, factor, *flat), 28,
         scratch=[pltpu.VMEM((depth, columns_all), jnp.bfloat16), pltpu.SemaphoreType.DMA((count * len(blocks),))],
         scalars=0, anywhere=count,
         flops=2 * rows * depth * columns_all, moved=2 * (rows + columns_all) * depth + 2 * rows * columns_all,
     )
+
+
+def act_columns(start, span, hidden, normed_ref, back_ref, weight_ref, hidden_ref, pair_ref):
+    def columns(base):
+        return pl.ds(start + base, span)
+
+    gate_act = dot_nn(normed_ref[...], weight_ref[:, columns(0)])
+    up_act = dot_nn(normed_ref[...], weight_ref[:, columns(hidden)])
+    d_hidden = dot_nn(back_ref[...], weight_ref[:, columns(2 * hidden)])
+    sigma = 1.0 / (1.0 + jnp.exp(-gate_act))
+    gated = gate_act * sigma
+    hidden_ref[:, columns(0)] = (gated * up_act).astype(jnp.bfloat16)
+    pair_ref[:, columns(hidden)] = (d_hidden * gated).astype(jnp.bfloat16)
+    pair_ref[:, columns(0)] = (d_hidden * up_act * (sigma * (1.0 + gate_act * (1.0 - sigma)))).astype(jnp.bfloat16)
 
 
 def feed_call(normed, back, pieces, parity, earlier, parts):
@@ -676,19 +790,7 @@
             held[3].start()
 
         def act(start, span):
-            def columns(base):
-                return pl.ds(start + base, span)
-
-            gate_act = dot_nn(normed_ref[...], weight_ref[:, columns(0)])
-            up_act = dot_nn(normed_ref[...], weight_ref[:, columns(hidden)])
-            d_hidden = dot_nn(back_ref[...], weight_ref[:, columns(2 * hidden)])
-            sigma = 1.0 / (1.0 + jnp.exp(-gate_act))
-            gated = gate_act * sigma
-            hidden_ref[:, columns(0)] = (gated * up_act).astype(jnp.bfloat16)
-            pair_ref[:, columns(hidden)] = (d_hidden * gated).astype(jnp.bfloat16)
-            pair_ref[:, columns(0)] = (
-                d_hidden * up_act * (sigma * (1.0 + gate_act * (1.0 - sigma)))
-            ).astype(jnp.bfloat16)
+            act_columns(start, span, hidden, normed_ref, back_ref, weight_ref, hidden_ref, pair_ref)
 
         finish(held[:2])
         finish(groups[0])
@@ -739,10 +841,109 @@
         scratch.append(pltpu.VMEM((2, rows, depth), low))
     scratch.append(pltpu.SemaphoreType.DMA((6 * count + 2 + given,)))
     return vmem_call(
-        body, outs, (parity, *flat, normed, back, *(earlier or ())),
+        body, outs, (parity, *flat, normed, back, *(earlier or ())), 48,
         scratch=scratch, anywhere=count + 2 + given,
         flops=2 * rows * depth * hidden * 6, moved=2 * (3 * rows * depth + 3 * depth * hidden + 3 * rows * hidden),
     )
+
+
+def act_call(normed, back, pieces):
+    rows, depth = normed.shape
+    flat = flat_pieces(pieces)
+    count = len(flat)
+    hidden = flat[0].shape[1] // 3
+    blocks = [
+        [(part * hidden, WIDE) for part in range(3)],
+        [(part * hidden + WIDE, hidden - WIDE) for part in range(3)],
+    ]
+
+    def body(*refs):
+        sources, (hidden_ref, pair_ref, weight_ref), (normed_ref, back_ref, sems) = refs[:-6], refs[-6:-3], refs[-3:]
+        held = [
+            pltpu.make_async_copy(sources[count], normed_ref, sems.at[6 * count]),
+            pltpu.make_async_copy(sources[count + 1], back_ref, sems.at[6 * count + 1]),
+        ]
+        held[0].start()
+        held[1].start()
+        groups = load_blocks(sources[:count], weight_ref, sems, blocks)
+
+        def act(start, span):
+            act_columns(start, span, hidden, normed_ref, back_ref, weight_ref, hidden_ref, pair_ref)
+
+        finish(held + groups[0])
+        act(0, WIDE)
+        finish(groups[1])
+
+        def act_wide(step, none):
+            act(pl.multiple_of(step * WIDE, WIDE), WIDE)
+            return none
+
+        lax.fori_loop(1, hidden // WIDE, act_wide, 0)
+        if hidden % WIDE:
+            act(hidden // WIDE * WIDE, hidden % WIDE)
+
+    low = jnp.bfloat16
+    return vmem_call(
+        body,
+        [
+            jax.ShapeDtypeStruct((rows, hidden), low),
+            jax.ShapeDtypeStruct((rows, 2 * hidden), low),
+            jax.ShapeDtypeStruct((depth, 3 * hidden), low),
+        ],
+        (*flat, normed, back), 36,
+        scratch=[
+            pltpu.VMEM((rows, depth), low),
+            pltpu.VMEM((rows, depth), low),
+            pltpu.SemaphoreType.DMA((6 * count + 2,)),
+        ],
+        scalars=0, anywhere=count + 2,
+        flops=2 * rows * depth * hidden * 3, moved=2 * (2 * rows * depth + 6 * depth * hidden + 3 * rows * hidden),
+    )
+
+
+def back_call(hidden_rows, pair_rows, weight, parity, earlier, parts):
+    rows, hidden = hidden_rows.shape
+    depth = weight.shape[0]
+
+    def body(parity_ref, hidden_ref, pair_ref, weight_ref, d_ref, y_ref, *refs):
+        outs, block_ref = refs[:-1], refs[-1]
+        parity, whole = parity_ref[0], slice(0, WIDE)
+        block_ref[...] = dot_nt(pair_ref[...], weight_ref[:, : 2 * hidden]) + d_ref[...].astype(jnp.float32)
+        give_halves(block_ref, parity, parts, whole, outs[:parts], outs[parts : 2 * parts])
+        block_ref[...] = dot_nt(hidden_ref[...], weight_ref[:, 2 * hidden :]) + y_ref[...].astype(jnp.float32)
+        give_halves(block_ref, parity, 1, whole, outs[2 * parts : 2 * parts + 1], outs[2 * parts + 1 :])
+
+    def still(step, parity_ref):
+        return (0, 0)
+
+    def across(step, parity_ref):
+        return (0, step)
+
+    def down(step, parity_ref):
+        return (step, 0)
+
+    heights = [rows // parts // 2] * (2 * parts) + [rows // 2] * 2
+    return pl.pallas_call(
+        body,
+        out_shape=[jax.ShapeDtypeStruct((height, depth), jnp.bfloat16) for height in heights],
+        grid_spec=pltpu.PrefetchScalarGridSpec(
+            num_scalar_prefetch=1,
+            grid=(depth // WIDE,),
+            in_specs=[
+                pl.BlockSpec((rows, hidden), still),
+                pl.BlockSpec((rows, 2 * hidden), still),
+                pl.BlockSpec((WIDE, 3 * hidden), down),
+                pl.BlockSpec((rows, WIDE), across),
+                pl.BlockSpec((rows, WIDE), across),
+            ],
+            out_specs=[pl.BlockSpec((height, WIDE), across) for height in heights],
+            scratch_shapes=[pltpu.VMEM((rows, WIDE), jnp.float32)],
+        ),
+        compiler_params=pltpu.CompilerParams(vmem_limit_bytes=26 * MEBI),
+        cost_estimate=pl.CostEstimate(
+            flops=2 * rows * depth * hidden * 3, bytes_accessed=2 * (4 * rows * depth + 3 * depth * hidden), transcendentals=0
+        ),
+    )(parity, hidden_rows, pair_rows, weight, *earlier)
 
 
 def sum_specs(parts, steps, rows, depth):
@@ -773,7 +974,7 @@
     return value.astype(jnp.float32)
 
 
-def row_call(body, scalars, parts, sums, whole, fixed, outs, narrow=()):
+def row_call(body, scalars, parts, sums, whole, fixed, outs, narrow=(), limit=16):
     rows, depth = whole[0].shape
     steps = rows // ROWS
     place = place_row(parts, steps)
@@ -791,7 +992,7 @@
             in_specs=sum_specs(parts, steps, ROWS, depth) + [block] * len(whole) + ones,
             out_specs=[block] * len(outs) + [pl.BlockSpec((ROWS, count), place) for count in narrow],
         ),
-        compiler_params=pltpu.CompilerParams(vmem_limit_bytes=LIMIT),
+        compiler_params=pltpu.CompilerParams(vmem_limit_bytes=limit * MEBI),
         cost_estimate=pl.CostEstimate(flops=10 * rows * depth, bytes_accessed=moved, transcendentals=0),
     )(scalars, *sums, *whole, *fixed)
 
@@ -864,7 +1065,7 @@
         slope = norm_back(total, rows_ref[...].astype(jnp.float32), gain_ref[...])
         store_placed(out_ref, d_resid_ref[...].astype(jnp.float32) + slope, scalar_ref, size)
 
-    (out,) = row_call(body, scalars, parts, sums, [d_resid, rows_in], [gain], [jnp.float32])
+    (out,) = row_call(body, scalars, parts, sums, [d_resid, rows_in], [gain], [jnp.float32], limit=60)
     return replaced(out, scalars[1:])
 
 
@@ -908,7 +1109,7 @@
     shapes = [(share, count), (share, count), (count, share), (share, 1)]
     return vmem_call(
         body, [jax.ShapeDtypeStruct(shape, jnp.float32) for shape in shapes],
-        (*grads, w_gate, w_up), scalars=0, moved=share * count * 36,
+        (*grads, w_gate, w_up), 24, scalars=0, moved=share * count * 36,
     )
 
 
@@ -929,20 +1130,21 @@
     shapes = [(share, width)] * 3 + [(share, slots), (width, share), (share, 1)]
     return vmem_call(
         body, [jax.ShapeDtypeStruct(shape, jnp.float32) for shape in shapes],
-        (*grads, mix_shard), scalars=0, moved=share * start * 14,
+        (*grads, mix_shard), 16, scalars=0, moved=share * start * 14,
     )
 
 
-def exchange(kept, sent):
+def exchange(kept, sent, held=()):
     heads = lax.axis_size(HEAD)
     near = [(i, i ^ 1) for i in range(heads)]
     far = [(i, i ^ 2) for i in range(heads)]
-    sums = []
+    sums, halves = [], []
     for own, given in zip(kept, sent):
         own = to_low(to_wide(own) + to_wide(lax.ppermute(given, HEAD, near)))
-        own = to_low(to_wide(own) + to_wide(lax.ppermute(own, HEAD, far)))
+        halves.append(own)
+        own = to_low(to_wide(own) + to_wide(tie(lax.ppermute(own, HEAD, far), *held)))
         sums += [own, lax.ppermute(own, HEAD, near)]
-    return sums
+    return sums, halves
 
 
 def layer(
@@ -996,7 +1198,7 @@
     bias = gate_bias[:, None]
     mixed, *saved = mixer_forward(lengths, qkv, logits, bias)
     kept, sent, (full_out,) = project_call(mixed, mix_pieces, parity, 2, mix_count, True)
-    sums = exchange(kept, sent)
+    sums, _ = exchange(kept, sent)
     resid, normed_two = norm_call(scalars, sums, rows_low, gain_two)
 
     middle = size // 2
@@ -1015,18 +1217,22 @@
 
     partial, feed_grads = None, []
     for pieces in feed_pieces:
-        hidden, pair, *partial = feed_call(normed_two, back_low, pieces, parity, partial, 2)
+        if partial is None:
+            hidden, pair, *partial = feed_call(normed_two, back_low, pieces, parity, None, 2)
+        else:
+            hidden, pair, weight = act_call(normed_two, back_low, pieces)
+            partial = back_call(hidden, pair, weight, parity, partial, 2)
         piece_of = grads_of([(normed_two, pair), (back_low, hidden)])
         feed_grads += ring_scatter(piece_of, order)
 
-    sums = exchange(partial[:2], partial[2:4])
+    sums, _ = exchange(partial[:2], partial[2:4])
     d_attn, d_mixed = norm_back_call(scalars, sums, resid, back_low, gain_two, full_out)
     d_all, d_bias = mixer_backward(lengths, qkv, logits, bias, d_mixed, saved)
     bias_sum = total_sum(d_bias[:, 0], DP)
     mix_grads = ring_scatter(grads_of([(normed, d_all), (d_attn, mixed)]), order)
     kept, sent, _ = project_call(d_all, mix_pieces, parity, 2, 0, False)
-    sums = exchange(kept, sent)
-    early = exchange([partial[4]], partial[5:])
+    sums, halves = exchange(kept, sent)
+    early, _ = exchange([partial[4]], partial[5:], halves)
     output = output_call(scalars, early, resid, size)
     *feed_out, gain_sum_two = finish_feed(feed_grads, w_gate, w_up, spans)
     sums[0] = tie(sums[0], output)

time: 834 us -> 758 us (0.909)
  Pallas kernels: 254 us -> 166 us
  local copies, waits for them, and re-layouts: 25.7 us -> 55.2 us
    ppermute x9, waiting for transfers between devices: 106 us -> 2.35 us  [ring_scatter(): up_sum = to_wide(lax.ppermute(to_low(up_piece), DP, up))]
    ppermute x9, waiting for transfers between devices: 40.6 us -> 96.1 us  [ring_scatter(): down_sum = to_wide(lax.ppermute(to_low(down_piece), DP, down))]
    ppermute x9, waiting for transfers between devices: 106 us -> 59.3 us  [ring_gather(): from_high = lax.ppermute(from_high, DP, down)]
    ppermute x9, waiting for transfers between devices: 61.5 us -> 98.7 us  [ring_gather(): from_low = lax.ppermute(from_low, DP, up)]
    pallas_call x7, Pallas kernels: 116 us -> 79.5 us  [vmem_call(): pl.pallas_call(body, out_shape=out_shape, in_specs=spaces, out_specs=[pl....]
    pallas_call x1, Pallas kernels: 52.6 us -> 20.2 us  [mixer_backward(): pl.pallas_call(backward_kernel, out_shape=(jax.ShapeDtypeStruct((rows, 3...]
    unnamed x138 -> x184, local copies, waits for them, and re-layouts: 6.43 us -> 33.6 us
    ppermute x7, waiting for transfers between devices: 34.5 us -> 57.9 us  [exchange(): lax.ppermute(own, HEAD, far)]
  transfers between devices with their start and end apart: 74 -> 74, of which waited for: 31 -> 29; matrix products, arithmetic and copies ran while one was open for 9% -> 13% of each run, Pallas kernels for 27% -> 18%
where the time goes in v1:
time: 758 us; the launch traced here: 748 us
  waiting for transfers between devices  378 us (50%)
  Pallas kernels  166 us (22%)
  starting transfers between devices  68.4 us (9%)
  local copies, waits for them, and re-layouts  55.2 us (7%)
  matrix products  44.3 us (6%)
  other arithmetic  34.3 us (5%)
    ppermute x9, waiting for transfers between devices, ring_gather(): from_low = lax.ppermute(from_low, DP, up)  98.7 us
    ppermute x9, waiting for transfers between devices, ring_scatter(): down_sum = to_wide(lax.ppermute(to_low(down_piece), DP, down))  96.1 us
    pallas_call x7, Pallas kernels, vmem_call(): pl.pallas_call(body, out_shape=out_shape, in_specs=spaces, out_specs=[pl....  79.5 us
    ppermute x9, waiting for transfers between devices, ring_gather(): from_high = lax.ppermute(from_high, DP, down)  59.3 us
    ppermute x7, waiting for transfers between devices, exchange(): lax.ppermute(own, HEAD, far)  57.9 us
    dot_general x12, matrix products, dot_tn(): lax.dot_general(left, right, (((0,), (0,)), ((), ())), preferred_element_...  44.3 us
    ppermute x5, waiting for transfers between devices, total_sum(): lax.ppermute(values, axis, [(i, i ^ step) for i in range(count)])  35.7 us
    pallas_call x4, Pallas kernels, row_call(): pl.pallas_call(body, out_shape=[jax.ShapeDtypeStruct((rows, depth), kind)...  34 us
  transfers between devices with their start and end apart: 74, of which 29 were waited for; matrix products, arithmetic and copies ran while one was open for 13% of the time, Pallas kernels for 18%

profile of v1, /device:TPU:0, one launch (start us, length us, event | category | flops | bytes accessed | tf_op | source)
XLA Modules:
  0.0 748.5 jit_solution(13243429554775967442)
XLA Ops:
  9.7 24.5 %collective-permute-done.4.refs_1_ = bf16[256,2176]{1,0:T(8,128)(2,1)S(1)} collective-permute-done((bf16[256,2176]{1,0:T(8,128)(2,1)S(1)}, bf16[256,2176]{1,0:T(8,128)(2,1)S(1)}, u32[]{:S(2)}, u32[]{:S(2)}) %collective-permute-start.4) | collective-permute-done | bytes 1114144 | tf_op jit(solution)/shard_map/ppermute | solution.py:519
  38.3 21.8 %collective-permute-done.5.refs_2_ = bf16[256,2176]{1,0:T(8,128)(2,1)} collective-permute-done((bf16[256,2176]{1,0:T(8,128)(2,1)S(1)}, bf16[256,2176]{1,0:T(8,128)(2,1)}, u32[]{:S(2)}, u32[]{:S(2)}) %collective-permute-start.5) | collective-permute-done | bytes 1114144 | tf_op jit(solution)/shard_map/ppermute | solution.py:519
  76.4 8.7 %collective-permute-done.6.refs_3_ = bf16[256,2176]{1,0:T(8,128)(2,1)S(1)} collective-permute-done((bf16[256,2176]{1,0:T(8,128)(2,1)}, bf16[256,2176]{1,0:T(8,128)(2,1)S(1)}, u32[]{:S(2)}, u32[]{:S(2)}) %collective-permute-start.6) | collective-permute-done | bytes 1114144 | tf_op jit(solution)/shard_map/ppermute | solution.py:519
  90.9 7.5 %collective-permute-done.7.refs_5_ = bf16[128,2176]{1,0:T(8,128)(2,1)} collective-permute-done((bf16[128,2176]{1,0:T(8,128)(2,1)}, bf16[128,2176]{1,0:T(8,128)(2,1)}, u32[]{:S(2)}, u32[]{:S(2)}) %collective-permute-start.7) | collective-permute-done | bytes 557088 | tf_op jit(solution)/shard_map/ppermute | solution.py:524
  105.6 11.8 %shard_map.257 = (bf16[1024,1536]{1,0:T(8,128)(2,1)S(1)}, f32[8,64,128]{2,1,0:T(8,128)S(1)}, bf16[1024,2048]{1,0:T(8,128)(2,1)S(1)}, f32[8,2048]{1,0:T(8,128)S(1)}) custom-call(bf16[1024,2048]{1,0:T(8,128)(2,1)S(1)} %copy-done.1, f32[1024,1]{1,0:T(8,128)S(1)} %copy-done.35, bf16[256,2176]{1,0:T(8,128)(2,1)S(1)} %concatenate.119.refs_0_.refs_3_, ...), custom_call_target="tpu_custom_call" | custom-call | flops 6979321856 | bytes 14417920 | tf_op jit(solution)/shard_map/pallas_call | solution.py:604
  119.4 12.9 %mixer_forward.1 = (bf16[1024,512]{1,0:T(8,128)(2,1)S(1)}, f32[8,128,1024]{2,1,0:T(8,128)S(1)}, f32[8,64,128]{2,1,0:T(8,128)S(1)}, f32[8,64,128]{2,1,0:T(8,128)S(1)}, bf16[8,128,128]{2,1,0:T(8,128)(2,1)S(1)}) custom-call(s32[1]{0:T(128)S(6)} %copy.62.length_ref, bf16[1024,1536]{1,0:T(8,128)(2,1)S(1)} %get-tuple-element.69.qkv_ref, ...), custom_call_target="tpu_custom_call" | custom-call | tf_op jit(solution)/shard_map/mixer_forward/pallas_call | solution.py:436
  134.4 6.4 shard_map.258
  144.6 21.2 %collective-permute-done.11.refs_8_ = bf16[256,1920]{1,0:T(8,128)(2,1)S(1)} collective-permute-done((bf16[256,1920]{1,0:T(8,128)(2,1)S(1)}, bf16[256,1920]{1,0:T(8,128)(2,1)S(1)}, u32[]{:S(2)}, u32[]{:S(2)}) %collective-permute-start.11) | collective-permute-done | bytes 983072 | tf_op jit(solution)/shard_map/ppermute | solution.py:518
  171.7 19.3 %collective-permute-done.25.refs_8_ = bf16[256,2304]{1,0:T(8,128)(2,1)S(1)} collective-permute-done((bf16[256,2304]{1,0:T(8,128)(2,1)S(1)}, bf16[256,2304]{1,0:T(8,128)(2,1)S(1)}, u32[]{:S(2)}, u32[]{:S(2)}) %collective-permute-start.25) | collective-permute-done | bytes 1179680 | tf_op jit(solution)/shard_map/ppermute | solution.py:518
  195.8 16.3 %collective-permute-done.12.refs_7_ = bf16[256,1920]{1,0:T(8,128)(2,1)S(1)} collective-permute-done((bf16[256,1920]{1,0:T(8,128)(2,1)S(1)}, bf16[256,1920]{1,0:T(8,128)(2,1)S(1)}, u32[]{:S(2)}, u32[]{:S(2)}) %collective-permute-start.12) | collective-permute-done | bytes 983072 | tf_op jit(solution)/shard_map/ppermute | solution.py:518
  216.7 41.2 %collective-permute-done.13.refs_6_ = bf16[256,1920]{1,0:T(8,128)(2,1)S(1)} collective-permute-done((bf16[256,1920]{1,0:T(8,128)(2,1)S(1)}, bf16[256,1920]{1,0:T(8,128)(2,1)S(1)}, u32[]{:S(2)}, u32[]{:S(2)}) %collective-permute-start.13) | collective-permute-done | bytes 983072 | tf_op jit(solution)/shard_map/ppermute | solution.py:518
  275.5 13.3 %shard_map.260 = (bf16[1024,640]{1,0:T(8,128)(2,1)S(1)}, bf16[1024,1280]{1,0:T(8,128)(2,1)S(1)}, bf16[2048,1920]{1,0:T(8,128)(2,1)}) custom-call(bf16[256,1920]{1,0:T(8,128)(2,1)S(1)} %pad_maximum_fusion.3.refs_0_, bf16[256,1920]{1,0:T(8,128)(2,1)S(1)} %collective-permute-done.8.refs_1_, bf16[256,1920]{1,0:T(8,128)(2,1)S(1)} %collective-permute-done.9.refs_2_, ...), custom_call_target="tpu_custom_call" | custom-call | flops 8053063680 | bytes 28049408 | tf_op jit(solution)/shard_map/pallas_call | solution.py:604
  290.4 7.8 %convolution_convert_fusion = bf16[2048,1280]{1,0:T(8,128)(2,1)S(1)} fusion(bf16[1024,2048]{1,0:T(8,128)(2,1)} %copy-done.45, bf16[1024,1280]{1,0:T(8,128)(2,1)S(1)} %get-tuple-element.79.pair_ref), kind=kOutput, calls=%fused_computation.2 | convolution fusion | flops 5371330560 | bytes 12058624 | tf_op jit(solution)/shard_map/dot_general | solution.py:496
  317.7 10.2 %collective-permute-done.28.refs_4_ = bf16[128,2304]{1,0:T(8,128)(2,1)S(1)} collective-permute-done((bf16[128,2304]{1,0:T(8,128)(2,1)S(1)}, bf16[128,2304]{1,0:T(8,128)(2,1)S(1)}, u32[]{:S(2)}, u32[]{:S(2)}) %collective-permute-start.28) | collective-permute-done | bytes 589856 | tf_op jit(solution)/shard_map/ppermute | solution.py:523
  331.7 29.4 %shard_map.261 = (bf16[1024,768]{1,0:T(8,128)(2,1)}, bf16[1024,1536]{1,0:T(8,128)(2,1)}, bf16[1024,2048]{1,0:T(8,128)(2,1)}, bf16[1024,2048]{1,0:T(8,128)(2,1)}) custom-call(s32[1]{0:T(128)} %bitcast.parity_ref, bf16[256,2304]{1,0:T(8,128)(2,1)S(1)} %copy-done.24, bf16[256,2304]{1,0:T(8,128)(2,1)S(1)} %copy-done.48, bf16[256,2304]{1,0:T(8,128)(2,1)S(1)} %copy-done.50, ...), custom_call_target="tpu_custom_call" | custom-call | flops 19327352832 | bytes 26738688 | tf_op jit(solution)/shard_map/pallas_call | solution.py:604
  363.3 5.0 convolution_convert_fusion.3
  369.3 9.2 %convolution_convert_fusion.1 = bf16[2048,1536]{1,0:T(8,128)(2,1)} fusion(bf16[1024,2048]{1,0:T(8,128)(2,1)S(1)} %copy-done.46, bf16[1024,1536]{1,0:T(8,128)(2,1)S(1)} %copy-done.89), kind=kOutput, calls=%fused_computation.3 | convolution fusion | flops 6445596672 | bytes 13631488 | tf_op jit(solution)/shard_map/dot_general | solution.py:496
  386.7 14.9 %shard_map.262 = (bf16[256,2048]{1,0:T(8,128)(2,1)S(1)}, bf16[256,2048]{1,0:T(8,128)(2,1)S(1)}, bf16[256,2048]{1,0:T(8,128)(2,1)S(1)}, bf16[256,2048]{1,0:T(8,12...) custom-call(s32[1]{0:T(128)} %bitcast.parity_ref, bf16[1024,640]{1,0:T(8,128)(2,1)S(1)} %copy-done.60, ...), custom_call_target="tpu_custom_call" | custom-call | flops 8053063680 | bytes 24641536 | tf_op jit(solution)/shard_map/pallas_call | solution.py:926
  417.7 44.0 %collective-permute-done.67 = bf16[256,1920]{1,0:T(8,128)(2,1)S(1)} collective-permute-done((bf16[256,1920]{1,0:T(8,128)(2,1)S(1)}, bf16[256,1920]{1,0:T(8,128)(2,1)S(1)}, u32[]{:S(2)}, u32[]{:S(2)}) %collective-permute-start.67) | collective-permute-done | bytes 983072 | tf_op jit(solution)/shard_map/ppermute | solution.py:546
  468.9 18.8 %collective-permute-done.33 = bf16[256,2048]{1,0:T(8,128)(2,1)S(1)} collective-permute-done((bf16[256,2048]{1,0:T(8,128)(2,1)S(1)}, bf16[256,2048]{1,0:T(8,128)(2,1)S(1)}, u32[]{:S(2)}, u32[]{:S(2)}) %collective-permute-start.33) | collective-permute-done | bytes 1048608 | tf_op jit(solution)/shard_map/ppermute | solution.py:1145
  488.2 20.3 %collective-permute-done.36 = bf16[256,2048]{1,0:T(8,128)(2,1)S(1)} collective-permute-done((bf16[256,2048]{1,0:T(8,128)(2,1)S(1)}, bf16[256,2048]{1,0:T(8,128)(2,1)S(1)}, u32[]{:S(2)}, u32[]{:S(2)}) %collective-permute-start.36) | collective-permute-done | bytes 1048608 | tf_op jit(solution)/shard_map/ppermute | solution.py:1145
  515.4 8.9 %shard_map.263 = (bf16[1024,2048]{1,0:T(8,128)(2,1)S(1)}, bf16[1024,512]{1,0:T(8,128)(2,1)S(1)}) custom-call(s32[9]{0:T(128)S(1)} %pad_add_fusion.scalar_ref, bf16[256,2048]{1,0:T(8,128)(2,1)S(1)} %add_convert_fusion.20.refs_0_, bf16[256,2048]{1,0:T(8,128)(2,1)S(1)} %collective-permute-done.34.refs_1_, bf16[256,2048]{1,0:T(8,128)(2,1)S(1)} %add_convert_fusion.18.refs_2_, ...), custom_call_target="tpu_custom_call" | custom-call | flops 20971520 | bytes 16777216 | tf_op jit(solution)/shard_map/pallas_call | solution.py:985
  524.4 20.2 %mixer_backward.1 = (bf16[1024,1664]{1,0:T(8,128)(2,1)S(1)}, f32[64,128]{1,0:T(8,128)S(1)}) custom-call(s32[1]{0:T(128)S(6)} %copy.62.length_ref, bf16[1024,1536]{1,0:T(8,128)(2,1)S(1)} %copy-done.9, f32[8,64,128]{2,1,0:T(8,128)S(1)} %copy-done.34, f32[64,1]{1,0:T(8,128)S(1)} %copy.47.bias_ref, bf16[1024,512]{1,0:T(8,128)(2,1)S(1)} %get-tuple-element.92.back_ref, ...), custom_call_target="tpu_custom_call" | custom-call | tf_op jit(solution)/shard_map/mixer_backward/pallas_call | solution.py:463
  545.8 9.9 %convolution_convert_fusion.2 = bf16[2048,1664]{1,0:T(8,128)(2,1)} fusion(bf16[1024,2048]{1,0:T(8,128)(2,1)S(1)} %copy-done.58, bf16[1024,1664]{1,0:T(8,128)(2,1)S(1)} %get-tuple-element.97.left_ref), kind=kOutput, calls=%fused_computation.4 | convolution fusion | flops 6982729728 | bytes 14417920 | tf_op jit(solution)/shard_map/dot_general | solution.py:496
  562.9 12.0 %shard_map.264 = (bf16[256,2048]{1,0:T(8,128)(2,1)S(1)}, bf16[256,2048]{1,0:T(8,128)(2,1)S(1)}, bf16[256,2048]{1,0:T(8,128)(2,1)S(1)}, bf16[256,2048]{1,0:T(8,128)(2,1)S(1)}) custom-call(s32[1]{0:T(128)} %bitcast.parity_ref, bf16[1024,1664]{1,0:T(8,128)(2,1)S(1)} %get-tuple-element.97.left_ref, bf16[256,2176]{1,0:T(8,128)(2,1)S(1)} %concatenate.119.refs_0_.refs_3_, ...), custom_call_target="tpu_custom_call" | custom-call | flops 6979321856 | bytes 14417920 | tf_op jit(solution)/shard_map/pallas_call | solution.py:604
  579.6 12.9 %collective-permute-done.72 = f32[64]{0:T(128)S(1)} collective-permute-done((f32[64]{0:T(128)S(1)}, f32[64]{0:T(128)S(1)}, u32[]{:S(2)}, u32[]{:S(2)}) %collective-permute-start.72) | collective-permute-done | bytes 288 | tf_op jit(solution)/shard_map/ppermute | solution.py:554
  602.9 36.7 %collective-permute-done.50 = bf16[256,2176]{1,0:T(8,128)(2,1)S(1)} collective-permute-done((bf16[256,2176]{1,0:T(8,128)(2,1)S(1)}, bf16[256,2176]{1,0:T(8,128)(2,1)S(1)}, u32[]{:S(2)}, u32[]{:S(2)}) %collective-permute-start.50) | collective-permute-done | bytes 1114144 | tf_op jit(solution)/shard_map/ppermute | solution.py:546
  644.6 18.7 %collective-permute-done.43 = bf16[256,2048]{1,0:T(8,128)(2,1)S(1)} collective-permute-done((bf16[256,2048]{1,0:T(8,128)(2,1)S(1)}, bf16[256,2048]{1,0:T(8,128)(2,1)S(1)}, u32[]{:S(2)}, u32[]{:S(2)}) %collective-permute-start.43) | collective-permute-done | bytes 1048608 | tf_op jit(solution)/shard_map/ppermute | solution.py:1145
  674.5 22.7 %collective-permute-done.73 = f32[64]{0:T(128)S(1)} collective-permute-done((f32[64]{0:T(128)S(1)}, f32[64]{0:T(128)S(1)}, u32[]{:S(2)}, u32[]{:S(2)}) %collective-permute-start.73) | collective-permute-done | bytes 288 | tf_op jit(solution)/shard_map/ppermute | solution.py:554
  705.0 13.1 %collective-permute-done.52.refs_2_ = bf16[256,2176]{1,0:T(8,128)(2,1)} collective-permute-done((bf16[256,2176]{1,0:T(8,128)(2,1)}, bf16[256,2176]{1,0:T(8,128)(2,1)}, u32[]{:S(2)}, u32[]{:S(2)}) %collective-permute-start.52) | collective-permute-done | bytes 1114144 | tf_op jit(solution)/shard_map/ppermute | solution.py:546
  725.7 7.8 %shard_map.265 = bf16[1024,2048]{1,0:T(8,128)(2,1)} custom-call(s32[9]{0:T(128)S(1)} %pad_add_fusion.scalar_ref, bf16[512,2048]{1,0:T(8,128)(2,1)} %add_convert_fusion.refs_0_, bf16[512,2048]{1,0:T(8,128)(2,1)} %collective-permute-done.40.refs_1_, bf16[1024,2048]{1,0:T(8,128)(2,1)S(1)} %copy-done.7), custom_call_target="tpu_custom_call" | custom-call | flops 20971520 | bytes 12582912 | tf_op jit(solution)/shard_map/pallas_call | solution.py:985
  734.1 12.8 %shard_map.266 = f32[1024,2048]{1,0:T(8,128)} custom-call(s32[9]{0:T(128)} %copy-done.44, bf16[256,2048]{1,0:T(8,128)(2,1)} %add_convert_fusion.15.refs_0_, bf16[256,2048]{1,0:T(8,128)(2,1)} %collective-permute-done.42.refs_1_, bf16[256,2048]{1,0:T(8,128)(2,1)} %add_convert_fusion.14.refs_2_, bf16[256,2048]{1,0:T(8,128)(2,1)} %collective-permute-done.44.refs_3_, ...), custom_call_target="tpu_custom_call" | custom-call | flops 20971520 | bytes 20971520 | tf_op jit(solution)/shard_map/pallas_call | solution.py:985
  (415 shorter events, 205.2 us)
Async XLA Ops:
  143.3 47.7 %collective-permute-start.25 = (bf16[256,2304]{1,0:T(8,128)(2,1)S(1)}, bf16[256,2304]{1,0:T(8,128)(2,1)S(1)}, u32[]{:S(2)}, u32[]{:S(2)}) collective-permute-start(bf16[256,2304]{1,0:T(8,128)(2,1)S(1)} %pad_maximum_fusion.refs_0_), channel_id=1, source_target_pairs={{0,8},{8,16},{16,24},{24,28},{28,20},{20,12},{12,4},{4,0},{1,9},{9... | collective-permute-start | bytes 3538952 | tf_op jit(solution)/shard_map/ppermute | solution.py:518
  167.3 44.8 %collective-permute-start.12 = (bf16[256,1920]{1,0:T(8,128)(2,1)S(1)}, bf16[256,1920]{1,0:T(8,128)(2,1)S(1)}, u32[]{:S(2)}, u32[]{:S(2)}) collective-permute-start(bf16[256,1920]{1,0:T(8,128)(2,1)S(1)} %collective-permute-done.11.refs_8_), channel_id=1, source_target_pairs={{0,8},{8,16},{16,24},{24,28},{28,20},{20,12},{12,4},{4,0},{1,9},{9... | collective-permute-start | bytes 2949128 | tf_op jit(solution)/shard_map/ppermute | solution.py:518
  167.8 46.0 %collective-permute-start.9 = (bf16[256,1920]{1,0:T(8,128)(2,1)S(1)}, bf16[256,1920]{1,0:T(8,128)(2,1)S(1)}, u32[]{:S(2)}, u32[]{:S(2)}) collective-permute-start(bf16[256,1920]{1,0:T(8,128)(2,1)S(1)} %collective-permute-done.8.refs_1_), channel_id=1, source_target_pairs={{0,4},{8,0},{16,8},{24,16},{28,24},{20,28},{12,20},{4,12},{1,5},{9... | collective-permute-start | bytes 2949128 | tf_op jit(solution)/shard_map/ppermute | solution.py:519
  169.7 45.2 %collective-permute-start.17 = (bf16[256,2048]{1,0:T(8,128)(2,1)S(1)}, bf16[256,2048]{1,0:T(8,128)(2,1)S(1)}, u32[]{:S(2)}, u32[]{:S(2)}) collective-permute-start(bf16[256,2048]{1,0:T(8,128)(2,1)S(1)} %add_convert_fusion.25), channel_id=1, source_target_pairs={{0,2},{1,3},{2,0},{3,1},{4,6},{5,7},{6,4},{7,5},{8,10},{9,11},{10,... | collective-permute-start | bytes 3145736 | tf_op jit(solution)/shard_map/ppermute | solution.py:1145
  194.6 66.8 %collective-permute-start.26 = (bf16[256,2304]{1,0:T(8,128)(2,1)S(1)}, bf16[256,2304]{1,0:T(8,128)(2,1)}, u32[]{:S(2)}, u32[]{:S(2)}) collective-permute-start(bf16[256,2304]{1,0:T(8,128)(2,1)S(1)} %collective-permute-done.25.refs_8_), channel_id=1, source_target_pairs={{0,8},{8,16},{16,24},{24,28},{28,20},{20,12},{12,4},{4,0},{1,9},{9... | collective-permute-start | bytes 3538952 | tf_op jit(solution)/shard_map/ppermute | solution.py:518
  212.1 50.9 %collective-permute-start.23 = (bf16[256,2304]{1,0:T(8,128)(2,1)S(1)}, bf16[256,2304]{1,0:T(8,128)(2,1)S(1)}, u32[]{:S(2)}, u32[]{:S(2)}) collective-permute-start(bf16[256,2304]{1,0:T(8,128)(2,1)S(1)} %collective-permute-done.22.refs_1_), channel_id=1, source_target_pairs={{0,4},{8,0},{16,8},{24,16},{28,24},{20,28},{12,20},{4,12},{1,5},{9... | collective-permute-start | bytes 3538952 | tf_op jit(solution)/shard_map/ppermute | solution.py:519
  213.8 44.1 %collective-permute-start.13 = (bf16[256,1920]{1,0:T(8,128)(2,1)S(1)}, bf16[256,1920]{1,0:T(8,128)(2,1)S(1)}, u32[]{:S(2)}, u32[]{:S(2)}) collective-permute-start(bf16[256,1920]{1,0:T(8,128)(2,1)S(1)} %collective-permute-done.12.refs_7_), channel_id=1, source_target_pairs={{0,8},{8,16},{16,24},{24,28},{28,20},{20,12},{12,4},{4,0},{1,9},{9... | collective-permute-start | bytes 2949128 | tf_op jit(solution)/shard_map/ppermute | solution.py:518
  215.0 45.1 %collective-permute-start.10 = (bf16[256,1920]{1,0:T(8,128)(2,1)S(1)}, bf16[256,1920]{1,0:T(8,128)(2,1)S(1)}, u32[]{:S(2)}, u32[]{:S(2)}) collective-permute-start(bf16[256,1920]{1,0:T(8,128)(2,1)S(1)} %collective-permute-done.9.refs_2_), channel_id=1, source_target_pairs={{0,4},{8,0},{16,8},{24,16},{28,24},{20,28},{12,20},{4,12},{1,5},{9... | collective-permute-start | bytes 2949128 | tf_op jit(solution)/shard_map/ppermute | solution.py:519
  216.2 47.9 %collective-permute-start.18 = (bf16[256,2048]{1,0:T(8,128)(2,1)S(1)}, bf16[256,2048]{1,0:T(8,128)(2,1)S(1)}, u32[]{:S(2)}, u32[]{:S(2)}) collective-permute-start(bf16[256,2048]{1,0:T(8,128)(2,1)S(1)} %add_convert_fusion.24.refs_0_), channel_id=1, source_target_pairs={{0,1},{1,0},{2,3},{3,2},{4,5},{5,4},{6,7},{7,6},{8,9},{9,8},{10,11... | collective-permute-start | bytes 3145736 | tf_op jit(solution)/shard_map/ppermute | solution.py:1146
  262.9 44.5 %collective-permute-start.27 = (bf16[256,2304]{1,0:T(8,128)(2,1)}, bf16[256,2304]{1,0:T(8,128)(2,1)S(1)}, u32[]{:S(2)}, u32[]{:S(2)}) collective-permute-start(bf16[256,2304]{1,0:T(8,128)(2,1)} %collective-permute-done.26.refs_7_), channel_id=1, source_target_pairs={{0,8},{8,16},{16,24},{24,28},{28,20},{20,12},{12,4},{4,0},{1,9},{9... | collective-permute-start | bytes 3538952 | tf_op jit(solution)/shard_map/ppermute | solution.py:518
  264.2 45.3 %collective-permute-start.24 = (bf16[256,2304]{1,0:T(8,128)(2,1)S(1)}, bf16[256,2304]{1,0:T(8,128)(2,1)S(1)}, u32[]{:S(2)}, u32[]{:S(2)}) collective-permute-start(bf16[256,2304]{1,0:T(8,128)(2,1)S(1)} %collective-permute-done.23.refs_2_), channel_id=1, source_target_pairs={{0,4},{8,0},{16,8},{24,16},{28,24},{20,28},{12,20},{4,12},{1,5},{9... | collective-permute-start | bytes 3538952 | tf_op jit(solution)/shard_map/ppermute | solution.py:519
  314.0 95.6 %collective-permute-start.66 = (bf16[256,1920]{1,0:T(8,128)(2,1)}, bf16[256,1920]{1,0:T(8,128)(2,1)}, u32[]{:S(2)}, u32[]{:S(2)}) collective-permute-start(bf16[256,1920]{1,0:T(8,128)(2,1)} %add_convert_fusion.28), channel_id=1, source_target_pairs={{0,4},{8,0},{16,8},{24,16},{28,24},{20,28},{12,20},{4,12},{1,5},{9... | collective-permute-start | bytes 2949128 | tf_op jit(solution)/shard_map/ppermute | solution.py:546
  316.3 96.3 %collective-permute-start.62 = (bf16[256,1920]{1,0:T(8,128)(2,1)}, bf16[256,1920]{1,0:T(8,128)(2,1)}, u32[]{:S(2)}, u32[]{:S(2)}) collective-permute-start(bf16[256,1920]{1,0:T(8,128)(2,1)} %add_convert_fusion.31), channel_id=1, source_target_pairs={{0,8},{8,16},{16,24},{24,28},{28,20},{20,12},{12,4},{4,0},{1,9},{9... | collective-permute-start | bytes 2949128 | tf_op jit(solution)/shard_map/ppermute | solution.py:545
  408.2 100.8 %collective-permute-start.30 = (bf16[512,2048]{1,0:T(8,128)(2,1)}, bf16[512,2048]{1,0:T(8,128)(2,1)S(1)}, u32[]{:S(2)}, u32[]{:S(2)}) collective-permute-start(bf16[512,2048]{1,0:T(8,128)(2,1)} %get-tuple-element.85), channel_id=1, source_target_pairs={{0,1},{1,0},{2,3},{3,2},{4,5},{5,4},{6,7},{7,6},{8,9},{9,8},{10,11... | collective-permute-start | bytes 6291464 | tf_op jit(solution)/shard_map/ppermute | solution.py:1143
  409.6 56.5 %collective-permute-start.54 = (bf16[256,2304]{1,0:T(8,128)(2,1)S(1)}, bf16[256,2304]{1,0:T(8,128)(2,1)S(1)}, u32[]{:S(2)}, u32[]{:S(2)}) collective-permute-start(bf16[256,2304]{1,0:T(8,128)(2,1)S(1)} %add_convert_fusion.7), channel_id=1, source_target_pairs={{0,8},{8,16},{16,24},{24,28},{28,20},{20,12},{12,4},{4,0},{1,9},{9... | collective-permute-start | bytes 3538952 | tf_op jit(solution)/shard_map/ppermute | solution.py:545
  412.6 54.4 %collective-permute-start.58 = (bf16[256,2304]{1,0:T(8,128)(2,1)S(1)}, bf16[256,2304]{1,0:T(8,128)(2,1)S(1)}, u32[]{:S(2)}, u32[]{:S(2)}) collective-permute-start(bf16[256,2304]{1,0:T(8,128)(2,1)S(1)} %add_convert_fusion.4), channel_id=1, source_target_pairs={{0,4},{8,0},{16,8},{24,16},{28,24},{20,28},{12,20},{4,12},{1,5},{9... | collective-permute-start | bytes 3538952 | tf_op jit(solution)/shard_map/ppermute | solution.py:546
  414.7 47.0 %collective-permute-start.67 = (bf16[256,1920]{1,0:T(8,128)(2,1)S(1)}, bf16[256,1920]{1,0:T(8,128)(2,1)S(1)}, u32[]{:S(2)}, u32[]{:S(2)}) collective-permute-start(bf16[256,1920]{1,0:T(8,128)(2,1)S(1)} %add_convert_fusion.27), channel_id=1, source_target_pairs={{0,4},{8,0},{16,8},{24,16},{28,24},{20,28},{12,20},{4,12},{1,5},{9... | collective-permute-start | bytes 2949128 | tf_op jit(solution)/shard_map/ppermute | solution.py:546
  416.9 46.6 %collective-permute-start.63 = (bf16[256,1920]{1,0:T(8,128)(2,1)S(1)}, bf16[256,1920]{1,0:T(8,128)(2,1)S(1)}, u32[]{:S(2)}, u32[]{:S(2)}) collective-permute-start(bf16[256,1920]{1,0:T(8,128)(2,1)S(1)} %add_convert_fusion.30), channel_id=1, source_target_pairs={{0,8},{8,16},{16,24},{24,28},{28,20},{20,12},{12,4},{4,0},{1,9},{9... | collective-permute-start | bytes 2949128 | tf_op jit(solution)/shard_map/ppermute | solution.py:545
  463.6 45.0 %collective-permute-start.36 = (bf16[256,2048]{1,0:T(8,128)(2,1)S(1)}, bf16[256,2048]{1,0:T(8,128)(2,1)S(1)}, u32[]{:S(2)}, u32[]{:S(2)}) collective-permute-start(bf16[256,2048]{1,0:T(8,128)(2,1)S(1)} %add_convert_fusion.19), channel_id=1, source_target_pairs={{0,2},{1,3},{2,0},{3,1},{4,6},{5,7},{6,4},{7,5},{8,10},{9,11},{10,... | collective-permute-start | bytes 3145736 | tf_op jit(solution)/shard_map/ppermute | solution.py:1145
  466.5 45.6 %collective-permute-start.55 = (bf16[256,2304]{1,0:T(8,128)(2,1)S(1)}, bf16[256,2304]{1,0:T(8,128)(2,1)S(1)}, u32[]{:S(2)}, u32[]{:S(2)}) collective-permute-start(bf16[256,2304]{1,0:T(8,128)(2,1)S(1)} %add_convert_fusion.6), channel_id=1, source_target_pairs={{0,8},{8,16},{16,24},{24,28},{28,20},{20,12},{12,4},{4,0},{1,9},{9... | collective-permute-start | bytes 3538952 | tf_op jit(solution)/shard_map/ppermute | solution.py:545
  467.3 46.1 %collective-permute-start.59 = (bf16[256,2304]{1,0:T(8,128)(2,1)S(1)}, bf16[256,2304]{1,0:T(8,128)(2,1)S(1)}, u32[]{:S(2)}, u32[]{:S(2)}) collective-permute-start(bf16[256,2304]{1,0:T(8,128)(2,1)S(1)} %add_convert_fusion.3), channel_id=1, source_target_pairs={{0,4},{8,0},{16,8},{24,16},{28,24},{20,28},{12,20},{4,12},{1,5},{9... | collective-permute-start | bytes 3538952 | tf_op jit(solution)/shard_map/ppermute | solution.py:546
  511.1 86.7 %collective-permute-start.31 = (bf16[512,2048]{1,0:T(8,128)(2,1)}, bf16[512,2048]{1,0:T(8,128)(2,1)}, u32[]{:S(2)}, u32[]{:S(2)}) collective-permute-start(bf16[512,2048]{1,0:T(8,128)(2,1)} %add_convert_fusion.1), channel_id=1, source_target_pairs={{0,2},{1,3},{2,0},{3,1},{4,6},{5,7},{6,4},{7,5},{8,10},{9,11},{10,... | collective-permute-start | bytes 6291464 | tf_op jit(solution)/shard_map/ppermute | solution.py:1145
  592.5 77.1 %collective-permute-start.68 = (bf16[256,1920]{1,0:T(8,128)(2,1)S(1)}, bf16[256,1920]{1,0:T(8,128)(2,1)S(1)}, u32[]{:S(2)}, u32[]{:S(2)}) collective-permute-start(bf16[256,1920]{1,0:T(8,128)(2,1)S(1)} %copy-done.82), channel_id=1, source_target_pairs={{0,4},{8,0},{16,8},{24,16},{28,24},{20,28},{12,20},{4,12},{1,5},{9... | collective-permute-start | bytes 2949128 | tf_op jit(solution)/shard_map/ppermute | solution.py:546
  592.8 80.2 %collective-permute-start.64 = (bf16[256,1920]{1,0:T(8,128)(2,1)S(1)}, bf16[256,1920]{1,0:T(8,128)(2,1)S(1)}, u32[]{:S(2)}, u32[]{:S(2)}) collective-permute-start(bf16[256,1920]{1,0:T(8,128)(2,1)S(1)} %copy-done.81), channel_id=1, source_target_pairs={{0,8},{8,16},{16,24},{24,28},{28,20},{20,12},{12,4},{4,0},{1,9},{9... | collective-permute-start | bytes 2949128 | tf_op jit(solution)/shard_map/ppermute | solution.py:545
  594.9 44.7 %collective-permute-start.50 = (bf16[256,2176]{1,0:T(8,128)(2,1)S(1)}, bf16[256,2176]{1,0:T(8,128)(2,1)S(1)}, u32[]{:S(2)}, u32[]{:S(2)}) collective-permute-start(bf16[256,2176]{1,0:T(8,128)(2,1)S(1)} %add_convert_fusion.10), channel_id=1, source_target_pairs={{0,4},{8,0},{16,8},{24,16},{28,24},{20,28},{12,20},{4,12},{1,5},{9... | collective-permute-start | bytes 3342344 | tf_op jit(solution)/shard_map/ppermute | solution.py:546
  595.5 45.4 %collective-permute-start.46 = (bf16[256,2176]{1,0:T(8,128)(2,1)S(1)}, bf16[256,2176]{1,0:T(8,128)(2,1)S(1)}, u32[]{:S(2)}, u32[]{:S(2)}) collective-permute-start(bf16[256,2176]{1,0:T(8,128)(2,1)S(1)} %add_convert_fusion.13), channel_id=1, source_target_pairs={{0,8},{8,16},{16,24},{24,28},{28,20},{20,12},{12,4},{4,0},{1,9},{9... | collective-permute-start | bytes 3342344 | tf_op jit(solution)/shard_map/ppermute | solution.py:545
  597.9 44.6 %collective-permute-start.41 = (bf16[256,2048]{1,0:T(8,128)(2,1)S(1)}, bf16[256,2048]{1,0:T(8,128)(2,1)S(1)}, u32[]{:S(2)}, u32[]{:S(2)}) collective-permute-start(bf16[256,2048]{1,0:T(8,128)(2,1)S(1)} %add_convert_fusion.17), channel_id=1, source_target_pairs={{0,2},{1,3},{2,0},{3,1},{4,6},{5,7},{6,4},{7,5},{8,10},{9,11},{10,... | collective-permute-start | bytes 3145736 | tf_op jit(solution)/shard_map/ppermute | solution.py:1145
  663.4 36.5 %collective-permute-start.56 = (bf16[256,2304]{1,0:T(8,128)(2,1)S(1)}, bf16[256,2304]{1,0:T(8,128)(2,1)S(1)}, u32[]{:S(2)}, u32[]{:S(2)}) collective-permute-start(bf16[256,2304]{1,0:T(8,128)(2,1)S(1)} %copy-done.79), channel_id=1, source_target_pairs={{0,8},{8,16},{16,24},{24,28},{28,20},{20,12},{12,4},{4,0},{1,9},{9... | collective-permute-start | bytes 3538952 | tf_op jit(solution)/shard_map/ppermute | solution.py:545
  671.7 51.8 %collective-permute-start.40 = (bf16[512,2048]{1,0:T(8,128)(2,1)}, bf16[512,2048]{1,0:T(8,128)(2,1)}, u32[]{:S(2)}, u32[]{:S(2)}) collective-permute-start(bf16[512,2048]{1,0:T(8,128)(2,1)} %add_convert_fusion.refs_0_), channel_id=1, source_target_pairs={{0,1},{1,0},{2,3},{3,2},{4,5},{5,4},{6,7},{7,6},{8,9},{9,8},{10,11... | collective-permute-start | bytes 6291464 | tf_op jit(solution)/shard_map/ppermute | solution.py:1146
  673.0 45.1 %collective-permute-start.52 = (bf16[256,2176]{1,0:T(8,128)(2,1)}, bf16[256,2176]{1,0:T(8,128)(2,1)}, u32[]{:S(2)}, u32[]{:S(2)}) collective-permute-start(bf16[256,2176]{1,0:T(8,128)(2,1)} %add_convert_fusion.8), channel_id=1, source_target_pairs={{0,4},{8,0},{16,8},{24,16},{28,24},{20,28},{12,20},{4,12},{1,5},{9... | collective-permute-start | bytes 3342344 | tf_op jit(solution)/shard_map/ppermute | solution.py:546
  699.9 34.2 %collective-permute-start.42 = (bf16[256,2048]{1,0:T(8,128)(2,1)}, bf16[256,2048]{1,0:T(8,128)(2,1)}, u32[]{:S(2)}, u32[]{:S(2)}) collective-permute-start(bf16[256,2048]{1,0:T(8,128)(2,1)} %add_convert_fusion.15.refs_0_), channel_id=1, source_target_pairs={{0,1},{1,0},{2,3},{3,2},{4,5},{5,4},{6,7},{7,6},{8,9},{9,8},{10,11... | collective-permute-start | bytes 3145736 | tf_op jit(solution)/shard_map/ppermute | solution.py:1146
  699.9 34.2 %collective-permute-start.44 = (bf16[256,2048]{1,0:T(8,128)(2,1)}, bf16[256,2048]{1,0:T(8,128)(2,1)}, u32[]{:S(2)}, u32[]{:S(2)}) collective-permute-start(bf16[256,2048]{1,0:T(8,128)(2,1)} %add_convert_fusion.14.refs_2_), channel_id=1, source_target_pairs={{0,1},{1,0},{2,3},{3,2},{4,5},{5,4},{6,7},{7,6},{8,9},{9,8},{10,11... | collective-permute-start | bytes 3145736 | tf_op jit(solution)/shard_map/ppermute | solution.py:1146
  (136 other events, 2834.9 us)

commit v2 on v1

--- a/solution.py
+++ b/solution.py
@@ -533,9 +533,11 @@
     up_sum, down_sum = None, None
     if size % 2 == 0:
         farthest = piece_of(size // 2)
-        half = farthest.shape[0] // 2
-        up_half = lax.ppermute(to_low(farthest[:half]), DP, up)
-        down_half = lax.ppermute(to_low(farthest[half:]), DP, down)
+        half = farthest.shape[0] // 2 if not isinstance(farthest, tuple) else 0
+        if half:
+            farthest = (farthest[:half], farthest[half:])
+        up_half = lax.ppermute(to_low(farthest[0]), DP, up)
+        down_half = lax.ppermute(to_low(farthest[1]), DP, down)
         up_sum = jnp.concatenate([to_wide(up_half), jnp.zeros(up_half.shape, jnp.float32)], axis=0)
         down_sum = jnp.concatenate([jnp.zeros(down_half.shape, jnp.float32), to_wide(down_half)], axis=0)
     for step in range(half_count, 0, -1):
@@ -741,6 +743,17 @@
     )
 
 
+def far_pieces(normed_ref, back_ref, hidden_ref, pair_ref, far_refs, share):
+    half, middle = share // 2, normed_ref.shape[1] // share // 2
+    columns = slice(middle * share, (middle + 1) * share)
+    width = pair_ref.shape[1]
+    pair = dot_tn(normed_ref[:, columns], pair_ref[...]).astype(jnp.bfloat16)
+    down = dot_tn(back_ref[:, columns], hidden_ref[...]).astype(jnp.bfloat16)
+    for part, far_ref in enumerate(far_refs):
+        far_ref[:, :width] = pair[part * half : (part + 1) * half]
+        far_ref[:, width:] = down[part * half : (part + 1) * half]
+
+
 def act_columns(start, span, hidden, normed_ref, back_ref, weight_ref, hidden_ref, pair_ref):
     def columns(base):
         return pl.ds(start + base, span)
@@ -770,8 +783,9 @@
         sources = refs[: count + 2 + given]
         outs = refs[count + 2 + given :]
         hidden_ref, pair_ref = outs[:2]
-        total_refs = outs[2 : 4 if earlier is None else 4 + 2 * parts]
-        outs = outs[2 + len(total_refs) :]
+        far_refs = outs[2:4]
+        total_refs = outs[4 : 6 if earlier is None else 6 + 2 * parts]
+        outs = outs[4 + len(total_refs) :]
         weight_ref, normed_ref, back_ref, block_ref = outs[:4]
         sems = outs[-1]
         held = [
@@ -805,6 +819,7 @@
         lax.fori_loop(1, hidden // WIDE, act_wide, 0)
         if hidden % WIDE:
             act(hidden // WIDE * WIDE, hidden % WIDE)
+        far_pieces(normed_ref, back_ref, hidden_ref, pair_ref, far_refs, share)
         finish(held[2:])
         parity = parity_ref[0]
 
@@ -825,7 +840,9 @@
         lax.fori_loop(0, depth // WIDE, one, 0)
 
     low = jnp.bfloat16
+    share = flat[0].shape[0]
     outs = [jax.ShapeDtypeStruct((rows, hidden), low), jax.ShapeDtypeStruct((rows, 2 * hidden), low)]
+    outs += [jax.ShapeDtypeStruct((share // 2, 3 * hidden), low)] * 2
     if earlier is None:
         outs += [jax.ShapeDtypeStruct((rows, depth), low)] * 2
     else:
@@ -841,7 +858,7 @@
         scratch.append(pltpu.VMEM((2, rows, depth), low))
     scratch.append(pltpu.SemaphoreType.DMA((6 * count + 2 + given,)))
     return vmem_call(
-        body, outs, (parity, *flat, normed, back, *(earlier or ())), 48,
+        body, outs, (parity, *flat, normed, back, *(earlier or ())), 50,
         scratch=scratch, anywhere=count + 2 + given,
         flops=2 * rows * depth * hidden * 6, moved=2 * (3 * rows * depth + 3 * depth * hidden + 3 * rows * hidden),
     )
@@ -858,7 +875,8 @@
     ]
 
     def body(*refs):
-        sources, (hidden_ref, pair_ref, weight_ref), (normed_ref, back_ref, sems) = refs[:-6], refs[-6:-3], refs[-3:]
+        sources, (hidden_ref, pair_ref, weight_ref), far_refs = refs[:-8], refs[-8:-5], refs[-5:-3]
+        normed_ref, back_ref, sems = refs[-3:]
         held = [
             pltpu.make_async_copy(sources[count], normed_ref, sems.at[6 * count]),
             pltpu.make_async_copy(sources[count + 1], back_ref, sems.at[6 * count + 1]),
@@ -881,16 +899,19 @@
         lax.fori_loop(1, hidden // WIDE, act_wide, 0)
         if hidden % WIDE:
             act(hidden // WIDE * WIDE, hidden % WIDE)
+        far_pieces(normed_ref, back_ref, hidden_ref, pair_ref, far_refs, share)
 
     low = jnp.bfloat16
+    share = flat[0].shape[0]
     return vmem_call(
         body,
         [
             jax.ShapeDtypeStruct((rows, hidden), low),
             jax.ShapeDtypeStruct((rows, 2 * hidden), low),
             jax.ShapeDtypeStruct((depth, 3 * hidden), low),
-        ],
-        (*flat, normed, back), 36,
+        ]
+        + [jax.ShapeDtypeStruct((share // 2, 3 * hidden), low)] * 2,
+        (*flat, normed, back), 42,
         scratch=[
             pltpu.VMEM((rows, depth), low),
             pltpu.VMEM((rows, depth), low),
@@ -939,7 +960,7 @@
             out_specs=[pl.BlockSpec((height, WIDE), across) for height in heights],
             scratch_shapes=[pltpu.VMEM((rows, WIDE), jnp.float32)],
         ),
-        compiler_params=pltpu.CompilerParams(vmem_limit_bytes=26 * MEBI),
+        compiler_params=pltpu.CompilerParams(vmem_limit_bytes=50 * MEBI),
         cost_estimate=pl.CostEstimate(
             flops=2 * rows * depth * hidden * 3, bytes_accessed=2 * (4 * rows * depth + 3 * depth * hidden), transcendentals=0
         ),
@@ -1203,9 +1224,9 @@
 
     middle = size // 2
 
-    def grads_of(pairs):
+    def grads_of(pairs, far=None):
         span = slice(middle * share, (middle + 1) * share)
-        far = to_low(jnp.concatenate([dot_tn(left[:, span], right) for left, right in pairs], axis=1))
+        far = far or to_low(jnp.concatenate([dot_tn(left[:, span], right) for left, right in pairs], axis=1))
         grads = [to_low(dot_tn(left, right)) for left, right in pairs]
 
         def piece_of(index):
@@ -1218,11 +1239,11 @@
     partial, feed_grads = None, []
     for pieces in feed_pieces:
         if partial is None:
-            hidden, pair, *partial = feed_call(normed_two, back_low, pieces, parity, None, 2)
+            hidden, pair, far_up, far_down, *partial = feed_call(normed_two, back_low, pieces, parity, None, 2)
         else:
-            hidden, pair, weight = act_call(normed_two, back_low, pieces)
+            hidden, pair, weight, far_up, far_down = act_call(normed_two, back_low, pieces)
             partial = back_call(hidden, pair, weight, parity, partial, 2)
-        piece_of = grads_of([(normed_two, pair), (back_low, hidden)])
+        piece_of = grads_of([(normed_two, pair), (back_low, hidden)], (far_up, far_down))
         feed_grads += ring_scatter(piece_of, order)
 
     sums, _ = exchange(partial[:2], partial[2:4])

time: 758 us -> 759 us (level)
  Pallas kernels: 166 us -> 176 us
    ppermute x9, waiting for transfers between devices: 98.7 us -> 158 us  [ring_gather(): from_low = lax.ppermute(from_low, DP, up)]
    ppermute x9, waiting for transfers between devices: 59.3 us -> 5.62 us  [ring_gather(): from_high = lax.ppermute(from_high, DP, down)]
    ppermute x6, waiting for transfers between devices: 2.88 us -> 12.7 us  [the longest x3 11.5 us: ring_scatter(): down_half = lax.ppermute(to_low(farthest[1]), DP, down)]
    ppermute x9, starting transfers between devices: 13.7 us -> 5.22 us  [ring_gather(): from_high = lax.ppermute(from_high, DP, down)]
    ppermute x9, starting transfers between devices: 7.8 us -> 15.7 us  [ring_gather(): from_low = lax.ppermute(from_low, DP, up)]
    unnamed x184 -> x156, local copies, waits for them, and re-layouts: 33.6 us -> 27.2 us
    dot_general x12 -> x8, matrix products: 44.3 us -> 39.2 us  [dot_tn(): lax.dot_general(left, right, (((0,), (0,)), ((), ())), preferred_element_...]
  transfers between devices with their start and end apart: 74 -> 74, of which waited for: 29 -> 30; matrix products, arithmetic and copies ran while one was open for 13% -> 12% of each run, Pallas kernels for 18% -> 19%
where the time goes in v2:
time: 759 us; the launch traced here: 749 us
  waiting for transfers between devices  383 us (50%)
  Pallas kernels  176 us (23%)
  starting transfers between devices  68.3 us (9%)
  local copies, waits for them, and re-layouts  49.1 us (6%)
  matrix products  39.2 us (5%)
  other arithmetic  30.1 us (4%)
    ppermute x9, waiting for transfers between devices, ring_gather(): from_low = lax.ppermute(from_low, DP, up)  158 us
    ppermute x9, waiting for transfers between devices, ring_scatter(): down_sum = to_wide(lax.ppermute(to_low(down_piece), DP, down))  98.4 us
    pallas_call x7, Pallas kernels, vmem_call(): pl.pallas_call(body, out_shape=out_shape, in_specs=spaces, out_specs=[pl....  87.1 us
    ppermute x7, waiting for transfers between devices, exchange(): lax.ppermute(own, HEAD, far)  56 us
    dot_general x8, matrix products, dot_tn(): lax.dot_general(left, right, (((0,), (0,)), ((), ())), preferred_element_...  39.2 us
    pallas_call x4, Pallas kernels, row_call(): pl.pallas_call(body, out_shape=[jax.ShapeDtypeStruct((rows, depth), kind)...  34.1 us
    ppermute x5, waiting for transfers between devices, total_sum(): lax.ppermute(values, axis, [(i, i ^ step) for i in range(count)])  29.4 us
    unnamed x156, local copies, waits for them, and re-layouts  27.2 us
  transfers between devices with their start and end apart: 74, of which 30 were waited for; matrix products, arithmetic and copies ran while one was open for 12% of the time, Pallas kernels for 19%

profile of v2, /device:TPU:0, one launch (start us, length us, event | category | flops | bytes accessed | tf_op | source)
XLA Modules:
  0.0 748.5 jit_solution(8462641666255320310)
XLA Ops:
  9.6 24.5 %collective-permute-done.refs_8_ = bf16[256,2176]{1,0:T(8,128)(2,1)S(1)} collective-permute-done((bf16[256,2176]{1,0:T(8,128)(2,1)S(1)}, bf16[256,2176]{1,0:T(8,128)(2,1)S(1)}, u32[]{:S(2)}, u32[]{:S(2)}) %collective-permute-start) | collective-permute-done | bytes 1114144 | tf_op jit(solution)/shard_map/ppermute | solution.py:518
  38.1 21.8 %collective-permute-done.1.refs_7_ = bf16[256,2176]{1,0:T(8,128)(2,1)} collective-permute-done((bf16[256,2176]{1,0:T(8,128)(2,1)S(1)}, bf16[256,2176]{1,0:T(8,128)(2,1)}, u32[]{:S(2)}, u32[]{:S(2)}) %collective-permute-start.1) | collective-permute-done | bytes 1114144 | tf_op jit(solution)/shard_map/ppermute | solution.py:518
  71.5 13.5 %collective-permute-done.2.refs_6_ = bf16[256,2176]{1,0:T(8,128)(2,1)S(1)} collective-permute-done((bf16[256,2176]{1,0:T(8,128)(2,1)}, bf16[256,2176]{1,0:T(8,128)(2,1)S(1)}, u32[]{:S(2)}, u32[]{:S(2)}) %collective-permute-start.2) | collective-permute-done | bytes 1114144 | tf_op jit(solution)/shard_map/ppermute | solution.py:518
  106.7 11.9 %shard_map.257 = (bf16[1024,1536]{1,0:T(8,128)(2,1)S(1)}, f32[8,64,128]{2,1,0:T(8,128)S(1)}, bf16[1024,2048]{1,0:T(8,128)(2,1)S(1)}, f32[8,2048]{1,0:T(8,128)S(1)}) custom-call(bf16[1024,2048]{1,0:T(8,128)(2,1)S(1)} %copy-done.1, f32[1024,1]{1,0:T(8,128)S(1)} %copy-done.32, bf16[256,2176]{1,0:T(8,128)(2,1)S(1)} %concatenate.111.refs_0_.refs_3_, ...), custom_call_target="tpu_custom_call" | custom-call | flops 6979321856 | bytes 14417920 | tf_op jit(solution)/shard_map/pallas_call | solution.py:606
  120.6 12.9 %mixer_forward.1 = (bf16[1024,512]{1,0:T(8,128)(2,1)S(1)}, f32[8,128,1024]{2,1,0:T(8,128)S(1)}, f32[8,64,128]{2,1,0:T(8,128)S(1)}, f32[8,64,128]{2,1,0:T(8,128)S(1)}, bf16[8,128,128]{2,1,0:T(8,128)(2,1)S(1)}) custom-call(s32[1]{0:T(128)S(6)} %copy.62.length_ref, bf16[1024,1536]{1,0:T(8,128)(2,1)S(1)} %get-tuple-element.73.qkv_ref, ...), custom_call_target="tpu_custom_call" | custom-call | tf_op jit(solution)/shard_map/mixer_forward/pallas_call | solution.py:436
  135.6 6.4 shard_map.258
  146.2 20.8 %collective-permute-done.11.refs_8_ = bf16[256,1920]{1,0:T(8,128)(2,1)S(1)} collective-permute-done((bf16[256,1920]{1,0:T(8,128)(2,1)S(1)}, bf16[256,1920]{1,0:T(8,128)(2,1)S(1)}, u32[]{:S(2)}, u32[]{:S(2)}) %collective-permute-start.11) | collective-permute-done | bytes 983072 | tf_op jit(solution)/shard_map/ppermute | solution.py:518
  172.2 20.1 %collective-permute-done.25.refs_8_ = bf16[256,2304]{1,0:T(8,128)(2,1)S(1)} collective-permute-done((bf16[256,2304]{1,0:T(8,128)(2,1)S(1)}, bf16[256,2304]{1,0:T(8,128)(2,1)S(1)}, u32[]{:S(2)}, u32[]{:S(2)}) %collective-permute-start.25) | collective-permute-done | bytes 1179680 | tf_op jit(solution)/shard_map/ppermute | solution.py:518
  197.4 15.9 %collective-permute-done.12.refs_7_ = bf16[256,1920]{1,0:T(8,128)(2,1)S(1)} collective-permute-done((bf16[256,1920]{1,0:T(8,128)(2,1)S(1)}, bf16[256,1920]{1,0:T(8,128)(2,1)S(1)}, u32[]{:S(2)}, u32[]{:S(2)}) %collective-permute-start.12) | collective-permute-done | bytes 983072 | tf_op jit(solution)/shard_map/ppermute | solution.py:518
  218.1 41.1 %collective-permute-done.13.refs_6_ = bf16[256,1920]{1,0:T(8,128)(2,1)S(1)} collective-permute-done((bf16[256,1920]{1,0:T(8,128)(2,1)S(1)}, bf16[256,1920]{1,0:T(8,128)(2,1)S(1)}, u32[]{:S(2)}, u32[]{:S(2)}) %collective-permute-start.13) | collective-permute-done | bytes 983072 | tf_op jit(solution)/shard_map/ppermute | solution.py:518
  277.2 19.0 %shard_map.260 = (bf16[1024,640]{1,0:T(8,128)(2,1)S(1)}, bf16[1024,1280]{1,0:T(8,128)(2,1)}, bf16[2048,1920]{1,0:T(8,128)(2,1)}, bf16[128,1920]{1,0:T(8,128)(2,1)S(1)}, bf16[128,1920]{1,0:T(8,128)(2,1)S(1)}) custom-call(bf16[256,1920]{1,0:T(8,128)(2,1)S(1)} %pad_maximum_fusion.3.refs_0_, bf16[256,1920]{1,0:T(8,128)(2,1)S(1)} %collective-permute-done.8.refs_1_, ...), custom_call_target="tpu_custom_call" | custom-call | flops 8053063680 | bytes 28049408 | tf_op jit(solution)/shard_map/pallas_call | solution.py:606
  296.2 8.2 %convolution_convert_fusion = bf16[2048,1280]{1,0:T(8,128)(2,1)S(1)} fusion(bf16[1024,2048]{1,0:T(8,128)(2,1)S(1)} %copy-done.41, bf16[1024,1280]{1,0:T(8,128)(2,1)} %get-tuple-element.83.pair_ref), kind=kOutput, calls=%fused_computation.2 | convolution fusion | flops 5371330560 | bytes 12058624 | tf_op jit(solution)/shard_map/dot_general | solution.py:496
  322.5 9.7 %collective-permute-done.28.refs_4_ = bf16[128,2304]{1,0:T(8,128)(2,1)S(1)} collective-permute-done((bf16[128,2304]{1,0:T(8,128)(2,1)S(1)}, bf16[128,2304]{1,0:T(8,128)(2,1)S(1)}, u32[]{:S(2)}, u32[]{:S(2)}) %collective-permute-start.28) | collective-permute-done | bytes 589856 | tf_op jit(solution)/shard_map/ppermute | solution.py:523
  333.1 31.2 %shard_map.261 = (bf16[1024,768]{1,0:T(8,128)(2,1)}, bf16[1024,1536]{1,0:T(8,128)(2,1)}, bf16[128,2304]{1,0:T(8,128)(2,1)S(1)}, bf16[128,2304]{1,0:T(8,128)(2,1)...) custom-call(s32[1]{0:T(128)} %bitcast.parity_ref, bf16[256,2304]{1,0:T(8,128)(2,1)S(1)} %copy-done.21, ...), custom_call_target="tpu_custom_call" | custom-call | flops 19327352832 | bytes 26738688 | tf_op jit(solution)/shard_map/pallas_call | solution.py:606
  365.9 17.1 %shard_map.262 = (bf16[256,2048]{1,0:T(8,128)(2,1)S(1)}, bf16[256,2048]{1,0:T(8,128)(2,1)S(1)}, bf16[256,2048]{1,0:T(8,128)(2,1)S(1)}, bf16[256,2048]{1,0:T(8,12...) custom-call(s32[1]{0:T(128)} %bitcast.parity_ref, bf16[1024,640]{1,0:T(8,128)(2,1)} %copy-done.49, ...), custom_call_target="tpu_custom_call" | custom-call | flops 8053063680 | bytes 24641536 | tf_op jit(solution)/shard_map/pallas_call | solution.py:947
  383.1 9.6 %convolution_convert_fusion.1 = bf16[2048,1536]{1,0:T(8,128)(2,1)S(1)} fusion(bf16[1024,2048]{1,0:T(8,128)(2,1)S(1)} %copy-done.42, bf16[1024,1536]{1,0:T(8,128)(2,1)} %get-tuple-element.111), kind=kOutput, calls=%fused_computation.3 | convolution fusion | flops 6445596672 | bytes 13631488 | tf_op jit(solution)/shard_map/dot_general | solution.py:496
  400.8 11.5 %collective-permute-done.57 = bf16[128,2304]{1,0:T(8,128)(2,1)S(1)} collective-permute-done((bf16[128,2304]{1,0:T(8,128)(2,1)S(1)}, bf16[128,2304]{1,0:T(8,128)(2,1)S(1)}, u32[]{:S(2)}, u32[]{:S(2)}) %collective-permute-start.57) | collective-permute-done | bytes 589856 | tf_op jit(solution)/shard_map/ppermute | solution.py:540
  422.0 41.4 %collective-permute-done.67 = bf16[256,1920]{1,0:T(8,128)(2,1)S(1)} collective-permute-done((bf16[256,1920]{1,0:T(8,128)(2,1)S(1)}, bf16[256,1920]{1,0:T(8,128)(2,1)S(1)}, u32[]{:S(2)}, u32[]{:S(2)}) %collective-permute-start.67) | collective-permute-done | bytes 983072 | tf_op jit(solution)/shard_map/ppermute | solution.py:548
  470.7 18.7 %collective-permute-done.36 = bf16[256,2048]{1,0:T(8,128)(2,1)S(1)} collective-permute-done((bf16[256,2048]{1,0:T(8,128)(2,1)S(1)}, bf16[256,2048]{1,0:T(8,128)(2,1)S(1)}, u32[]{:S(2)}, u32[]{:S(2)}) %collective-permute-start.36) | collective-permute-done | bytes 1048608 | tf_op jit(solution)/shard_map/ppermute | solution.py:1166
  489.9 20.7 %collective-permute-done.33 = bf16[256,2048]{1,0:T(8,128)(2,1)S(1)} collective-permute-done((bf16[256,2048]{1,0:T(8,128)(2,1)S(1)}, bf16[256,2048]{1,0:T(8,128)(2,1)S(1)}, u32[]{:S(2)}, u32[]{:S(2)}) %collective-permute-start.33) | collective-permute-done | bytes 1048608 | tf_op jit(solution)/shard_map/ppermute | solution.py:1166
  516.8 9.0 %shard_map.263 = (bf16[1024,2048]{1,0:T(8,128)(2,1)S(1)}, bf16[1024,512]{1,0:T(8,128)(2,1)S(1)}) custom-call(s32[9]{0:T(128)S(1)} %pad_add_fusion.scalar_ref, bf16[256,2048]{1,0:T(8,128)(2,1)S(1)} %add_convert_fusion.20.refs_0_, bf16[256,2048]{1,0:T(8,128)(2,1)S(1)} %collective-permute-done.34.refs_1_, bf16[256,2048]{1,0:T(8,128)(2,1)S(1)} %add_convert_fusion.18.refs_2_, ...), custom_call_target="tpu_custom_call" | custom-call | flops 20971520 | bytes 16777216 | tf_op jit(solution)/shard_map/pallas_call | solution.py:1006
  525.9 20.3 %mixer_backward.1 = (bf16[1024,1664]{1,0:T(8,128)(2,1)S(1)}, f32[64,128]{1,0:T(8,128)S(1)}) custom-call(s32[1]{0:T(128)S(6)} %copy.62.length_ref, bf16[1024,1536]{1,0:T(8,128)(2,1)S(1)} %copy-done.9, f32[8,64,128]{2,1,0:T(8,128)S(1)} %get-tuple-element.74.logit_ref, f32[64,1]{1,0:T(8,128)S(1)} %copy.47.bias_ref, ...), custom_call_target="tpu_custom_call" | custom-call | tf_op jit(solution)/shard_map/mixer_backward/pallas_call | solution.py:463
  547.3 9.9 %convolution_convert_fusion.2 = bf16[2048,1664]{1,0:T(8,128)(2,1)} fusion(bf16[1024,2048]{1,0:T(8,128)(2,1)S(1)} %copy-done.48, bf16[1024,1664]{1,0:T(8,128)(2,1)S(1)} %get-tuple-element.101.left_ref), kind=kOutput, calls=%fused_computation.4 | convolution fusion | flops 6982729728 | bytes 14417920 | tf_op jit(solution)/shard_map/dot_general | solution.py:496
  563.2 12.1 %shard_map.264 = (bf16[256,2048]{1,0:T(8,128)(2,1)S(1)}, bf16[256,2048]{1,0:T(8,128)(2,1)S(1)}, bf16[256,2048]{1,0:T(8,128)(2,1)S(1)}, bf16[256,2048]{1,0:T(8,128)(2,1)S(1)}) custom-call(s32[1]{0:T(128)} %bitcast.parity_ref, bf16[1024,1664]{1,0:T(8,128)(2,1)S(1)} %get-tuple-element.101.left_ref, bf16[256,2176]{1,0:T(8,128)(2,1)S(1)} %concatenate.111.refs_0_.refs_3_, ...), custom_call_target="tpu_custom_call" | custom-call | flops 6979321856 | bytes 14417920 | tf_op jit(solution)/shard_map/pallas_call | solution.py:606
  580.5 10.7 %collective-permute-done.72 = f32[64]{0:T(128)S(1)} collective-permute-done((f32[64]{0:T(128)S(1)}, f32[64]{0:T(128)S(1)}, u32[]{:S(2)}, u32[]{:S(2)}) %collective-permute-start.72) | collective-permute-done | bytes 288 | tf_op jit(solution)/shard_map/ppermute | solution.py:556
  602.2 37.0 %collective-permute-done.50 = bf16[256,2176]{1,0:T(8,128)(2,1)S(1)} collective-permute-done((bf16[256,2176]{1,0:T(8,128)(2,1)S(1)}, bf16[256,2176]{1,0:T(8,128)(2,1)S(1)}, u32[]{:S(2)}, u32[]{:S(2)}) %collective-permute-start.50) | collective-permute-done | bytes 1114144 | tf_op jit(solution)/shard_map/ppermute | solution.py:548
  646.6 16.6 %collective-permute-done.41 = bf16[256,2048]{1,0:T(8,128)(2,1)S(1)} collective-permute-done((bf16[256,2048]{1,0:T(8,128)(2,1)S(1)}, bf16[256,2048]{1,0:T(8,128)(2,1)S(1)}, u32[]{:S(2)}, u32[]{:S(2)}) %collective-permute-start.41) | collective-permute-done | bytes 1048608 | tf_op jit(solution)/shard_map/ppermute | solution.py:1166
  665.4 4.9 collective-permute-done.51
  676.7 18.6 %collective-permute-done.73 = f32[64]{0:T(128)S(1)} collective-permute-done((f32[64]{0:T(128)S(1)}, f32[64]{0:T(128)S(1)}, u32[]{:S(2)}, u32[]{:S(2)}) %collective-permute-start.73) | collective-permute-done | bytes 288 | tf_op jit(solution)/shard_map/ppermute | solution.py:556
  703.1 15.1 %collective-permute-done.52.refs_2_ = bf16[256,2176]{1,0:T(8,128)(2,1)} collective-permute-done((bf16[256,2176]{1,0:T(8,128)(2,1)}, bf16[256,2176]{1,0:T(8,128)(2,1)}, u32[]{:S(2)}, u32[]{:S(2)}) %collective-permute-start.52) | collective-permute-done | bytes 1114144 | tf_op jit(solution)/shard_map/ppermute | solution.py:548
  725.7 7.8 %shard_map.265 = bf16[1024,2048]{1,0:T(8,128)(2,1)} custom-call(s32[9]{0:T(128)S(1)} %pad_add_fusion.scalar_ref, bf16[512,2048]{1,0:T(8,128)(2,1)} %add_convert_fusion.refs_0_, bf16[512,2048]{1,0:T(8,128)(2,1)} %collective-permute-done.40.refs_1_, bf16[1024,2048]{1,0:T(8,128)(2,1)S(1)} %copy-done.4), custom_call_target="tpu_custom_call" | custom-call | flops 20971520 | bytes 12582912 | tf_op jit(solution)/shard_map/pallas_call | solution.py:1006
  734.1 12.8 %shard_map.266 = f32[1024,2048]{1,0:T(8,128)} custom-call(s32[9]{0:T(128)} %copy-done.39, bf16[256,2048]{1,0:T(8,128)(2,1)} %add_convert_fusion.15.refs_0_, bf16[256,2048]{1,0:T(8,128)(2,1)} %collective-permute-done.42.refs_1_, bf16[256,2048]{1,0:T(8,128)(2,1)} %add_convert_fusion.14.refs_2_, bf16[256,2048]{1,0:T(8,128)(2,1)} %collective-permute-done.44.refs_3_, ...), custom_call_target="tpu_custom_call" | custom-call | flops 20971520 | bytes 20971520 | tf_op jit(solution)/shard_map/pallas_call | solution.py:1006
  (381 shorter events, 194.8 us)
Async XLA Ops:
  144.6 47.7 %collective-permute-start.25 = (bf16[256,2304]{1,0:T(8,128)(2,1)S(1)}, bf16[256,2304]{1,0:T(8,128)(2,1)S(1)}, u32[]{:S(2)}, u32[]{:S(2)}) collective-permute-start(bf16[256,2304]{1,0:T(8,128)(2,1)S(1)} %pad_maximum_fusion.refs_0_), channel_id=1, source_target_pairs={{0,8},{8,16},{16,24},{24,28},{28,20},{20,12},{12,4},{4,0},{1,9},{9... | collective-permute-start | bytes 3538952 | tf_op jit(solution)/shard_map/ppermute | solution.py:518
  168.0 45.3 %collective-permute-start.12 = (bf16[256,1920]{1,0:T(8,128)(2,1)S(1)}, bf16[256,1920]{1,0:T(8,128)(2,1)S(1)}, u32[]{:S(2)}, u32[]{:S(2)}) collective-permute-start(bf16[256,1920]{1,0:T(8,128)(2,1)S(1)} %collective-permute-done.11.refs_8_), channel_id=1, source_target_pairs={{0,8},{8,16},{16,24},{24,28},{28,20},{20,12},{12,4},{4,0},{1,9},{9... | collective-permute-start | bytes 2949128 | tf_op jit(solution)/shard_map/ppermute | solution.py:518
  169.4 45.7 %collective-permute-start.9 = (bf16[256,1920]{1,0:T(8,128)(2,1)S(1)}, bf16[256,1920]{1,0:T(8,128)(2,1)S(1)}, u32[]{:S(2)}, u32[]{:S(2)}) collective-permute-start(bf16[256,1920]{1,0:T(8,128)(2,1)S(1)} %collective-permute-done.8.refs_1_), channel_id=1, source_target_pairs={{0,4},{8,0},{16,8},{24,16},{28,24},{20,28},{12,20},{4,12},{1,5},{9... | collective-permute-start | bytes 2949128 | tf_op jit(solution)/shard_map/ppermute | solution.py:519
  170.4 46.2 %collective-permute-start.20 = (bf16[256,2048]{1,0:T(8,128)(2,1)S(1)}, bf16[256,2048]{1,0:T(8,128)(2,1)S(1)}, u32[]{:S(2)}, u32[]{:S(2)}) collective-permute-start(bf16[256,2048]{1,0:T(8,128)(2,1)S(1)} %add_convert_fusion.23), channel_id=1, source_target_pairs={{0,2},{1,3},{2,0},{3,1},{4,6},{5,7},{6,4},{7,5},{8,10},{9,11},{10,... | collective-permute-start | bytes 3145736 | tf_op jit(solution)/shard_map/ppermute | solution.py:1166
  195.8 67.2 %collective-permute-start.26 = (bf16[256,2304]{1,0:T(8,128)(2,1)S(1)}, bf16[256,2304]{1,0:T(8,128)(2,1)}, u32[]{:S(2)}, u32[]{:S(2)}) collective-permute-start(bf16[256,2304]{1,0:T(8,128)(2,1)S(1)} %collective-permute-done.25.refs_8_), channel_id=1, source_target_pairs={{0,8},{8,16},{16,24},{24,28},{28,20},{20,12},{12,4},{4,0},{1,9},{9... | collective-permute-start | bytes 3538952 | tf_op jit(solution)/shard_map/ppermute | solution.py:518
  213.3 50.9 %collective-permute-start.23 = (bf16[256,2304]{1,0:T(8,128)(2,1)S(1)}, bf16[256,2304]{1,0:T(8,128)(2,1)}, u32[]{:S(2)}, u32[]{:S(2)}) collective-permute-start(bf16[256,2304]{1,0:T(8,128)(2,1)S(1)} %collective-permute-done.22.refs_1_), channel_id=1, source_target_pairs={{0,4},{8,0},{16,8},{24,16},{28,24},{20,28},{12,20},{4,12},{1,5},{9... | collective-permute-start | bytes 3538952 | tf_op jit(solution)/shard_map/ppermute | solution.py:519
  215.1 44.1 %collective-permute-start.13 = (bf16[256,1920]{1,0:T(8,128)(2,1)S(1)}, bf16[256,1920]{1,0:T(8,128)(2,1)S(1)}, u32[]{:S(2)}, u32[]{:S(2)}) collective-permute-start(bf16[256,1920]{1,0:T(8,128)(2,1)S(1)} %collective-permute-done.12.refs_7_), channel_id=1, source_target_pairs={{0,8},{8,16},{16,24},{24,28},{28,20},{20,12},{12,4},{4,0},{1,9},{9... | collective-permute-start | bytes 2949128 | tf_op jit(solution)/shard_map/ppermute | solution.py:518
  216.6 44.8 %collective-permute-start.10 = (bf16[256,1920]{1,0:T(8,128)(2,1)S(1)}, bf16[256,1920]{1,0:T(8,128)(2,1)S(1)}, u32[]{:S(2)}, u32[]{:S(2)}) collective-permute-start(bf16[256,1920]{1,0:T(8,128)(2,1)S(1)} %collective-permute-done.9.refs_2_), channel_id=1, source_target_pairs={{0,4},{8,0},{16,8},{24,16},{28,24},{20,28},{12,20},{4,12},{1,5},{9... | collective-permute-start | bytes 2949128 | tf_op jit(solution)/shard_map/ppermute | solution.py:519
  217.5 48.3 %collective-permute-start.21 = (bf16[256,2048]{1,0:T(8,128)(2,1)S(1)}, bf16[256,2048]{1,0:T(8,128)(2,1)S(1)}, u32[]{:S(2)}, u32[]{:S(2)}) collective-permute-start(bf16[256,2048]{1,0:T(8,128)(2,1)S(1)} %add_convert_fusion.22.refs_2_), channel_id=1, source_target_pairs={{0,1},{1,0},{2,3},{3,2},{4,5},{5,4},{6,7},{7,6},{8,9},{9,8},{10,11... | collective-permute-start | bytes 3145736 | tf_op jit(solution)/shard_map/ppermute | solution.py:1167
  264.2 48.7 %collective-permute-start.27 = (bf16[256,2304]{1,0:T(8,128)(2,1)}, bf16[256,2304]{1,0:T(8,128)(2,1)}, u32[]{:S(2)}, u32[]{:S(2)}) collective-permute-start(bf16[256,2304]{1,0:T(8,128)(2,1)} %collective-permute-done.26.refs_7_), channel_id=1, source_target_pairs={{0,8},{8,16},{16,24},{24,28},{28,20},{20,12},{12,4},{4,0},{1,9},{9... | collective-permute-start | bytes 3538952 | tf_op jit(solution)/shard_map/ppermute | solution.py:518
  265.8 49.9 %collective-permute-start.24 = (bf16[256,2304]{1,0:T(8,128)(2,1)}, bf16[256,2304]{1,0:T(8,128)(2,1)}, u32[]{:S(2)}, u32[]{:S(2)}) collective-permute-start(bf16[256,2304]{1,0:T(8,128)(2,1)} %collective-permute-done.23.refs_2_), channel_id=1, source_target_pairs={{0,4},{8,0},{16,8},{24,16},{28,24},{20,28},{12,20},{4,12},{1,5},{9... | collective-permute-start | bytes 3538952 | tf_op jit(solution)/shard_map/ppermute | solution.py:519
  319.5 94.4 %collective-permute-start.66 = (bf16[256,1920]{1,0:T(8,128)(2,1)}, bf16[256,1920]{1,0:T(8,128)(2,1)}, u32[]{:S(2)}, u32[]{:S(2)}) collective-permute-start(bf16[256,1920]{1,0:T(8,128)(2,1)} %add_convert_fusion.28), channel_id=1, source_target_pairs={{0,4},{8,0},{16,8},{24,16},{28,24},{20,28},{12,20},{4,12},{1,5},{9... | collective-permute-start | bytes 2949128 | tf_op jit(solution)/shard_map/ppermute | solution.py:548
  321.0 95.1 %collective-permute-start.62 = (bf16[256,1920]{1,0:T(8,128)(2,1)}, bf16[256,1920]{1,0:T(8,128)(2,1)}, u32[]{:S(2)}, u32[]{:S(2)}) collective-permute-start(bf16[256,1920]{1,0:T(8,128)(2,1)} %add_convert_fusion.31), channel_id=1, source_target_pairs={{0,8},{8,16},{16,24},{24,28},{28,20},{20,12},{12,4},{4,0},{1,9},{9... | collective-permute-start | bytes 2949128 | tf_op jit(solution)/shard_map/ppermute | solution.py:547
  413.7 97.4 %collective-permute-start.30 = (bf16[512,2048]{1,0:T(8,128)(2,1)S(1)}, bf16[512,2048]{1,0:T(8,128)(2,1)S(1)}, u32[]{:S(2)}, u32[]{:S(2)}) collective-permute-start(bf16[512,2048]{1,0:T(8,128)(2,1)S(1)} %copy-done.71), channel_id=1, source_target_pairs={{0,1},{1,0},{2,3},{3,2},{4,5},{5,4},{6,7},{7,6},{8,9},{9,8},{10,11... | collective-permute-start | bytes 6291464 | tf_op jit(solution)/shard_map/ppermute | solution.py:1164
  413.9 54.1 %collective-permute-start.58 = (bf16[256,2304]{1,0:T(8,128)(2,1)S(1)}, bf16[256,2304]{1,0:T(8,128)(2,1)S(1)}, u32[]{:S(2)}, u32[]{:S(2)}) collective-permute-start(bf16[256,2304]{1,0:T(8,128)(2,1)S(1)} %add_convert_fusion.4), channel_id=1, source_target_pairs={{0,4},{8,0},{16,8},{24,16},{28,24},{20,28},{12,20},{4,12},{1,5},{9... | collective-permute-start | bytes 3538952 | tf_op jit(solution)/shard_map/ppermute | solution.py:548
  416.1 53.8 %collective-permute-start.54 = (bf16[256,2304]{1,0:T(8,128)(2,1)S(1)}, bf16[256,2304]{1,0:T(8,128)(2,1)S(1)}, u32[]{:S(2)}, u32[]{:S(2)}) collective-permute-start(bf16[256,2304]{1,0:T(8,128)(2,1)S(1)} %add_convert_fusion.7), channel_id=1, source_target_pairs={{0,8},{8,16},{16,24},{24,28},{28,20},{20,12},{12,4},{4,0},{1,9},{9... | collective-permute-start | bytes 3538952 | tf_op jit(solution)/shard_map/ppermute | solution.py:547
  419.0 44.4 %collective-permute-start.67 = (bf16[256,1920]{1,0:T(8,128)(2,1)S(1)}, bf16[256,1920]{1,0:T(8,128)(2,1)S(1)}, u32[]{:S(2)}, u32[]{:S(2)}) collective-permute-start(bf16[256,1920]{1,0:T(8,128)(2,1)S(1)} %add_convert_fusion.27), channel_id=1, source_target_pairs={{0,4},{8,0},{16,8},{24,16},{28,24},{20,28},{12,20},{4,12},{1,5},{9... | collective-permute-start | bytes 2949128 | tf_op jit(solution)/shard_map/ppermute | solution.py:548
  420.2 46.0 %collective-permute-start.63 = (bf16[256,1920]{1,0:T(8,128)(2,1)S(1)}, bf16[256,1920]{1,0:T(8,128)(2,1)S(1)}, u32[]{:S(2)}, u32[]{:S(2)}) collective-permute-start(bf16[256,1920]{1,0:T(8,128)(2,1)S(1)} %add_convert_fusion.30), channel_id=1, source_target_pairs={{0,8},{8,16},{16,24},{24,28},{28,20},{20,12},{12,4},{4,0},{1,9},{9... | collective-permute-start | bytes 2949128 | tf_op jit(solution)/shard_map/ppermute | solution.py:547
  466.1 44.4 %collective-permute-start.33 = (bf16[256,2048]{1,0:T(8,128)(2,1)S(1)}, bf16[256,2048]{1,0:T(8,128)(2,1)S(1)}, u32[]{:S(2)}, u32[]{:S(2)}) collective-permute-start(bf16[256,2048]{1,0:T(8,128)(2,1)S(1)} %add_convert_fusion.21), channel_id=1, source_target_pairs={{0,2},{1,3},{2,0},{3,1},{4,6},{5,7},{6,4},{7,5},{8,10},{9,11},{10,... | collective-permute-start | bytes 3145736 | tf_op jit(solution)/shard_map/ppermute | solution.py:1166
  468.3 45.2 %collective-permute-start.59 = (bf16[256,2304]{1,0:T(8,128)(2,1)S(1)}, bf16[256,2304]{1,0:T(8,128)(2,1)S(1)}, u32[]{:S(2)}, u32[]{:S(2)}) collective-permute-start(bf16[256,2304]{1,0:T(8,128)(2,1)S(1)} %add_convert_fusion.3), channel_id=1, source_target_pairs={{0,4},{8,0},{16,8},{24,16},{28,24},{20,28},{12,20},{4,12},{1,5},{9... | collective-permute-start | bytes 3538952 | tf_op jit(solution)/shard_map/ppermute | solution.py:548
  470.3 44.5 %collective-permute-start.55 = (bf16[256,2304]{1,0:T(8,128)(2,1)S(1)}, bf16[256,2304]{1,0:T(8,128)(2,1)S(1)}, u32[]{:S(2)}, u32[]{:S(2)}) collective-permute-start(bf16[256,2304]{1,0:T(8,128)(2,1)S(1)} %add_convert_fusion.6), channel_id=1, source_target_pairs={{0,8},{8,16},{16,24},{24,28},{28,20},{20,12},{12,4},{4,0},{1,9},{9... | collective-permute-start | bytes 3538952 | tf_op jit(solution)/shard_map/ppermute | solution.py:547
  511.9 86.0 %collective-permute-start.31 = (bf16[512,2048]{1,0:T(8,128)(2,1)S(1)}, bf16[512,2048]{1,0:T(8,128)(2,1)}, u32[]{:S(2)}, u32[]{:S(2)}) collective-permute-start(bf16[512,2048]{1,0:T(8,128)(2,1)S(1)} %add_convert_fusion.1), channel_id=1, source_target_pairs={{0,2},{1,3},{2,0},{3,1},{4,6},{5,7},{6,4},{7,5},{8,10},{9,11},{10,... | collective-permute-start | bytes 6291464 | tf_op jit(solution)/shard_map/ppermute | solution.py:1166
  558.6 36.0 %collective-permute-start.49 = (bf16[128,2176]{1,0:T(8,128)(2,1)S(1)}, bf16[128,2176]{1,0:T(8,128)(2,1)S(1)}, u32[]{:S(2)}, u32[]{:S(2)}) collective-permute-start(bf16[128,2176]{1,0:T(8,128)(2,1)S(1)} %get-tuple-element.195), channel_id=1, source_target_pairs={{0,4},{8,0},{16,8},{24,16},{28,24},{20,28},{12,20},{4,12},{1,5},{9... | collective-permute-start | bytes 1671176 | tf_op jit(solution)/shard_map/ppermute | solution.py:540
  591.3 80.6 %collective-permute-start.68 = (bf16[256,1920]{1,0:T(8,128)(2,1)S(1)}, bf16[256,1920]{1,0:T(8,128)(2,1)S(1)}, u32[]{:S(2)}, u32[]{:S(2)}) collective-permute-start(bf16[256,1920]{1,0:T(8,128)(2,1)S(1)} %copy-done.67), channel_id=1, source_target_pairs={{0,4},{8,0},{16,8},{24,16},{28,24},{20,28},{12,20},{4,12},{1,5},{9... | collective-permute-start | bytes 2949128 | tf_op jit(solution)/shard_map/ppermute | solution.py:548
  594.7 80.1 %collective-permute-start.64 = (bf16[256,1920]{1,0:T(8,128)(2,1)S(1)}, bf16[256,1920]{1,0:T(8,128)(2,1)S(1)}, u32[]{:S(2)}, u32[]{:S(2)}) collective-permute-start(bf16[256,1920]{1,0:T(8,128)(2,1)S(1)} %copy-done.66), channel_id=1, source_target_pairs={{0,8},{8,16},{16,24},{24,28},{28,20},{20,12},{12,4},{4,0},{1,9},{9... | collective-permute-start | bytes 2949128 | tf_op jit(solution)/shard_map/ppermute | solution.py:547
  595.0 44.2 %collective-permute-start.50 = (bf16[256,2176]{1,0:T(8,128)(2,1)S(1)}, bf16[256,2176]{1,0:T(8,128)(2,1)S(1)}, u32[]{:S(2)}, u32[]{:S(2)}) collective-permute-start(bf16[256,2176]{1,0:T(8,128)(2,1)S(1)} %add_convert_fusion.10), channel_id=1, source_target_pairs={{0,4},{8,0},{16,8},{24,16},{28,24},{20,28},{12,20},{4,12},{1,5},{9... | collective-permute-start | bytes 3342344 | tf_op jit(solution)/shard_map/ppermute | solution.py:548
  597.4 45.4 %collective-permute-start.46 = (bf16[256,2176]{1,0:T(8,128)(2,1)S(1)}, bf16[256,2176]{1,0:T(8,128)(2,1)S(1)}, u32[]{:S(2)}, u32[]{:S(2)}) collective-permute-start(bf16[256,2176]{1,0:T(8,128)(2,1)S(1)} %add_convert_fusion.13), channel_id=1, source_target_pairs={{0,8},{8,16},{16,24},{24,28},{28,20},{20,12},{12,4},{4,0},{1,9},{9... | collective-permute-start | bytes 3342344 | tf_op jit(solution)/shard_map/ppermute | solution.py:547
  597.9 45.9 %collective-permute-start.43 = (bf16[256,2048]{1,0:T(8,128)(2,1)S(1)}, bf16[256,2048]{1,0:T(8,128)(2,1)S(1)}, u32[]{:S(2)}, u32[]{:S(2)}) collective-permute-start(bf16[256,2048]{1,0:T(8,128)(2,1)S(1)} %add_convert_fusion.16), channel_id=1, source_target_pairs={{0,2},{1,3},{2,0},{3,1},{4,6},{5,7},{6,4},{7,5},{8,10},{9,11},{10,... | collective-permute-start | bytes 3145736 | tf_op jit(solution)/shard_map/ppermute | solution.py:1166
  673.6 49.9 %collective-permute-start.40 = (bf16[512,2048]{1,0:T(8,128)(2,1)}, bf16[512,2048]{1,0:T(8,128)(2,1)}, u32[]{:S(2)}, u32[]{:S(2)}) collective-permute-start(bf16[512,2048]{1,0:T(8,128)(2,1)} %add_convert_fusion.refs_0_), channel_id=1, source_target_pairs={{0,1},{1,0},{2,3},{3,2},{4,5},{5,4},{6,7},{7,6},{8,9},{9,8},{10,11... | collective-permute-start | bytes 6291464 | tf_op jit(solution)/shard_map/ppermute | solution.py:1167
  674.8 43.4 %collective-permute-start.52 = (bf16[256,2176]{1,0:T(8,128)(2,1)}, bf16[256,2176]{1,0:T(8,128)(2,1)}, u32[]{:S(2)}, u32[]{:S(2)}) collective-permute-start(bf16[256,2176]{1,0:T(8,128)(2,1)} %add_convert_fusion.8), channel_id=1, source_target_pairs={{0,4},{8,0},{16,8},{24,16},{28,24},{20,28},{12,20},{4,12},{1,5},{9... | collective-permute-start | bytes 3342344 | tf_op jit(solution)/shard_map/ppermute | solution.py:548
  697.8 36.3 %collective-permute-start.44 = (bf16[256,2048]{1,0:T(8,128)(2,1)}, bf16[256,2048]{1,0:T(8,128)(2,1)}, u32[]{:S(2)}, u32[]{:S(2)}) collective-permute-start(bf16[256,2048]{1,0:T(8,128)(2,1)} %add_convert_fusion.14.refs_2_), channel_id=1, source_target_pairs={{0,1},{1,0},{2,3},{3,2},{4,5},{5,4},{6,7},{7,6},{8,9},{9,8},{10,11... | collective-permute-start | bytes 3145736 | tf_op jit(solution)/shard_map/ppermute | solution.py:1167
  697.8 36.3 %collective-permute-start.42 = (bf16[256,2048]{1,0:T(8,128)(2,1)}, bf16[256,2048]{1,0:T(8,128)(2,1)}, u32[]{:S(2)}, u32[]{:S(2)}) collective-permute-start(bf16[256,2048]{1,0:T(8,128)(2,1)} %add_convert_fusion.15.refs_0_), channel_id=1, source_target_pairs={{0,1},{1,0},{2,3},{3,2},{4,5},{5,4},{6,7},{7,6},{8,9},{9,8},{10,11... | collective-permute-start | bytes 3145736 | tf_op jit(solution)/shard_map/ppermute | solution.py:1167
  (122 other events, 2577.0 us)
